TPU v7x, 512 devices: a 4x2x32 block of a 4x8x32 slice. The times are simulated.
512 devices in a mesh: grp: 2 (over y), gx: 32 (over z), gy: 4 (over x), gz: 2 (over core).
Axes of the slice: x: 4, y: 2, z: 32, core: 2. Of those that a mesh axis runs over, the one named last changes fastest.
The devices are a block of a 4x8x32 slice.
Arguments:
- position: float32 [64, 128, 8, 256], P(None, ('grp', 'gx'), 'gy', 'gz'), parts along dimension 1, may hold values from -6 to 6
- momentum: float32 [64, 128, 8, 256], P(None, ('grp', 'gx'), 'gy', 'gz'), parts along dimension 1, may hold values from -6 to 6
- noise: bfloat16 [3, 64, 128, 8, 256], P(None, None, ('grp', 'gx'), 'gy', 'gz'), parts along dimension 2, may hold values from -6 to 6
- filter_in: bfloat16 [64, 64, 3, 3, 3], P('gx', 'gy'), may hold values from -0.15625 to 0.15625
- filter_out: bfloat16 [64, 64, 3, 3, 3], P('gx', 'gy'), may hold values from -0.15625 to 0.15625
- bias: float32 [64], replicated, may hold values from -4 to 4
Outputs:
- final_position: float32 [64, 128, 8, 256], P(None, ('grp', 'gx'), 'gy', 'gz'), parts along dimension 1
- final_momentum: float32 [64, 128, 8, 256], P(None, ('grp', 'gx'), 'gy', 'gz'), parts along dimension 1
There are 2 independent parts, one for each index of `grp`. A program takes and returns all parts, laid end to end along the dimension named above; an argument that names none is the same for every part. Nothing has to cross between parts.
All inputs are finite; a program needn't handle non-finite values.
Results may differ from a plain program's by a relative error of at most 0.0013.
Values may be sent and summed in bfloat16 or wider, within the bound.
No kernel may reach another device: no remote copies, remote signals or barrier semaphores. Data moves between devices by JAX's collectives and lax.ppermute only.
A program may use at most 64 MiB of HBM per device.

v0:
```python
import functools
import math

import jax
import jax.numpy as jnp
from jax import lax
from jax.experimental import pallas as pl
from jax.experimental.pallas import tpu as pltpu
from jax.sharding import Mesh, PartitionSpec as P

F32, BF16 = jnp.float32, jnp.bfloat16
STEP = 0.25
XB, ZB = 4, 16
HALO = 4
PITCH = ZB + 2 * HALO
VMEM = pltpu.VMEM
LIMIT = 24 * 1024 * 1024


def cycle(rows, cols):
    path = [(0, b) for b in range(cols)]
    for b in range(cols - 1, 0, -1):
        column = [(a, b) for a in range(1, rows)]
        path += column if (cols - 1 - b) % 2 == 0 else column[::-1]
    return path + [(a, 0) for a in range(rows - 1, 0, -1)]


def kernel_call(body, outs, args, scratch=(), name=None):
    spec = pl.BlockSpec(memory_space=VMEM)
    args = [pltpu.with_memory_space_constraint(v, VMEM) for v in args]
    return pl.pallas_call(
        body,
        out_shape=[VMEM(o.shape, o.dtype) for o in outs],
        in_specs=[spec] * len(args),
        out_specs=[spec] * len(outs),
        scratch_shapes=list(scratch),
        compiler_params=pltpu.CompilerParams(vmem_limit_bytes=LIMIT),
        name=name,
    )(*args)


def spread_body(place, q_ref, p_ref, n_ref, out_ref):
    for k in range(2 + n_ref.shape[0]):
        for x in range(q_ref.shape[1]):
            if k < 2:
                ref = (q_ref, p_ref)[k]
                parts = [ref[:, x, y, :] for y in range(ref.shape[2])]
            else:
                parts = [n_ref[k - 2, :, x, y, :].astype(F32) for y in range(n_ref.shape[3])]
            flat = jnp.concatenate(parts, axis=0).T
            for member, block in enumerate(place):
                out_ref[member, k, x] = flat[block * ZB : (block + 1) * ZB, :]


def collect_body(place, in_ref, q_ref, p_ref):
    for k, ref in enumerate((q_ref, p_ref)):
        chans = ref.shape[0]
        for x in range(ref.shape[1]):
            rows = [None] * len(place)
            for member, block in enumerate(place):
                rows[block] = in_ref[member, k, x]
            flat = jnp.concatenate(rows, axis=0).T
            for y in range(ref.shape[2]):
                ref[:, x, y, :] = flat[y * chans : (y + 1) * chans, :]


def weights_body(m_ref, out_ref, fwd_ref):
    groups, chans, _ = m_ref.shape
    per = chans // groups
    taps = 27
    turned = [m_ref[g].astype(F32).T.astype(BF16) for g in range(groups)]
    for f in range(2):
        for tap in range(taps):
            at = (f * taps + tap) * per
            for g in range(groups):
                fwd_ref[f, tap * chans + g * per : tap * chans + (g + 1) * per, :] = turned[g][
                    at : at + per, :
                ].astype(F32)
    zero = jnp.zeros((chans, chans), BF16)

    def place(w, tap, block):
        a, b, c = tap // 9, tap // 3 % 3, tap % 3
        for u in range(2):
            t = b + u
            row = ((t // 2 * 3 + c) * 2 + t % 2) * chans
            col = (a * 2 + u) * chans
            out_ref[w, row : row + chans, col : col + chans] = block

    for w in range(4):
        for c in range(3):
            for a in range(3):
                for t, u in ((3, 0), (0, 1)):
                    row = ((t // 2 * 3 + c) * 2 + t % 2) * chans
                    col = (a * 2 + u) * chans
                    out_ref[w, row : row + chans, col : col + chans] = zero
    for f in range(2):
        for tap in range(0, taps, 2):
            n = min(2, taps - tap)
            pair = fwd_ref[f, tap * chans : (tap + n) * chans, :]
            adj = pair.T
            for i in range(n):
                part = slice(i * chans, (i + 1) * chans)
                place(f, tap + i, pair[part].astype(BF16))
                place(f + 2, taps - 1 - tap - i, adj[:, part].astype(BF16))


def gradient_body(kind, coef, *refs):
    decay, kick = coef
    it = iter(refs)
    r_ref = next(it)
    if kind == "first":
        q_of = lambda x, j: r_ref[x // 2 * 4 + j, 0, x % 2]
        p_of = lambda x, j: r_ref[x // 2 * 4 + j, 1, x % 2]
    else:
        q_ref, p_ref = next(it), next(it)
        q_of = lambda x, j: q_ref[x, j]
        p_of = lambda x, j: p_ref[x, j]
    xl_ref, xh_ref, zl_ref, zh_ref, w_ref, bias_ref = (next(it) for _ in range(6))
    if kind == "last":
        out_ref = next(it)
    else:
        qo_ref, po_ref, qb_ref = (next(it) for _ in range(3))
    buf, rows_ref, act = (next(it) for _ in range(3))
    step_at = {"first": 0}.get(kind, kind)

    x_all = XB + 2 * HALO
    lo, hi = 8 + HALO, 8 + HALO + ZB
    edge = jnp.zeros((x_all, 4, 8, 128), F32)
    buf[:, :, 0:8, :] = edge
    buf[:, :, 8 + PITCH : 16 + PITCH, :] = edge
    buf[0:HALO, :, lo:hi, :] = xl_ref[...].astype(F32)
    buf[HALO + XB :, :, lo:hi, :] = xh_ref[...].astype(F32)
    for x in range(XB):
        for j in range(4):
            buf[HALO + x, j, lo:hi, :] = q_of(x, j)
    buf[:, :, 8:lo, :] = zl_ref[...].astype(F32)
    buf[:, :, hi : 8 + PITCH, :] = zh_ref[...].astype(F32)

    def conv(x_in, w, use):
        n = x_in * PITCH
        for j in range(4):
            for c in range(3):
                v = buf[0:x_in, j, 7 + c : 7 + c + PITCH, :].reshape(n, 128).astype(BF16)
                rows_ref[0:n, (j * 3 + c) * 128 : (j * 3 + c + 1) * 128] = v
                if j == 0:
                    rows_ref[0:n, (12 + c) * 128 : (13 + c) * 128] = v
        x_out = x_in - 2
        m = x_out * PITCH
        for p in range(4):
            t = jnp.dot(
                rows_ref[0:n, 384 * p : 384 * p + 768], w_ref[w], preferred_element_type=F32
            )
            o = t[0:m, 0:128] + t[PITCH : PITCH + m, 128:256] + t[2 * PITCH :, 256:384]
            use(p, o.reshape(x_out, PITCH, 128))

    def hidden(p, h):
        t = jnp.tanh(h + bias_ref[...])
        act[:, p] = 1.0 - t * t
        buf[0 : XB + 6, p, 8 : 8 + PITCH, :] = t

    def second(p, h):
        buf[0 : XB + 4, p, 8 : 8 + PITCH, :] = h

    def back(p, g):
        buf[0 : XB + 2, p, 8 : 8 + PITCH, :] = g * act[2 : XB + 4, (p + 1) % 4]

    half = 0.5 * STEP

    def final(p, g):
        buf[0:XB, p, 8 : 8 + PITCH, :] = g
        j = (p + 2) % 4
        for x in range(XB):
            q = q_of(x, j)
            force = buf[x, p, lo:hi, :] + q
            mom = p_of(x, j) - half * force
            if kind == "last":
                out_ref[x // 2, j, 0, x % 2] = q
                out_ref[x // 2, j, 1, x % 2] = mom
                continue
            if kind != "first":
                mom = mom - half * force
            q = q + half * mom
            mom = decay * mom + kick * r_ref[x // 2 * 4 + j, 2 + step_at, x % 2]
            q = q + half * mom
            qo_ref[x, j] = q
            po_ref[x, j] = mom
            qb_ref[x, j] = q.astype(BF16)

    conv(XB + 8, 0, hidden)
    conv(XB + 6, 1, second)
    conv(XB + 4, 3, back)
    conv(XB + 2, 2, final)


def solution(mesh):
    gy, gz = mesh.shape["gy"], mesh.shape["gz"]
    gs = XB // 2
    gX = mesh.shape["gx"] // gs
    fine = Mesh(
        mesh.devices.reshape(mesh.shape["grp"], gX, gs, gy, gz), ("grp", "gX", "gs", "gy", "gz")
    )
    walk = cycle(gs, gy)
    place = [walk.index((a, b)) for a in range(gs) for b in range(gy)]
    ring = [(a * gy + b) * gz + c for c in range(gz) for a, b in walk]

    def x_shift(d):
        return [(i, (i + d) % gX) for i in range(gX)]

    def z_shift(d):
        n = len(ring)
        return [(ring[i], ring[(i + d) % n]) for i in range(n)]

    decay = math.exp(-0.25)
    kick = math.sqrt(1.0 - decay * decay)

    def halos(block):
        xl = lax.ppermute(block, "gX", x_shift(1))
        xh = lax.ppermute(block, "gX", x_shift(-1))
        whole = jnp.concatenate([xl, block, xh], axis=0)
        zl = lax.ppermute(whole[:, :, ZB - HALO :], ("gs", "gy", "gz"), z_shift(1))
        zh = lax.ppermute(whole[:, :, :HALO], ("gs", "gy", "gz"), z_shift(-1))
        return xl, xh, zl, zh

    def on_device(position, momentum, noise, filter_in, filter_out, bias):
        chans = position.shape[0]
        steps = noise.shape[0]
        members = gs * gy

        own = [f.reshape(*f.shape[:2], 27).transpose(0, 2, 1) for f in (filter_in, filter_out)]
        own = jnp.concatenate([f.reshape(f.shape[0], -1) for f in own], axis=1)
        own = jnp.pad(own, ((0, 0), (0, -own.shape[1] % 128)))
        far = lax.all_to_all(
            jnp.broadcast_to(own, (gX, *own.shape)), "gX", 0, 0, tiled=True
        )
        far = far.reshape(-1, far.shape[-1])
        near = lax.all_to_all(
            jnp.broadcast_to(far, (members, *far.shape)), ("gs", "gy"), 0, 0, tiled=True
        )
        near = near.reshape(gs, gy, gX, *own.shape).transpose(1, 2, 0, 3, 4)
        (weights,) = kernel_call(
            weights_body,
            [jax.ShapeDtypeStruct((4, 12 * chans, 6 * chans), BF16)],
            (near.reshape(gy, chans, own.shape[1]),),
            [VMEM((2, 27 * chans, chans), F32)],
            name="weights",
        )
        bias_row = jnp.concatenate([bias, bias])[None, :]

        (spread,) = kernel_call(
            functools.partial(spread_body, place),
            [jax.ShapeDtypeStruct((members, 2 + steps, 2, ZB, 128), F32)],
            (position, momentum, noise),
            name="spread",
        )
        held = lax.all_to_all(spread, ("gs", "gy"), 0, 0, tiled=True)

        start = held[:, 0].reshape(gs, gy, 2, ZB, 128).transpose(0, 2, 1, 3, 4)
        block = start.reshape(XB, gy, ZB, 128).astype(BF16)

        shape = jax.ShapeDtypeStruct(block.shape, F32)
        scratch = (
            VMEM((XB + 8, gy, PITCH + 16, 128), F32),
            VMEM(((XB + 8) * PITCH, 15 * 128), BF16),
            VMEM((XB + 6, gy, PITCH, 128), F32),
        )
        coef = (decay, kick)
        state = ()
        for k in range(steps + 1):
            kind = "first" if k == 0 else "last" if k == steps else k
            edges = halos(block)
            args = (held, *state, *edges, weights, bias_row)
            if kind == "last":
                outs = [jax.ShapeDtypeStruct((gs, gy, 2, 2, ZB, 128), F32)]
            else:
                outs = [shape, shape, jax.ShapeDtypeStruct(block.shape, BF16)]
            res = kernel_call(
                functools.partial(gradient_body, kind, coef), outs, args, scratch, name="gradient"
            )
            if kind != "last":
                state, block = tuple(res[:2]), res[2]
        back = lax.all_to_all(
            res[0].reshape(members, 2, 2, ZB, 128), ("gs", "gy"), 0, 0, tiled=True
        )
        out = jax.ShapeDtypeStruct(position.shape, F32)
        return tuple(
            kernel_call(functools.partial(collect_body, place), [out, out], (back,), name="collect")
        )

    where = ("grp", "gX", "gs")
    lattice = P(None, where, "gy", "gz")
    filters = P(("gX", "gs"), "gy", None, None, None)
    return jax.shard_map(
        on_device,
        mesh=fine,
        in_specs=(lattice, lattice, P(None, None, where, "gy", "gz"), filters, filters, P()),
        out_specs=(lattice, lattice),
        check_vma=False,
    )
```

profile of v0, /device:TPU:40, one launch (start us, length us, event | category | flops | bytes accessed | tf_op | source)
XLA Modules:
  0.0 196.3 jit_solution(9720612614285733917)
XLA Ops:
  0.6 0.7 copy.16
  1.4 0.7 copy.15
  2.3 0.7 broadcast_in_dim.9
  3.0 44.6 %all-to-all-start.1 = ((bf16[16,2,896]{2,1,0:T(2,128)(2,1)}), bf16[16,2,896]{2,1,0:T(2,128)(2,1)S(1)}, u32[]{:S(2)}, u32[]{:S(2)}) async-start(bf16[16,2,896]{2,1,0:T(2,128)(2,1)} %broadcast_in_dim.9), calls=%async_computation.1 | async-start | bytes 114688 | tf_op jit(solution)/shard_map/all_to_all | solution.py:232
  47.6 0.9 copy-done
  48.5 0.9 copy-done.1
  49.4 0.9 copy-done.2
  50.3 1.4 spread.1
  51.8 19.4 %all-to-all-done.1 = bf16[16,2,896]{2,1,0:T(2,128)(2,1)S(1)} async-done(((bf16[16,2,896]{2,1,0:T(2,128)(2,1)}), bf16[16,2,896]{2,1,0:T(2,128)(2,1)S(1)}, u32[]{:S(2)}, u32[]{:S(2)}) %all-to-all-start.1) | async-done | bytes 57376 | tf_op jit(solution)/shard_map/all_to_all | solution.py:232
  71.2 4.6 %all-to-all-start = ((f32[8,5,2,16,128]{4,3,2,1,0:T(8,128)}), f32[8,5,2,16,128]{4,3,2,1,0:T(8,128)S(1)}, u32[]{:S(2)}, u32[]{:S(2)}) async-start(f32[8,5,2,16,128]{4,3,2,1,0:T(8,128)} %spread.1), calls=%async_computation | async-start | bytes 1310720 | tf_op jit(solution)/shard_map/all_to_all | solution.py:255
  75.8 9.0 %all-to-all-done.refs_0_ = f32[8,5,2,16,128]{4,3,2,1,0:T(8,128)S(1)} async-done(((f32[8,5,2,16,128]{4,3,2,1,0:T(8,128)}), f32[8,5,2,16,128]{4,3,2,1,0:T(8,128)S(1)}, u32[]{:S(2)}, u32[]{:S(2)}) %all-to-all-start) | async-done | bytes 655392 | tf_op jit(solution)/shard_map/all_to_all | solution.py:255
  84.9 0.8 broadcast_in_dim.10
  85.7 3.7 %all-to-all-start.2 = ((bf16[8,32,896]{2,1,0:T(8,128)(2,1)}), bf16[8,32,896]{2,1,0:T(8,128)(2,1)S(1)}, u32[]{:S(2)}, u32[]{:S(2)}) async-start(bf16[8,32,896]{2,1,0:T(8,128)(2,1)} %broadcast_in_dim.10), calls=%async_computation.2 | async-start | bytes 917504 | tf_op jit(solution)/shard_map/all_to_all | solution.py:236
  89.4 4.4 %collective-permute-start = (bf16[4,4,16,128]{3,2,1,0:T(8,128)(2,1)S(1)}, bf16[4,4,16,128]{3,2,1,0:T(8,128)(2,1)S(1)}, u32[]{:S(2)}, u32[]{:S(2)}) collective-permute-start(bf16[4,4,16,128]{3,2,1,0:T(8,128)(2,1)S(1)} %bitcast.19), channel_id=1, source_target_pairs={{0,16},{16,32},{32,48},{48,64},{64,80},{80,96},{96,112},{112,128},... | collective-permute-start | bytes 196616 | tf_op jit(solution)/shard_map/ppermute | solution.py:217
  93.8 3.6 %collective-permute-start.1 = (bf16[4,4,16,128]{3,2,1,0:T(8,128)(2,1)S(1)}, bf16[4,4,16,128]{3,2,1,0:T(8,128)(2,1)S(1)}, u32[]{:S(2)}, u32[]{:S(2)}) collective-permute-start(bf16[4,4,16,128]{3,2,1,0:T(8,128)(2,1)S(1)} %bitcast.20), channel_id=1, source_target_pairs={{0,240},{16,0},{32,16},{48,32},{64,48},{80,64},{96,80},{112,96},{1... | collective-permute-start | bytes 196616 | tf_op jit(solution)/shard_map/ppermute | solution.py:218
  97.4 0.7 collective-permute-done.refs_1_
  98.2 2.7 %collective-permute-done.1.refs_2_ = bf16[4,4,16,128]{3,2,1,0:T(8,128)(2,1)S(1)} collective-permute-done((bf16[4,4,16,128]{3,2,1,0:T(8,128)(2,1)S(1)}, bf16[4,4,16,128]{3,2,1,0:T(8,128)(2,1)S(1)}, u32[]{:S(2)}, u32[]{:S(2)}) %collective-permute-start.1) | collective-permute-done | bytes 65568 | tf_op jit(solution)/shard_map/ppermute | solution.py:218
  100.9 3.7 %collective-permute-start.2 = (bf16[12,4,4,128]{3,2,1,0:T(4,128)(2,1)S(1)}, bf16[12,4,4,128]{3,2,1,0:T(4,128)(2,1)S(1)}, u32[]{:S(2)}, u32[]{:S(2)}) collective-permute-start(bf16[12,4,4,128]{3,2,1,0:T(4,128)(2,1)S(1)} %get-tuple-element.27), channel_id=1, source_target_pairs={{0,2},{2,4},{4,6},{6,14},{14,12},{12,10},{10,8},{8,1},{1,3},{3,5},... | collective-permute-start | bytes 147464 | tf_op jit(solution)/shard_map/ppermute | solution.py:220
  104.6 2.0 collective-permute-start.3
  107.3 1.4 weights.1.refs_5_.refs_7_
  108.8 1.8 collective-permute-done.3.refs_4_
  110.6 3.2 %gradient.4 = (f32[4,4,16,128]{3,2,1,0:T(8,128)S(1)}, f32[4,4,16,128]{3,2,1,0:T(8,128)S(1)}, bf16[4,4,16,128]{3,2,1,0:T(8,128)(2,1)S(1)}) custom-call(f32[8,5,2,16,128]{4,3,2,1,0:T(8,128)S(1)} %all-to-all-done.refs_0_, bf16[4,4,16,128]{3,2,1,0:T(8,128)(2,1)S(1)} %collective-permute-done.refs_1_, bf16[4,4,16,128]{3,2,1,0:T(8,128)(2,1)S(1)} %collective-permute-done.1.refs_2_, ...), custom_call_target="tpu_custom_call" | custom-call | tf_op jit(solution)/shard_map/gradient/pallas_call | solution.py:31
  113.9 3.4 %collective-permute-start.4 = (bf16[4,4,16,128]{3,2,1,0:T(8,128)(2,1)S(1)}, bf16[4,4,16,128]{3,2,1,0:T(8,128)(2,1)S(1)}, u32[]{:S(2)}, u32[]{:S(2)}) collective-permute-start(bf16[4,4,16,128]{3,2,1,0:T(8,128)(2,1)S(1)} %get-tuple-element.13), channel_id=1, source_target_pairs={{0,16},{16,32},{32,48},{48,64},{64,80},{80,96},{96,112},{112,128},... | collective-permute-start | bytes 196616 | tf_op jit(solution)/shard_map/ppermute | solution.py:217
  117.3 4.6 %collective-permute-start.5 = (bf16[4,4,16,128]{3,2,1,0:T(8,128)(2,1)S(1)}, bf16[4,4,16,128]{3,2,1,0:T(8,128)(2,1)S(1)}, u32[]{:S(2)}, u32[]{:S(2)}) collective-permute-start(bf16[4,4,16,128]{3,2,1,0:T(8,128)(2,1)S(1)} %get-tuple-element.13), channel_id=1, source_target_pairs={{0,240},{16,0},{32,16},{48,32},{64,48},{80,64},{96,80},{112,96},{1... | collective-permute-start | bytes 196616 | tf_op jit(solution)/shard_map/ppermute | solution.py:218
  121.9 1.0 collective-permute-done.4.refs_3_
  122.9 1.9 collective-permute-done.5.refs_4_
  124.9 3.8 %collective-permute-start.6 = (bf16[12,4,4,128]{3,2,1,0:T(4,128)(2,1)S(1)}, bf16[12,4,4,128]{3,2,1,0:T(4,128)(2,1)S(1)}, u32[]{:S(2)}, u32[]{:S(2)}) collective-permute-start(bf16[12,4,4,128]{3,2,1,0:T(4,128)(2,1)S(1)} %get-tuple-element.25), channel_id=1, source_target_pairs={{0,2},{2,4},{4,6},{6,14},{14,12},{12,10},{10,8},{8,1},{1,3},{3,5},... | collective-permute-start | bytes 147464 | tf_op jit(solution)/shard_map/ppermute | solution.py:220
  128.6 2.0 collective-permute-start.7
  130.6 4.0 %collective-permute-done.7.refs_6_ = bf16[12,4,4,128]{3,2,1,0:T(4,128)(2,1)S(1)} collective-permute-done((bf16[12,4,4,128]{3,2,1,0:T(4,128)(2,1)S(1)}, bf16[12,4,4,128]{3,2,1,0:T(4,128)(2,1)S(1)}, u32[]{:S(2)}, u32[]{:S(2)}) %collective-permute-start.7) | collective-permute-done | bytes 49184 | tf_op jit(solution)/shard_map/ppermute | solution.py:221
  134.7 3.2 %gradient.5 = (f32[4,4,16,128]{3,2,1,0:T(8,128)S(1)}, f32[4,4,16,128]{3,2,1,0:T(8,128)S(1)}, bf16[4,4,16,128]{3,2,1,0:T(8,128)(2,1)S(1)}) custom-call(f32[8,5,2,16,128]{4,3,2,1,0:T(8,128)S(1)} %all-to-all-done.refs_0_, f32[4,4,16,128]{3,2,1,0:T(8,128)S(1)} %get-tuple-element.11.refs_1_, f32[4,4,16,128]{3,2,1,0:T(8,128)S(1)} %get-tuple-element.12.refs_2_, ...), custom_call_target="tpu_custom_call" | custom-call | tf_op jit(solution)/shard_map/gradient/pallas_call | solution.py:31
  137.9 3.9 %collective-permute-start.8 = (bf16[4,4,16,128]{3,2,1,0:T(8,128)(2,1)S(1)}, bf16[4,4,16,128]{3,2,1,0:T(8,128)(2,1)S(1)}, u32[]{:S(2)}, u32[]{:S(2)}) collective-permute-start(bf16[4,4,16,128]{3,2,1,0:T(8,128)(2,1)S(1)} %get-tuple-element.16), channel_id=1, source_target_pairs={{0,16},{16,32},{32,48},{48,64},{64,80},{80,96},{96,112},{112,128},... | collective-permute-start | bytes 196616 | tf_op jit(solution)/shard_map/ppermute | solution.py:217
  141.9 4.1 %collective-permute-start.9 = (bf16[4,4,16,128]{3,2,1,0:T(8,128)(2,1)S(1)}, bf16[4,4,16,128]{3,2,1,0:T(8,128)(2,1)S(1)}, u32[]{:S(2)}, u32[]{:S(2)}) collective-permute-start(bf16[4,4,16,128]{3,2,1,0:T(8,128)(2,1)S(1)} %get-tuple-element.16), channel_id=1, source_target_pairs={{0,240},{16,0},{32,16},{48,32},{64,48},{80,64},{96,80},{112,96},{1... | collective-permute-start | bytes 196616 | tf_op jit(solution)/shard_map/ppermute | solution.py:218
  145.9 1.0 collective-permute-done.8.refs_3_
  146.9 2.0 %collective-permute-done.9.refs_4_ = bf16[4,4,16,128]{3,2,1,0:T(8,128)(2,1)S(1)} collective-permute-done((bf16[4,4,16,128]{3,2,1,0:T(8,128)(2,1)S(1)}, bf16[4,4,16,128]{3,2,1,0:T(8,128)(2,1)S(1)}, u32[]{:S(2)}, u32[]{:S(2)}) %collective-permute-start.9) | collective-permute-done | bytes 65568 | tf_op jit(solution)/shard_map/ppermute | solution.py:218
  149.0 3.2 %collective-permute-start.10 = (bf16[12,4,4,128]{3,2,1,0:T(4,128)(2,1)S(1)}, bf16[12,4,4,128]{3,2,1,0:T(4,128)(2,1)S(1)}, u32[]{:S(2)}, u32[]{:S(2)}) collective-permute-start(bf16[12,4,4,128]{3,2,1,0:T(4,128)(2,1)S(1)} %get-tuple-element.23), channel_id=1, source_target_pairs={{0,2},{2,4},{4,6},{6,14},{14,12},{12,10},{10,8},{8,1},{1,3},{3,5},... | collective-permute-start | bytes 147464 | tf_op jit(solution)/shard_map/ppermute | solution.py:220
  152.3 2.6 %collective-permute-start.11 = (bf16[12,4,4,128]{3,2,1,0:T(4,128)(2,1)S(1)}, bf16[12,4,4,128]{3,2,1,0:T(4,128)(2,1)S(1)}, u32[]{:S(2)}, u32[]{:S(2)}) collective-permute-start(bf16[12,4,4,128]{3,2,1,0:T(4,128)(2,1)S(1)} %get-tuple-element.22), channel_id=1, source_target_pairs={{0,9},{2,0},{4,2},{6,4},{14,6},{12,14},{10,12},{8,10},{1,8},{3,1},... | collective-permute-start | bytes 147464 | tf_op jit(solution)/shard_map/ppermute | solution.py:221
  154.8 3.4 %collective-permute-done.11.refs_6_ = bf16[12,4,4,128]{3,2,1,0:T(4,128)(2,1)S(1)} collective-permute-done((bf16[12,4,4,128]{3,2,1,0:T(4,128)(2,1)S(1)}, bf16[12,4,4,128]{3,2,1,0:T(4,128)(2,1)S(1)}, u32[]{:S(2)}, u32[]{:S(2)}) %collective-permute-start.11) | collective-permute-done | bytes 49184 | tf_op jit(solution)/shard_map/ppermute | solution.py:221
  158.3 3.2 %gradient.6 = (f32[4,4,16,128]{3,2,1,0:T(8,128)S(1)}, f32[4,4,16,128]{3,2,1,0:T(8,128)S(1)}, bf16[4,4,16,128]{3,2,1,0:T(8,128)(2,1)S(1)}) custom-call(f32[8,5,2,16,128]{4,3,2,1,0:T(8,128)S(1)} %all-to-all-done.refs_0_, f32[4,4,16,128]{3,2,1,0:T(8,128)S(1)} %get-tuple-element.14.refs_1_, f32[4,4,16,128]{3,2,1,0:T(8,128)S(1)} %get-tuple-element.15.refs_2_, ...), custom_call_target="tpu_custom_call" | custom-call | tf_op jit(solution)/shard_map/gradient/pallas_call | solution.py:31
  161.5 3.2 %collective-permute-start.12 = (bf16[4,4,16,128]{3,2,1,0:T(8,128)(2,1)S(1)}, bf16[4,4,16,128]{3,2,1,0:T(8,128)(2,1)S(1)}, u32[]{:S(2)}, u32[]{:S(2)}) collective-permute-start(bf16[4,4,16,128]{3,2,1,0:T(8,128)(2,1)S(1)} %get-tuple-element.19), channel_id=1, source_target_pairs={{0,16},{16,32},{32,48},{48,64},{64,80},{80,96},{96,112},{112,128},... | collective-permute-start | bytes 196616 | tf_op jit(solution)/shard_map/ppermute | solution.py:217
  164.7 4.9 %collective-permute-start.13 = (bf16[4,4,16,128]{3,2,1,0:T(8,128)(2,1)S(1)}, bf16[4,4,16,128]{3,2,1,0:T(8,128)(2,1)S(1)}, u32[]{:S(2)}, u32[]{:S(2)}) collective-permute-start(bf16[4,4,16,128]{3,2,1,0:T(8,128)(2,1)S(1)} %get-tuple-element.19), channel_id=1, source_target_pairs={{0,240},{16,0},{32,16},{48,32},{64,48},{80,64},{96,80},{112,96},{1... | collective-permute-start | bytes 196616 | tf_op jit(solution)/shard_map/ppermute | solution.py:218
  169.9 1.8 collective-permute-done.13.refs_4_
  171.8 3.2 %collective-permute-start.14 = (bf16[12,4,4,128]{3,2,1,0:T(4,128)(2,1)S(1)}, bf16[12,4,4,128]{3,2,1,0:T(4,128)(2,1)S(1)}, u32[]{:S(2)}, u32[]{:S(2)}) collective-permute-start(bf16[12,4,4,128]{3,2,1,0:T(4,128)(2,1)S(1)} %get-tuple-element.21), channel_id=1, source_target_pairs={{0,2},{2,4},{4,6},{6,14},{14,12},{12,10},{10,8},{8,1},{1,3},{3,5},... | collective-permute-start | bytes 147464 | tf_op jit(solution)/shard_map/ppermute | solution.py:220
  175.1 2.4 %collective-permute-start.15 = (bf16[12,4,4,128]{3,2,1,0:T(4,128)(2,1)S(1)}, bf16[12,4,4,128]{3,2,1,0:T(4,128)(2,1)S(1)}, u32[]{:S(2)}, u32[]{:S(2)}) collective-permute-start(bf16[12,4,4,128]{3,2,1,0:T(4,128)(2,1)S(1)} %get-tuple-element.20), channel_id=1, source_target_pairs={{0,9},{2,0},{4,2},{6,4},{14,6},{12,14},{10,12},{8,10},{1,8},{3,1},... | collective-permute-start | bytes 147464 | tf_op jit(solution)/shard_map/ppermute | solution.py:221
  177.5 3.6 %collective-permute-done.15.refs_6_ = bf16[12,4,4,128]{3,2,1,0:T(4,128)(2,1)S(1)} collective-permute-done((bf16[12,4,4,128]{3,2,1,0:T(4,128)(2,1)S(1)}, bf16[12,4,4,128]{3,2,1,0:T(4,128)(2,1)S(1)}, u32[]{:S(2)}, u32[]{:S(2)}) %collective-permute-start.15) | collective-permute-done | bytes 49184 | tf_op jit(solution)/shard_map/ppermute | solution.py:221
  181.1 3.2 %gradient.7 = f32[2,4,2,2,16,128]{5,4,3,2,1,0:T(8,128)S(1)} custom-call(f32[8,5,2,16,128]{4,3,2,1,0:T(8,128)S(1)} %all-to-all-done.refs_0_, f32[4,4,16,128]{3,2,1,0:T(8,128)S(1)} %get-tuple-element.17.refs_1_, f32[4,4,16,128]{3,2,1,0:T(8,128)S(1)} %get-tuple-element.18.refs_2_, bf16[4,4,16,128]{3,2,1,0:T(8,128)(2,1)S(1)} %collective-permute-done.12.refs_3_, ...), custom_call_target="tpu_custom_call" | custom-call | tf_op jit(solution)/shard_map/gradient/pallas_call | solution.py:31
  184.3 10.4 %all_to_all.20.in_ref = f32[8,2,2,16,128]{4,3,2,1,0:T(8,128)S(1)} all-to-all(f32[8,2,2,16,128]{4,3,2,1,0:T(8,128)S(1)} %bitcast.16), channel_id=1, replica_groups=mesh['grp'=2,'gX'=16,'gs'=2,'gy'=4,'gz'=2] {'gs','gy'}, dimensions={0} | all-to-all | bytes 524288 | tf_op jit(solution)/shard_map/all_to_all | solution.py:281
  195.0 0.7 copy.23
  195.6 0.7 copy.24
  (35 shorter events, 1.9 us)
Async XLA Ops:
  2.2 104.3 %copy-start.3 = (f32[64]{0:T(128)S(1)}, f32[64]{0:T(128)}, u32[]{:S(2)}) copy-start(f32[64]{0:T(128)} %param.11) | copy-start | bytes 772
  3.0 68.2 %all-to-all-start.1 = ((bf16[16,2,896]{2,1,0:T(2,128)(2,1)}), bf16[16,2,896]{2,1,0:T(2,128)(2,1)S(1)}, u32[]{:S(2)}, u32[]{:S(2)}) async-start(bf16[16,2,896]{2,1,0:T(2,128)(2,1)} %broadcast_in_dim.9), calls=%async_computation.1 | async-start | bytes 114688 | tf_op jit(solution)/shard_map/all_to_all | solution.py:232
  47.6 0.9 copy-start
  48.5 0.9 copy-start.1
  49.4 0.9 copy-start.2
  71.2 13.7 %all-to-all-start = ((f32[8,5,2,16,128]{4,3,2,1,0:T(8,128)}), f32[8,5,2,16,128]{4,3,2,1,0:T(8,128)S(1)}, u32[]{:S(2)}, u32[]{:S(2)}) async-start(f32[8,5,2,16,128]{4,3,2,1,0:T(8,128)} %spread.1), calls=%async_computation | async-start | bytes 1310720 | tf_op jit(solution)/shard_map/all_to_all | solution.py:255
  85.7 21.0 %all-to-all-start.2 = ((bf16[8,32,896]{2,1,0:T(8,128)(2,1)}), bf16[8,32,896]{2,1,0:T(8,128)(2,1)S(1)}, u32[]{:S(2)}, u32[]{:S(2)}) async-start(bf16[8,32,896]{2,1,0:T(8,128)(2,1)} %broadcast_in_dim.10), calls=%async_computation.2 | async-start | bytes 917504 | tf_op jit(solution)/shard_map/all_to_all | solution.py:236
  89.4 8.8 %collective-permute-start = (bf16[4,4,16,128]{3,2,1,0:T(8,128)(2,1)S(1)}, bf16[4,4,16,128]{3,2,1,0:T(8,128)(2,1)S(1)}, u32[]{:S(2)}, u32[]{:S(2)}) collective-permute-start(bf16[4,4,16,128]{3,2,1,0:T(8,128)(2,1)S(1)} %bitcast.19), channel_id=1, source_target_pairs={{0,16},{16,32},{32,48},{48,64},{64,80},{80,96},{96,112},{112,128},... | collective-permute-start | bytes 196616 | tf_op jit(solution)/shard_map/ppermute | solution.py:217
  93.8 7.1 %collective-permute-start.1 = (bf16[4,4,16,128]{3,2,1,0:T(8,128)(2,1)S(1)}, bf16[4,4,16,128]{3,2,1,0:T(8,128)(2,1)S(1)}, u32[]{:S(2)}, u32[]{:S(2)}) collective-permute-start(bf16[4,4,16,128]{3,2,1,0:T(8,128)(2,1)S(1)} %bitcast.20), channel_id=1, source_target_pairs={{0,240},{16,0},{32,16},{48,32},{64,48},{80,64},{96,80},{112,96},{1... | collective-permute-start | bytes 196616 | tf_op jit(solution)/shard_map/ppermute | solution.py:218
  100.9 7.9 %collective-permute-start.2 = (bf16[12,4,4,128]{3,2,1,0:T(4,128)(2,1)S(1)}, bf16[12,4,4,128]{3,2,1,0:T(4,128)(2,1)S(1)}, u32[]{:S(2)}, u32[]{:S(2)}) collective-permute-start(bf16[12,4,4,128]{3,2,1,0:T(4,128)(2,1)S(1)} %get-tuple-element.27), channel_id=1, source_target_pairs={{0,2},{2,4},{4,6},{6,14},{14,12},{12,10},{10,8},{8,1},{1,3},{3,5},... | collective-permute-start | bytes 147464 | tf_op jit(solution)/shard_map/ppermute | solution.py:220
  104.6 6.0 %collective-permute-start.3 = (bf16[12,4,4,128]{3,2,1,0:T(4,128)(2,1)S(1)}, bf16[12,4,4,128]{3,2,1,0:T(4,128)(2,1)S(1)}, u32[]{:S(2)}, u32[]{:S(2)}) collective-permute-start(bf16[12,4,4,128]{3,2,1,0:T(4,128)(2,1)S(1)} %get-tuple-element.26), channel_id=1, source_target_pairs={{0,9},{2,0},{4,2},{6,4},{14,6},{12,14},{10,12},{8,10},{1,8},{3,1},... | collective-permute-start | bytes 147464 | tf_op jit(solution)/shard_map/ppermute | solution.py:221
  113.9 9.0 %collective-permute-start.4 = (bf16[4,4,16,128]{3,2,1,0:T(8,128)(2,1)S(1)}, bf16[4,4,16,128]{3,2,1,0:T(8,128)(2,1)S(1)}, u32[]{:S(2)}, u32[]{:S(2)}) collective-permute-start(bf16[4,4,16,128]{3,2,1,0:T(8,128)(2,1)S(1)} %get-tuple-element.13), channel_id=1, source_target_pairs={{0,16},{16,32},{32,48},{48,64},{64,80},{80,96},{96,112},{112,128},... | collective-permute-start | bytes 196616 | tf_op jit(solution)/shard_map/ppermute | solution.py:217
  117.3 7.5 %collective-permute-start.5 = (bf16[4,4,16,128]{3,2,1,0:T(8,128)(2,1)S(1)}, bf16[4,4,16,128]{3,2,1,0:T(8,128)(2,1)S(1)}, u32[]{:S(2)}, u32[]{:S(2)}) collective-permute-start(bf16[4,4,16,128]{3,2,1,0:T(8,128)(2,1)S(1)} %get-tuple-element.13), channel_id=1, source_target_pairs={{0,240},{16,0},{32,16},{48,32},{64,48},{80,64},{96,80},{112,96},{1... | collective-permute-start | bytes 196616 | tf_op jit(solution)/shard_map/ppermute | solution.py:218
  124.9 5.7 %collective-permute-start.6 = (bf16[12,4,4,128]{3,2,1,0:T(4,128)(2,1)S(1)}, bf16[12,4,4,128]{3,2,1,0:T(4,128)(2,1)S(1)}, u32[]{:S(2)}, u32[]{:S(2)}) collective-permute-start(bf16[12,4,4,128]{3,2,1,0:T(4,128)(2,1)S(1)} %get-tuple-element.25), channel_id=1, source_target_pairs={{0,2},{2,4},{4,6},{6,14},{14,12},{12,10},{10,8},{8,1},{1,3},{3,5},... | collective-permute-start | bytes 147464 | tf_op jit(solution)/shard_map/ppermute | solution.py:220
  128.6 6.0 %collective-permute-start.7 = (bf16[12,4,4,128]{3,2,1,0:T(4,128)(2,1)S(1)}, bf16[12,4,4,128]{3,2,1,0:T(4,128)(2,1)S(1)}, u32[]{:S(2)}, u32[]{:S(2)}) collective-permute-start(bf16[12,4,4,128]{3,2,1,0:T(4,128)(2,1)S(1)} %get-tuple-element.24), channel_id=1, source_target_pairs={{0,9},{2,0},{4,2},{6,4},{14,6},{12,14},{10,12},{8,10},{1,8},{3,1},... | collective-permute-start | bytes 147464 | tf_op jit(solution)/shard_map/ppermute | solution.py:221
  137.9 9.0 %collective-permute-start.8 = (bf16[4,4,16,128]{3,2,1,0:T(8,128)(2,1)S(1)}, bf16[4,4,16,128]{3,2,1,0:T(8,128)(2,1)S(1)}, u32[]{:S(2)}, u32[]{:S(2)}) collective-permute-start(bf16[4,4,16,128]{3,2,1,0:T(8,128)(2,1)S(1)} %get-tuple-element.16), channel_id=1, source_target_pairs={{0,16},{16,32},{32,48},{48,64},{64,80},{80,96},{96,112},{112,128},... | collective-permute-start | bytes 196616 | tf_op jit(solution)/shard_map/ppermute | solution.py:217
  141.9 7.1 %collective-permute-start.9 = (bf16[4,4,16,128]{3,2,1,0:T(8,128)(2,1)S(1)}, bf16[4,4,16,128]{3,2,1,0:T(8,128)(2,1)S(1)}, u32[]{:S(2)}, u32[]{:S(2)}) collective-permute-start(bf16[4,4,16,128]{3,2,1,0:T(8,128)(2,1)S(1)} %get-tuple-element.16), channel_id=1, source_target_pairs={{0,240},{16,0},{32,16},{48,32},{64,48},{80,64},{96,80},{112,96},{1... | collective-permute-start | bytes 196616 | tf_op jit(solution)/shard_map/ppermute | solution.py:218
  149.0 5.8 %collective-permute-start.10 = (bf16[12,4,4,128]{3,2,1,0:T(4,128)(2,1)S(1)}, bf16[12,4,4,128]{3,2,1,0:T(4,128)(2,1)S(1)}, u32[]{:S(2)}, u32[]{:S(2)}) collective-permute-start(bf16[12,4,4,128]{3,2,1,0:T(4,128)(2,1)S(1)} %get-tuple-element.23), channel_id=1, source_target_pairs={{0,2},{2,4},{4,6},{6,14},{14,12},{12,10},{10,8},{8,1},{1,3},{3,5},... | collective-permute-start | bytes 147464 | tf_op jit(solution)/shard_map/ppermute | solution.py:220
  152.3 6.0 %collective-permute-start.11 = (bf16[12,4,4,128]{3,2,1,0:T(4,128)(2,1)S(1)}, bf16[12,4,4,128]{3,2,1,0:T(4,128)(2,1)S(1)}, u32[]{:S(2)}, u32[]{:S(2)}) collective-permute-start(bf16[12,4,4,128]{3,2,1,0:T(4,128)(2,1)S(1)} %get-tuple-element.22), channel_id=1, source_target_pairs={{0,9},{2,0},{4,2},{6,4},{14,6},{12,14},{10,12},{8,10},{1,8},{3,1},... | collective-permute-start | bytes 147464 | tf_op jit(solution)/shard_map/ppermute | solution.py:221
  161.5 8.4 %collective-permute-start.12 = (bf16[4,4,16,128]{3,2,1,0:T(8,128)(2,1)S(1)}, bf16[4,4,16,128]{3,2,1,0:T(8,128)(2,1)S(1)}, u32[]{:S(2)}, u32[]{:S(2)}) collective-permute-start(bf16[4,4,16,128]{3,2,1,0:T(8,128)(2,1)S(1)} %get-tuple-element.19), channel_id=1, source_target_pairs={{0,16},{16,32},{32,48},{48,64},{64,80},{80,96},{96,112},{112,128},... | collective-permute-start | bytes 196616 | tf_op jit(solution)/shard_map/ppermute | solution.py:217
  164.7 7.1 %collective-permute-start.13 = (bf16[4,4,16,128]{3,2,1,0:T(8,128)(2,1)S(1)}, bf16[4,4,16,128]{3,2,1,0:T(8,128)(2,1)S(1)}, u32[]{:S(2)}, u32[]{:S(2)}) collective-permute-start(bf16[4,4,16,128]{3,2,1,0:T(8,128)(2,1)S(1)} %get-tuple-element.19), channel_id=1, source_target_pairs={{0,240},{16,0},{32,16},{48,32},{64,48},{80,64},{96,80},{112,96},{1... | collective-permute-start | bytes 196616 | tf_op jit(solution)/shard_map/ppermute | solution.py:218
  171.8 5.6 %collective-permute-start.14 = (bf16[12,4,4,128]{3,2,1,0:T(4,128)(2,1)S(1)}, bf16[12,4,4,128]{3,2,1,0:T(4,128)(2,1)S(1)}, u32[]{:S(2)}, u32[]{:S(2)}) collective-permute-start(bf16[12,4,4,128]{3,2,1,0:T(4,128)(2,1)S(1)} %get-tuple-element.21), channel_id=1, source_target_pairs={{0,2},{2,4},{4,6},{6,14},{14,12},{12,10},{10,8},{8,1},{1,3},{3,5},... | collective-permute-start | bytes 147464 | tf_op jit(solution)/shard_map/ppermute | solution.py:220
  175.1 6.0 %collective-permute-start.15 = (bf16[12,4,4,128]{3,2,1,0:T(4,128)(2,1)S(1)}, bf16[12,4,4,128]{3,2,1,0:T(4,128)(2,1)S(1)}, u32[]{:S(2)}, u32[]{:S(2)}) collective-permute-start(bf16[12,4,4,128]{3,2,1,0:T(4,128)(2,1)S(1)} %get-tuple-element.20), channel_id=1, source_target_pairs={{0,9},{2,0},{4,2},{6,4},{14,6},{12,14},{10,12},{8,10},{1,8},{3,1},... | collective-permute-start | bytes 147464 | tf_op jit(solution)/shard_map/ppermute | solution.py:221
where the time goes:
time: 197 us; the launch traced here: 196 us
  starting transfers between devices  108 us (55%)
  waiting for transfers between devices  52.9 us (27%)
  Pallas kernels  16 us (8%)
  blocking collectives  10.4 us (5%)
  local copies, waits for them, and re-layouts  8.06 us (4%)
    all_to_all x1, starting transfers between devices, on_device(): lax.all_to_all(jnp.broadcast_to(own, (gX, *own.shape)), 'gX', 0, 0, tiled...  44.6 us
    all_to_all x1, waiting for transfers between devices, on_device(): lax.all_to_all(jnp.broadcast_to(own, (gX, *own.shape)), 'gX', 0, 0, tiled...  19.4 us
    ppermute x4, starting transfers between devices, halos(): xh = lax.ppermute(block, 'gX', x_shift(-1))  17.2 us
    pallas_call x7, Pallas kernels, kernel_call(): pl.pallas_call(body, out_shape=[VMEM(o.shape, o.dtype) for o in outs], in...  16 us
    ppermute x4, starting transfers between devices, halos(): xl = lax.ppermute(block, 'gX', x_shift(1))  14.9 us
    ppermute x4, starting transfers between devices, halos(): zl = lax.ppermute(whole[:, :, ZB - HALO:], ('gs', 'gy', 'gz'), z_shift(1))  13.9 us
    ppermute x4, waiting for transfers between devices, halos(): zh = lax.ppermute(whole[:, :, :HALO], ('gs', 'gy', 'gz'), z_shift(-1))  12.9 us
    all_to_all x1, blocking collectives, on_device(): lax.all_to_all(res[0].reshape(members, 2, 2, ZB, 128), ('gs', 'gy'), 0, 0...  10.4 us
  transfers between devices with their start and end apart: 19, of which 14 were waited for; matrix products, arithmetic and copies ran while one was open for 0% of the time, Pallas kernels for 1%

commit v1 on v0

--- a/solution.py
+++ b/solution.py
@@ -7,6 +7,7 @@
 from jax.experimental import pallas as pl
 from jax.experimental.pallas import tpu as pltpu
 from jax.sharding import Mesh, PartitionSpec as P
+
 
 F32, BF16 = jnp.float32, jnp.bfloat16
 STEP = 0.25
@@ -25,17 +26,17 @@
     return path + [(a, 0) for a in range(rows - 1, 0, -1)]
 
 
-def kernel_call(body, outs, args, scratch=(), name=None):
+def kernel_call(body, outs, args, scratch=(), hbm_in=False, hbm_out=False):
     spec = pl.BlockSpec(memory_space=VMEM)
-    args = [pltpu.with_memory_space_constraint(v, VMEM) for v in args]
+    space = pltpu.HBM if hbm_in else VMEM
+    args = [pltpu.with_memory_space_constraint(v, space) for v in args]
     return pl.pallas_call(
         body,
-        out_shape=[VMEM(o.shape, o.dtype) for o in outs],
+        out_shape=outs if hbm_out else [VMEM(o.shape, o.dtype) for o in outs],
         in_specs=[spec] * len(args),
         out_specs=[spec] * len(outs),
         scratch_shapes=list(scratch),
         compiler_params=pltpu.CompilerParams(vmem_limit_bytes=LIMIT),
-        name=name,
     )(*args)
 
 
@@ -221,7 +222,7 @@
         zh = lax.ppermute(whole[:, :, :HALO], ("gs", "gy", "gz"), z_shift(-1))
         return xl, xh, zl, zh
 
-    def on_device(position, momentum, noise, filter_in, filter_out, bias):
+    def body(position, momentum, noise, filter_in, filter_out, bias):
         chans = position.shape[0]
         steps = noise.shape[0]
         members = gs * gy
@@ -242,7 +243,6 @@
             [jax.ShapeDtypeStruct((4, 12 * chans, 6 * chans), BF16)],
             (near.reshape(gy, chans, own.shape[1]),),
             [VMEM((2, 27 * chans, chans), F32)],
-            name="weights",
         )
         bias_row = jnp.concatenate([bias, bias])[None, :]
 
@@ -250,7 +250,8 @@
             functools.partial(spread_body, place),
             [jax.ShapeDtypeStruct((members, 2 + steps, 2, ZB, 128), F32)],
             (position, momentum, noise),
-            name="spread",
+            hbm_in=True,
+            hbm_out=True,
         )
         held = lax.all_to_all(spread, ("gs", "gy"), 0, 0, tiled=True)
 
@@ -273,9 +274,7 @@
                 outs = [jax.ShapeDtypeStruct((gs, gy, 2, 2, ZB, 128), F32)]
             else:
                 outs = [shape, shape, jax.ShapeDtypeStruct(block.shape, BF16)]
-            res = kernel_call(
-                functools.partial(gradient_body, kind, coef), outs, args, scratch, name="gradient"
-            )
+            res = kernel_call(functools.partial(gradient_body, kind, coef), outs, args, scratch)
             if kind != "last":
                 state, block = tuple(res[:2]), res[2]
         back = lax.all_to_all(
@@ -283,14 +282,14 @@
         )
         out = jax.ShapeDtypeStruct(position.shape, F32)
         return tuple(
-            kernel_call(functools.partial(collect_body, place), [out, out], (back,), name="collect")
+            kernel_call(functools.partial(collect_body, place), [out, out], (back,), hbm_out=True)
         )
 
     where = ("grp", "gX", "gs")
     lattice = P(None, where, "gy", "gz")
     filters = P(("gX", "gs"), "gy", None, None, None)
     return jax.shard_map(
-        on_device,
+        body,
         mesh=fine,
         in_specs=(lattice, lattice, P(None, None, where, "gy", "gz"), filters, filters, P()),
         out_specs=(lattice, lattice),

time: 197 us -> 197 us (level)
  local copies, waits for them, and re-layouts: 8.06 us -> 4.02 us
    unnamed x16 -> x8, local copies, waits for them, and re-layouts: 4.1 us -> 0.06 us
  transfers between devices with their start and end apart: 19 -> 19, of which waited for: 14 -> 14; matrix products, arithmetic and copies ran while one was open for 0% -> 0% of each run, Pallas kernels for 1% -> 2%
where the time goes in v1:
time: 197 us; the launch traced here: 196 us
  starting transfers between devices  108 us (55%)
  waiting for transfers between devices  54.6 us (28%)
  Pallas kernels  17.7 us (9%)
  blocking collectives  10.4 us (5%)
  local copies, waits for them, and re-layouts  4.02 us (2%)
    all_to_all x1, starting transfers between devices, body(): lax.all_to_all(jnp.broadcast_to(own, (gX, *own.shape)), 'gX', 0, 0, tiled...  44.6 us
    all_to_all x1, waiting for transfers between devices, body(): lax.all_to_all(jnp.broadcast_to(own, (gX, *own.shape)), 'gX', 0, 0, tiled...  21.1 us
    pallas_call x7, Pallas kernels, kernel_call(): pl.pallas_call(body, out_shape=outs if hbm_out else [VMEM(o.shape, o.dtyp...  17.7 us
    ppermute x4, starting transfers between devices, halos(): xh = lax.ppermute(block, 'gX', x_shift(-1))  17.2 us
    ppermute x4, starting transfers between devices, halos(): xl = lax.ppermute(block, 'gX', x_shift(1))  14.9 us
    ppermute x4, starting transfers between devices, halos(): zl = lax.ppermute(whole[:, :, ZB - HALO:], ('gs', 'gy', 'gz'), z_shift(1))  13.9 us
    ppermute x4, waiting for transfers between devices, halos(): zh = lax.ppermute(whole[:, :, :HALO], ('gs', 'gy', 'gz'), z_shift(-1))  12.9 us
    all_to_all x1, blocking collectives, body(): lax.all_to_all(res[0].reshape(members, 2, 2, ZB, 128), ('gs', 'gy'), 0, 0...  10.4 us
  transfers between devices with their start and end apart: 19, of which 14 were waited for; matrix products, arithmetic and copies ran while one was open for 0% of the time, Pallas kernels for 2%

profile of v1, /device:TPU:40, one launch (start us, length us, event | category | flops | bytes accessed | tf_op | source)
XLA Modules:
  0.0 195.6 jit_solution(6932207067308815407)
XLA Ops:
  0.6 0.7 copy.16
  1.4 0.7 copy.15
  2.3 0.7 broadcast_in_dim.9
  3.0 44.6 %all-to-all-start.1 = ((bf16[16,2,896]{2,1,0:T(2,128)(2,1)}), bf16[16,2,896]{2,1,0:T(2,128)(2,1)S(1)}, u32[]{:S(2)}, u32[]{:S(2)}) async-start(bf16[16,2,896]{2,1,0:T(2,128)(2,1)} %broadcast_in_dim.9), calls=%async_computation.1 | async-start | bytes 114688 | tf_op jit(solution)/shard_map/all_to_all | solution.py:233
  47.6 2.5 %shard_map.77 = f32[8,5,2,16,128]{4,3,2,1,0:T(8,128)} custom-call(f32[64,2,2,128]{3,2,1,0:T(2,128)} %q_ref.1, f32[64,2,2,128]{3,2,1,0:T(2,128)} %p_ref.1, bf16[3,64,2,2,128]{4,3,2,1,0:T(2,128)(2,1)} %n_ref.1), custom_call_target="tpu_custom_call" | custom-call | tf_op jit(solution)/shard_map/pallas_call | solution.py:33
  50.1 21.1 %all-to-all-done.1 = bf16[16,2,896]{2,1,0:T(2,128)(2,1)S(1)} async-done(((bf16[16,2,896]{2,1,0:T(2,128)(2,1)}), bf16[16,2,896]{2,1,0:T(2,128)(2,1)S(1)}, u32[]{:S(2)}, u32[]{:S(2)}) %all-to-all-start.1) | async-done | bytes 57376 | tf_op jit(solution)/shard_map/all_to_all | solution.py:233
  71.2 4.6 %all-to-all-start = ((f32[8,5,2,16,128]{4,3,2,1,0:T(8,128)}), f32[8,5,2,16,128]{4,3,2,1,0:T(8,128)S(1)}, u32[]{:S(2)}, u32[]{:S(2)}) async-start(f32[8,5,2,16,128]{4,3,2,1,0:T(8,128)} %shard_map.77), calls=%async_computation | async-start | bytes 1310720 | tf_op jit(solution)/shard_map/all_to_all | solution.py:256
  75.8 9.0 %all-to-all-done.refs_0_ = f32[8,5,2,16,128]{4,3,2,1,0:T(8,128)S(1)} async-done(((f32[8,5,2,16,128]{4,3,2,1,0:T(8,128)}), f32[8,5,2,16,128]{4,3,2,1,0:T(8,128)S(1)}, u32[]{:S(2)}, u32[]{:S(2)}) %all-to-all-start) | async-done | bytes 655392 | tf_op jit(solution)/shard_map/all_to_all | solution.py:256
  84.9 0.8 broadcast_in_dim.10
  85.7 3.7 %all-to-all-start.2 = ((bf16[8,32,896]{2,1,0:T(8,128)(2,1)}), bf16[8,32,896]{2,1,0:T(8,128)(2,1)S(1)}, u32[]{:S(2)}, u32[]{:S(2)}) async-start(bf16[8,32,896]{2,1,0:T(8,128)(2,1)} %broadcast_in_dim.10), calls=%async_computation.2 | async-start | bytes 917504 | tf_op jit(solution)/shard_map/all_to_all | solution.py:237
  89.4 4.4 %collective-permute-start = (bf16[4,4,16,128]{3,2,1,0:T(8,128)(2,1)S(1)}, bf16[4,4,16,128]{3,2,1,0:T(8,128)(2,1)S(1)}, u32[]{:S(2)}, u32[]{:S(2)}) collective-permute-start(bf16[4,4,16,128]{3,2,1,0:T(8,128)(2,1)S(1)} %bitcast.19), channel_id=1, source_target_pairs={{0,16},{16,32},{32,48},{48,64},{64,80},{80,96},{96,112},{112,128},... | collective-permute-start | bytes 196616 | tf_op jit(solution)/shard_map/ppermute | solution.py:218
  93.8 3.6 %collective-permute-start.1 = (bf16[4,4,16,128]{3,2,1,0:T(8,128)(2,1)S(1)}, bf16[4,4,16,128]{3,2,1,0:T(8,128)(2,1)S(1)}, u32[]{:S(2)}, u32[]{:S(2)}) collective-permute-start(bf16[4,4,16,128]{3,2,1,0:T(8,128)(2,1)S(1)} %bitcast.20), channel_id=1, source_target_pairs={{0,240},{16,0},{32,16},{48,32},{64,48},{80,64},{96,80},{112,96},{1... | collective-permute-start | bytes 196616 | tf_op jit(solution)/shard_map/ppermute | solution.py:219
  97.4 0.7 collective-permute-done.refs_1_
  98.2 2.7 %collective-permute-done.1.refs_2_ = bf16[4,4,16,128]{3,2,1,0:T(8,128)(2,1)S(1)} collective-permute-done((bf16[4,4,16,128]{3,2,1,0:T(8,128)(2,1)S(1)}, bf16[4,4,16,128]{3,2,1,0:T(8,128)(2,1)S(1)}, u32[]{:S(2)}, u32[]{:S(2)}) %collective-permute-start.1) | collective-permute-done | bytes 65568 | tf_op jit(solution)/shard_map/ppermute | solution.py:219
  100.9 3.7 %collective-permute-start.2 = (bf16[12,4,4,128]{3,2,1,0:T(4,128)(2,1)S(1)}, bf16[12,4,4,128]{3,2,1,0:T(4,128)(2,1)S(1)}, u32[]{:S(2)}, u32[]{:S(2)}) collective-permute-start(bf16[12,4,4,128]{3,2,1,0:T(4,128)(2,1)S(1)} %get-tuple-element.27), channel_id=1, source_target_pairs={{0,2},{2,4},{4,6},{6,14},{14,12},{12,10},{10,8},{8,1},{1,3},{3,5},... | collective-permute-start | bytes 147464 | tf_op jit(solution)/shard_map/ppermute | solution.py:221
  104.6 2.0 collective-permute-start.3
  106.7 0.2 reshape.36
  106.8 0.3 copy.12
  107.2 0.2 reshape.37.m_ref
  107.3 1.4 shard_map.78.refs_5_.refs_7_
  108.8 1.8 collective-permute-done.3.refs_4_
  110.6 3.2 %shard_map.79 = (f32[4,4,16,128]{3,2,1,0:T(8,128)S(1)}, f32[4,4,16,128]{3,2,1,0:T(8,128)S(1)}, bf16[4,4,16,128]{3,2,1,0:T(8,128)(2,1)S(1)}) custom-call(f32[8,5,2,16,128]{4,3,2,1,0:T(8,128)S(1)} %all-to-all-done.refs_0_, bf16[4,4,16,128]{3,2,1,0:T(8,128)(2,1)S(1)} %collective-permute-done.refs_1_, ...), custom_call_target="tpu_custom_call" | custom-call | tf_op jit(solution)/shard_map/pallas_call | solution.py:33
  113.9 3.4 %collective-permute-start.4 = (bf16[4,4,16,128]{3,2,1,0:T(8,128)(2,1)S(1)}, bf16[4,4,16,128]{3,2,1,0:T(8,128)(2,1)S(1)}, u32[]{:S(2)}, u32[]{:S(2)}) collective-permute-start(bf16[4,4,16,128]{3,2,1,0:T(8,128)(2,1)S(1)} %get-tuple-element.13), channel_id=1, source_target_pairs={{0,16},{16,32},{32,48},{48,64},{64,80},{80,96},{96,112},{112,128},... | collective-permute-start | bytes 196616 | tf_op jit(solution)/shard_map/ppermute | solution.py:218
  117.3 4.6 %collective-permute-start.5 = (bf16[4,4,16,128]{3,2,1,0:T(8,128)(2,1)S(1)}, bf16[4,4,16,128]{3,2,1,0:T(8,128)(2,1)S(1)}, u32[]{:S(2)}, u32[]{:S(2)}) collective-permute-start(bf16[4,4,16,128]{3,2,1,0:T(8,128)(2,1)S(1)} %get-tuple-element.13), channel_id=1, source_target_pairs={{0,240},{16,0},{32,16},{48,32},{64,48},{80,64},{96,80},{112,96},{1... | collective-permute-start | bytes 196616 | tf_op jit(solution)/shard_map/ppermute | solution.py:219
  121.9 1.0 collective-permute-done.4.refs_3_
  122.9 1.9 collective-permute-done.5.refs_4_
  124.9 3.8 %collective-permute-start.6 = (bf16[12,4,4,128]{3,2,1,0:T(4,128)(2,1)S(1)}, bf16[12,4,4,128]{3,2,1,0:T(4,128)(2,1)S(1)}, u32[]{:S(2)}, u32[]{:S(2)}) collective-permute-start(bf16[12,4,4,128]{3,2,1,0:T(4,128)(2,1)S(1)} %get-tuple-element.25), channel_id=1, source_target_pairs={{0,2},{2,4},{4,6},{6,14},{14,12},{12,10},{10,8},{8,1},{1,3},{3,5},... | collective-permute-start | bytes 147464 | tf_op jit(solution)/shard_map/ppermute | solution.py:221
  128.6 2.0 collective-permute-start.7
  130.6 4.0 %collective-permute-done.7.refs_6_ = bf16[12,4,4,128]{3,2,1,0:T(4,128)(2,1)S(1)} collective-permute-done((bf16[12,4,4,128]{3,2,1,0:T(4,128)(2,1)S(1)}, bf16[12,4,4,128]{3,2,1,0:T(4,128)(2,1)S(1)}, u32[]{:S(2)}, u32[]{:S(2)}) %collective-permute-start.7) | collective-permute-done | bytes 49184 | tf_op jit(solution)/shard_map/ppermute | solution.py:222
  134.7 3.2 %shard_map.80 = (f32[4,4,16,128]{3,2,1,0:T(8,128)S(1)}, f32[4,4,16,128]{3,2,1,0:T(8,128)S(1)}, bf16[4,4,16,128]{3,2,1,0:T(8,128)(2,1)S(1)}) custom-call(f32[8,5,2,16,128]{4,3,2,1,0:T(8,128)S(1)} %all-to-all-done.refs_0_, f32[4,4,16,128]{3,2,1,0:T(8,128)S(1)} %get-tuple-element.11.refs_1_, f32[4,4,16,128]{3,2,1,0:T(8,128)S(1)} %get-tuple-element.12.refs_2_, ...), custom_call_target="tpu_custom_call" | custom-call | tf_op jit(solution)/shard_map/pallas_call | solution.py:33
  137.9 3.9 %collective-permute-start.8 = (bf16[4,4,16,128]{3,2,1,0:T(8,128)(2,1)S(1)}, bf16[4,4,16,128]{3,2,1,0:T(8,128)(2,1)S(1)}, u32[]{:S(2)}, u32[]{:S(2)}) collective-permute-start(bf16[4,4,16,128]{3,2,1,0:T(8,128)(2,1)S(1)} %get-tuple-element.16), channel_id=1, source_target_pairs={{0,16},{16,32},{32,48},{48,64},{64,80},{80,96},{96,112},{112,128},... | collective-permute-start | bytes 196616 | tf_op jit(solution)/shard_map/ppermute | solution.py:218
  141.9 4.1 %collective-permute-start.9 = (bf16[4,4,16,128]{3,2,1,0:T(8,128)(2,1)S(1)}, bf16[4,4,16,128]{3,2,1,0:T(8,128)(2,1)S(1)}, u32[]{:S(2)}, u32[]{:S(2)}) collective-permute-start(bf16[4,4,16,128]{3,2,1,0:T(8,128)(2,1)S(1)} %get-tuple-element.16), channel_id=1, source_target_pairs={{0,240},{16,0},{32,16},{48,32},{64,48},{80,64},{96,80},{112,96},{1... | collective-permute-start | bytes 196616 | tf_op jit(solution)/shard_map/ppermute | solution.py:219
  145.9 1.0 collective-permute-done.8.refs_3_
  146.9 2.0 %collective-permute-done.9.refs_4_ = bf16[4,4,16,128]{3,2,1,0:T(8,128)(2,1)S(1)} collective-permute-done((bf16[4,4,16,128]{3,2,1,0:T(8,128)(2,1)S(1)}, bf16[4,4,16,128]{3,2,1,0:T(8,128)(2,1)S(1)}, u32[]{:S(2)}, u32[]{:S(2)}) %collective-permute-start.9) | collective-permute-done | bytes 65568 | tf_op jit(solution)/shard_map/ppermute | solution.py:219
  149.0 3.2 %collective-permute-start.10 = (bf16[12,4,4,128]{3,2,1,0:T(4,128)(2,1)S(1)}, bf16[12,4,4,128]{3,2,1,0:T(4,128)(2,1)S(1)}, u32[]{:S(2)}, u32[]{:S(2)}) collective-permute-start(bf16[12,4,4,128]{3,2,1,0:T(4,128)(2,1)S(1)} %get-tuple-element.23), channel_id=1, source_target_pairs={{0,2},{2,4},{4,6},{6,14},{14,12},{12,10},{10,8},{8,1},{1,3},{3,5},... | collective-permute-start | bytes 147464 | tf_op jit(solution)/shard_map/ppermute | solution.py:221
  152.3 2.6 %collective-permute-start.11 = (bf16[12,4,4,128]{3,2,1,0:T(4,128)(2,1)S(1)}, bf16[12,4,4,128]{3,2,1,0:T(4,128)(2,1)S(1)}, u32[]{:S(2)}, u32[]{:S(2)}) collective-permute-start(bf16[12,4,4,128]{3,2,1,0:T(4,128)(2,1)S(1)} %get-tuple-element.22), channel_id=1, source_target_pairs={{0,9},{2,0},{4,2},{6,4},{14,6},{12,14},{10,12},{8,10},{1,8},{3,1},... | collective-permute-start | bytes 147464 | tf_op jit(solution)/shard_map/ppermute | solution.py:222
  154.8 3.4 %collective-permute-done.11.refs_6_ = bf16[12,4,4,128]{3,2,1,0:T(4,128)(2,1)S(1)} collective-permute-done((bf16[12,4,4,128]{3,2,1,0:T(4,128)(2,1)S(1)}, bf16[12,4,4,128]{3,2,1,0:T(4,128)(2,1)S(1)}, u32[]{:S(2)}, u32[]{:S(2)}) %collective-permute-start.11) | collective-permute-done | bytes 49184 | tf_op jit(solution)/shard_map/ppermute | solution.py:222
  158.3 3.2 %shard_map.81 = (f32[4,4,16,128]{3,2,1,0:T(8,128)S(1)}, f32[4,4,16,128]{3,2,1,0:T(8,128)S(1)}, bf16[4,4,16,128]{3,2,1,0:T(8,128)(2,1)S(1)}) custom-call(f32[8,5,2,16,128]{4,3,2,1,0:T(8,128)S(1)} %all-to-all-done.refs_0_, f32[4,4,16,128]{3,2,1,0:T(8,128)S(1)} %get-tuple-element.14.refs_1_, f32[4,4,16,128]{3,2,1,0:T(8,128)S(1)} %get-tuple-element.15.refs_2_, ...), custom_call_target="tpu_custom_call" | custom-call | tf_op jit(solution)/shard_map/pallas_call | solution.py:33
  161.5 3.2 %collective-permute-start.12 = (bf16[4,4,16,128]{3,2,1,0:T(8,128)(2,1)S(1)}, bf16[4,4,16,128]{3,2,1,0:T(8,128)(2,1)S(1)}, u32[]{:S(2)}, u32[]{:S(2)}) collective-permute-start(bf16[4,4,16,128]{3,2,1,0:T(8,128)(2,1)S(1)} %get-tuple-element.19), channel_id=1, source_target_pairs={{0,16},{16,32},{32,48},{48,64},{64,80},{80,96},{96,112},{112,128},... | collective-permute-start | bytes 196616 | tf_op jit(solution)/shard_map/ppermute | solution.py:218
  164.7 4.9 %collective-permute-start.13 = (bf16[4,4,16,128]{3,2,1,0:T(8,128)(2,1)S(1)}, bf16[4,4,16,128]{3,2,1,0:T(8,128)(2,1)S(1)}, u32[]{:S(2)}, u32[]{:S(2)}) collective-permute-start(bf16[4,4,16,128]{3,2,1,0:T(8,128)(2,1)S(1)} %get-tuple-element.19), channel_id=1, source_target_pairs={{0,240},{16,0},{32,16},{48,32},{64,48},{80,64},{96,80},{112,96},{1... | collective-permute-start | bytes 196616 | tf_op jit(solution)/shard_map/ppermute | solution.py:219
  169.6 0.4 collective-permute-done.12.refs_3_
  169.9 1.8 collective-permute-done.13.refs_4_
  171.8 3.2 %collective-permute-start.14 = (bf16[12,4,4,128]{3,2,1,0:T(4,128)(2,1)S(1)}, bf16[12,4,4,128]{3,2,1,0:T(4,128)(2,1)S(1)}, u32[]{:S(2)}, u32[]{:S(2)}) collective-permute-start(bf16[12,4,4,128]{3,2,1,0:T(4,128)(2,1)S(1)} %get-tuple-element.21), channel_id=1, source_target_pairs={{0,2},{2,4},{4,6},{6,14},{14,12},{12,10},{10,8},{8,1},{1,3},{3,5},... | collective-permute-start | bytes 147464 | tf_op jit(solution)/shard_map/ppermute | solution.py:221
  175.1 2.4 %collective-permute-start.15 = (bf16[12,4,4,128]{3,2,1,0:T(4,128)(2,1)S(1)}, bf16[12,4,4,128]{3,2,1,0:T(4,128)(2,1)S(1)}, u32[]{:S(2)}, u32[]{:S(2)}) collective-permute-start(bf16[12,4,4,128]{3,2,1,0:T(4,128)(2,1)S(1)} %get-tuple-element.20), channel_id=1, source_target_pairs={{0,9},{2,0},{4,2},{6,4},{14,6},{12,14},{10,12},{8,10},{1,8},{3,1},... | collective-permute-start | bytes 147464 | tf_op jit(solution)/shard_map/ppermute | solution.py:222
  177.5 3.6 %collective-permute-done.15.refs_6_ = bf16[12,4,4,128]{3,2,1,0:T(4,128)(2,1)S(1)} collective-permute-done((bf16[12,4,4,128]{3,2,1,0:T(4,128)(2,1)S(1)}, bf16[12,4,4,128]{3,2,1,0:T(4,128)(2,1)S(1)}, u32[]{:S(2)}, u32[]{:S(2)}) %collective-permute-start.15) | collective-permute-done | bytes 49184 | tf_op jit(solution)/shard_map/ppermute | solution.py:222
  181.1 3.2 %shard_map.82 = f32[2,4,2,2,16,128]{5,4,3,2,1,0:T(8,128)S(1)} custom-call(f32[8,5,2,16,128]{4,3,2,1,0:T(8,128)S(1)} %all-to-all-done.refs_0_, f32[4,4,16,128]{3,2,1,0:T(8,128)S(1)} %get-tuple-element.17.refs_1_, f32[4,4,16,128]{3,2,1,0:T(8,128)S(1)} %get-tuple-element.18.refs_2_, bf16[4,4,16,128]{3,2,1,0:T(8,128)(2,1)S(1)} %collective-permute-done.12.refs_3_, ...), custom_call_target="tpu_custom_call" | custom-call | tf_op jit(solution)/shard_map/pallas_call | solution.py:33
  184.3 10.4 %all_to_all.20.in_ref = f32[8,2,2,16,128]{4,3,2,1,0:T(8,128)S(1)} all-to-all(f32[8,2,2,16,128]{4,3,2,1,0:T(8,128)S(1)} %bitcast.16), channel_id=1, replica_groups=mesh['grp'=2,'gX'=16,'gs'=2,'gy'=4,'gz'=2] {'gs','gy'}, dimensions={0} | all-to-all | bytes 524288 | tf_op jit(solution)/shard_map/all_to_all | solution.py:280
  194.7 0.9 shard_map.83
  (27 shorter events, 0.7 us)
Async XLA Ops:
  2.2 104.3 %copy-start = (f32[64]{0:T(128)S(1)}, f32[64]{0:T(128)}, u32[]{:S(2)}) copy-start(f32[64]{0:T(128)} %param.11) | copy-start | bytes 772
  3.0 68.2 %all-to-all-start.1 = ((bf16[16,2,896]{2,1,0:T(2,128)(2,1)}), bf16[16,2,896]{2,1,0:T(2,128)(2,1)S(1)}, u32[]{:S(2)}, u32[]{:S(2)}) async-start(bf16[16,2,896]{2,1,0:T(2,128)(2,1)} %broadcast_in_dim.9), calls=%async_computation.1 | async-start | bytes 114688 | tf_op jit(solution)/shard_map/all_to_all | solution.py:233
  71.2 13.7 %all-to-all-start = ((f32[8,5,2,16,128]{4,3,2,1,0:T(8,128)}), f32[8,5,2,16,128]{4,3,2,1,0:T(8,128)S(1)}, u32[]{:S(2)}, u32[]{:S(2)}) async-start(f32[8,5,2,16,128]{4,3,2,1,0:T(8,128)} %shard_map.77), calls=%async_computation | async-start | bytes 1310720 | tf_op jit(solution)/shard_map/all_to_all | solution.py:256
  85.7 21.0 %all-to-all-start.2 = ((bf16[8,32,896]{2,1,0:T(8,128)(2,1)}), bf16[8,32,896]{2,1,0:T(8,128)(2,1)S(1)}, u32[]{:S(2)}, u32[]{:S(2)}) async-start(bf16[8,32,896]{2,1,0:T(8,128)(2,1)} %broadcast_in_dim.10), calls=%async_computation.2 | async-start | bytes 917504 | tf_op jit(solution)/shard_map/all_to_all | solution.py:237
  89.4 8.8 %collective-permute-start = (bf16[4,4,16,128]{3,2,1,0:T(8,128)(2,1)S(1)}, bf16[4,4,16,128]{3,2,1,0:T(8,128)(2,1)S(1)}, u32[]{:S(2)}, u32[]{:S(2)}) collective-permute-start(bf16[4,4,16,128]{3,2,1,0:T(8,128)(2,1)S(1)} %bitcast.19), channel_id=1, source_target_pairs={{0,16},{16,32},{32,48},{48,64},{64,80},{80,96},{96,112},{112,128},... | collective-permute-start | bytes 196616 | tf_op jit(solution)/shard_map/ppermute | solution.py:218
  93.8 7.1 %collective-permute-start.1 = (bf16[4,4,16,128]{3,2,1,0:T(8,128)(2,1)S(1)}, bf16[4,4,16,128]{3,2,1,0:T(8,128)(2,1)S(1)}, u32[]{:S(2)}, u32[]{:S(2)}) collective-permute-start(bf16[4,4,16,128]{3,2,1,0:T(8,128)(2,1)S(1)} %bitcast.20), channel_id=1, source_target_pairs={{0,240},{16,0},{32,16},{48,32},{64,48},{80,64},{96,80},{112,96},{1... | collective-permute-start | bytes 196616 | tf_op jit(solution)/shard_map/ppermute | solution.py:219
  100.9 7.9 %collective-permute-start.2 = (bf16[12,4,4,128]{3,2,1,0:T(4,128)(2,1)S(1)}, bf16[12,4,4,128]{3,2,1,0:T(4,128)(2,1)S(1)}, u32[]{:S(2)}, u32[]{:S(2)}) collective-permute-start(bf16[12,4,4,128]{3,2,1,0:T(4,128)(2,1)S(1)} %get-tuple-element.27), channel_id=1, source_target_pairs={{0,2},{2,4},{4,6},{6,14},{14,12},{12,10},{10,8},{8,1},{1,3},{3,5},... | collective-permute-start | bytes 147464 | tf_op jit(solution)/shard_map/ppermute | solution.py:221
  104.6 6.0 %collective-permute-start.3 = (bf16[12,4,4,128]{3,2,1,0:T(4,128)(2,1)S(1)}, bf16[12,4,4,128]{3,2,1,0:T(4,128)(2,1)S(1)}, u32[]{:S(2)}, u32[]{:S(2)}) collective-permute-start(bf16[12,4,4,128]{3,2,1,0:T(4,128)(2,1)S(1)} %get-tuple-element.26), channel_id=1, source_target_pairs={{0,9},{2,0},{4,2},{6,4},{14,6},{12,14},{10,12},{8,10},{1,8},{3,1},... | collective-permute-start | bytes 147464 | tf_op jit(solution)/shard_map/ppermute | solution.py:222
  113.9 9.0 %collective-permute-start.4 = (bf16[4,4,16,128]{3,2,1,0:T(8,128)(2,1)S(1)}, bf16[4,4,16,128]{3,2,1,0:T(8,128)(2,1)S(1)}, u32[]{:S(2)}, u32[]{:S(2)}) collective-permute-start(bf16[4,4,16,128]{3,2,1,0:T(8,128)(2,1)S(1)} %get-tuple-element.13), channel_id=1, source_target_pairs={{0,16},{16,32},{32,48},{48,64},{64,80},{80,96},{96,112},{112,128},... | collective-permute-start | bytes 196616 | tf_op jit(solution)/shard_map/ppermute | solution.py:218
  117.3 7.5 %collective-permute-start.5 = (bf16[4,4,16,128]{3,2,1,0:T(8,128)(2,1)S(1)}, bf16[4,4,16,128]{3,2,1,0:T(8,128)(2,1)S(1)}, u32[]{:S(2)}, u32[]{:S(2)}) collective-permute-start(bf16[4,4,16,128]{3,2,1,0:T(8,128)(2,1)S(1)} %get-tuple-element.13), channel_id=1, source_target_pairs={{0,240},{16,0},{32,16},{48,32},{64,48},{80,64},{96,80},{112,96},{1... | collective-permute-start | bytes 196616 | tf_op jit(solution)/shard_map/ppermute | solution.py:219
  124.9 5.7 %collective-permute-start.6 = (bf16[12,4,4,128]{3,2,1,0:T(4,128)(2,1)S(1)}, bf16[12,4,4,128]{3,2,1,0:T(4,128)(2,1)S(1)}, u32[]{:S(2)}, u32[]{:S(2)}) collective-permute-start(bf16[12,4,4,128]{3,2,1,0:T(4,128)(2,1)S(1)} %get-tuple-element.25), channel_id=1, source_target_pairs={{0,2},{2,4},{4,6},{6,14},{14,12},{12,10},{10,8},{8,1},{1,3},{3,5},... | collective-permute-start | bytes 147464 | tf_op jit(solution)/shard_map/ppermute | solution.py:221
  128.6 6.0 %collective-permute-start.7 = (bf16[12,4,4,128]{3,2,1,0:T(4,128)(2,1)S(1)}, bf16[12,4,4,128]{3,2,1,0:T(4,128)(2,1)S(1)}, u32[]{:S(2)}, u32[]{:S(2)}) collective-permute-start(bf16[12,4,4,128]{3,2,1,0:T(4,128)(2,1)S(1)} %get-tuple-element.24), channel_id=1, source_target_pairs={{0,9},{2,0},{4,2},{6,4},{14,6},{12,14},{10,12},{8,10},{1,8},{3,1},... | collective-permute-start | bytes 147464 | tf_op jit(solution)/shard_map/ppermute | solution.py:222
  137.9 9.0 %collective-permute-start.8 = (bf16[4,4,16,128]{3,2,1,0:T(8,128)(2,1)S(1)}, bf16[4,4,16,128]{3,2,1,0:T(8,128)(2,1)S(1)}, u32[]{:S(2)}, u32[]{:S(2)}) collective-permute-start(bf16[4,4,16,128]{3,2,1,0:T(8,128)(2,1)S(1)} %get-tuple-element.16), channel_id=1, source_target_pairs={{0,16},{16,32},{32,48},{48,64},{64,80},{80,96},{96,112},{112,128},... | collective-permute-start | bytes 196616 | tf_op jit(solution)/shard_map/ppermute | solution.py:218
  141.9 7.1 %collective-permute-start.9 = (bf16[4,4,16,128]{3,2,1,0:T(8,128)(2,1)S(1)}, bf16[4,4,16,128]{3,2,1,0:T(8,128)(2,1)S(1)}, u32[]{:S(2)}, u32[]{:S(2)}) collective-permute-start(bf16[4,4,16,128]{3,2,1,0:T(8,128)(2,1)S(1)} %get-tuple-element.16), channel_id=1, source_target_pairs={{0,240},{16,0},{32,16},{48,32},{64,48},{80,64},{96,80},{112,96},{1... | collective-permute-start | bytes 196616 | tf_op jit(solution)/shard_map/ppermute | solution.py:219
  149.0 5.8 %collective-permute-start.10 = (bf16[12,4,4,128]{3,2,1,0:T(4,128)(2,1)S(1)}, bf16[12,4,4,128]{3,2,1,0:T(4,128)(2,1)S(1)}, u32[]{:S(2)}, u32[]{:S(2)}) collective-permute-start(bf16[12,4,4,128]{3,2,1,0:T(4,128)(2,1)S(1)} %get-tuple-element.23), channel_id=1, source_target_pairs={{0,2},{2,4},{4,6},{6,14},{14,12},{12,10},{10,8},{8,1},{1,3},{3,5},... | collective-permute-start | bytes 147464 | tf_op jit(solution)/shard_map/ppermute | solution.py:221
  152.3 6.0 %collective-permute-start.11 = (bf16[12,4,4,128]{3,2,1,0:T(4,128)(2,1)S(1)}, bf16[12,4,4,128]{3,2,1,0:T(4,128)(2,1)S(1)}, u32[]{:S(2)}, u32[]{:S(2)}) collective-permute-start(bf16[12,4,4,128]{3,2,1,0:T(4,128)(2,1)S(1)} %get-tuple-element.22), channel_id=1, source_target_pairs={{0,9},{2,0},{4,2},{6,4},{14,6},{12,14},{10,12},{8,10},{1,8},{3,1},... | collective-permute-start | bytes 147464 | tf_op jit(solution)/shard_map/ppermute | solution.py:222
  161.5 8.4 %collective-permute-start.12 = (bf16[4,4,16,128]{3,2,1,0:T(8,128)(2,1)S(1)}, bf16[4,4,16,128]{3,2,1,0:T(8,128)(2,1)S(1)}, u32[]{:S(2)}, u32[]{:S(2)}) collective-permute-start(bf16[4,4,16,128]{3,2,1,0:T(8,128)(2,1)S(1)} %get-tuple-element.19), channel_id=1, source_target_pairs={{0,16},{16,32},{32,48},{48,64},{64,80},{80,96},{96,112},{112,128},... | collective-permute-start | bytes 196616 | tf_op jit(solution)/shard_map/ppermute | solution.py:218
  164.7 7.1 %collective-permute-start.13 = (bf16[4,4,16,128]{3,2,1,0:T(8,128)(2,1)S(1)}, bf16[4,4,16,128]{3,2,1,0:T(8,128)(2,1)S(1)}, u32[]{:S(2)}, u32[]{:S(2)}) collective-permute-start(bf16[4,4,16,128]{3,2,1,0:T(8,128)(2,1)S(1)} %get-tuple-element.19), channel_id=1, source_target_pairs={{0,240},{16,0},{32,16},{48,32},{64,48},{80,64},{96,80},{112,96},{1... | collective-permute-start | bytes 196616 | tf_op jit(solution)/shard_map/ppermute | solution.py:219
  171.8 5.6 %collective-permute-start.14 = (bf16[12,4,4,128]{3,2,1,0:T(4,128)(2,1)S(1)}, bf16[12,4,4,128]{3,2,1,0:T(4,128)(2,1)S(1)}, u32[]{:S(2)}, u32[]{:S(2)}) collective-permute-start(bf16[12,4,4,128]{3,2,1,0:T(4,128)(2,1)S(1)} %get-tuple-element.21), channel_id=1, source_target_pairs={{0,2},{2,4},{4,6},{6,14},{14,12},{12,10},{10,8},{8,1},{1,3},{3,5},... | collective-permute-start | bytes 147464 | tf_op jit(solution)/shard_map/ppermute | solution.py:221
  175.1 6.0 %collective-permute-start.15 = (bf16[12,4,4,128]{3,2,1,0:T(4,128)(2,1)S(1)}, bf16[12,4,4,128]{3,2,1,0:T(4,128)(2,1)S(1)}, u32[]{:S(2)}, u32[]{:S(2)}) collective-permute-start(bf16[12,4,4,128]{3,2,1,0:T(4,128)(2,1)S(1)} %get-tuple-element.20), channel_id=1, source_target_pairs={{0,9},{2,0},{4,2},{6,4},{14,6},{12,14},{10,12},{8,10},{1,8},{3,1},... | collective-permute-start | bytes 147464 | tf_op jit(solution)/shard_map/ppermute | solution.py:222

commit v2 on v1

--- a/solution.py
+++ b/solution.py
@@ -13,7 +13,6 @@
 STEP = 0.25
 XB, ZB = 4, 16
 HALO = 4
-PITCH = ZB + 2 * HALO
 VMEM = pltpu.VMEM
 LIMIT = 24 * 1024 * 1024
 
@@ -105,8 +104,31 @@
                 place(f + 2, taps - 1 - tap - i, adj[:, part].astype(BF16))
 
 
-def gradient_body(kind, coef, *refs):
-    decay, kick = coef
+def strips(r):
+    high = r.astype(BF16).astype(F32)
+    low = r - high
+    upper = lax.broadcasted_iota(jnp.int32, (8, 128), 0) < HALO
+    first = jnp.where(upper, high[:8], pltpu.roll(low[:8], HALO, 0))
+    last = jnp.where(upper, pltpu.roll(high[-8:], HALO, 0), low[-8:])
+    return first.astype(BF16), last.astype(BF16)
+
+
+def ahead(coef, turns, q, p, n):
+    decay, kick, half = coef
+    c = turns * half * half * (1.0 + decay)
+    return (1.0 - c) * q + half * (1.0 + decay) * p + half * kick * n, c
+
+
+def prepare_body(coef, r_ref, block_ref, rl_ref, rh_ref):
+    for x in range(XB):
+        for j in range(4):
+            q, p, n = (r_ref[x // 2 * 4 + j, k, x % 2] for k in range(3))
+            block_ref[x, j] = q.astype(BF16)
+            rl_ref[x, j], rh_ref[x, j] = strips(ahead(coef, 1, q, p, n)[0])
+
+
+def gradient_body(kind, wide, coef, *refs):
+    decay, kick, half = coef
     it = iter(refs)
     r_ref = next(it)
     if kind == "first":
@@ -116,59 +138,70 @@
         q_ref, p_ref = next(it), next(it)
         q_of = lambda x, j: q_ref[x, j]
         p_of = lambda x, j: p_ref[x, j]
-    xl_ref, xh_ref, zl_ref, zh_ref, w_ref, bias_ref = (next(it) for _ in range(6))
+    step_at = {"first": 0}.get(kind, kind)
+    noise_of = lambda x, j, k: r_ref[x // 2 * 4 + j, 2 + k, x % 2]
+    if wide:
+        xl_ref, xh_ref, zl_ref, zh_ref, w_ref, bias_ref = (next(it) for _ in range(6))
+    else:
+        xl_ref, xh_ref, own_ref, w_ref, bias_ref = (next(it) for _ in range(5))
     if kind == "last":
         out_ref = next(it)
     else:
         qo_ref, po_ref, qb_ref = (next(it) for _ in range(3))
+        if not wide:
+            rl_ref, rh_ref = next(it), next(it)
     buf, rows_ref, act = (next(it) for _ in range(3))
-    step_at = {"first": 0}.get(kind, kind)
-
+
+    pad = 2 * HALO if wide else HALO
+    pitch = ZB + 2 * pad
     x_all = XB + 2 * HALO
-    lo, hi = 8 + HALO, 8 + HALO + ZB
+    lo, hi, end = 8 + pad, 8 + pad + ZB, 8 + pitch
     edge = jnp.zeros((x_all, 4, 8, 128), F32)
     buf[:, :, 0:8, :] = edge
-    buf[:, :, 8 + PITCH : 16 + PITCH, :] = edge
-    buf[0:HALO, :, lo:hi, :] = xl_ref[...].astype(F32)
-    buf[HALO + XB :, :, lo:hi, :] = xh_ref[...].astype(F32)
-    for x in range(XB):
-        for j in range(4):
-            buf[HALO + x, j, lo:hi, :] = q_of(x, j)
-    buf[:, :, 8:lo, :] = zl_ref[...].astype(F32)
-    buf[:, :, hi : 8 + PITCH, :] = zh_ref[...].astype(F32)
+    buf[:, :, end : end + 8, :] = edge
+    if wide:
+        buf[0:HALO, :, lo:hi, :] = xl_ref[...].astype(F32)
+        buf[HALO + XB :, :, lo:hi, :] = xh_ref[...].astype(F32)
+        for x in range(XB):
+            for j in range(4):
+                buf[HALO + x, j, lo:hi, :] = q_of(x, j)
+        buf[:, :, 8:lo, :] = zl_ref[0:x_all].astype(F32)
+        buf[:, :, hi:end, :] = zh_ref[0:x_all].astype(F32)
+    else:
+        buf[0:HALO, :, 8:end, :] = xl_ref[...].astype(F32)
+        buf[HALO : HALO + XB, :, 8:end, :] = own_ref[...].astype(F32)
+        buf[HALO + XB :, :, 8:end, :] = xh_ref[...].astype(F32)
 
     def conv(x_in, w, use):
-        n = x_in * PITCH
+        n = x_in * pitch
         for j in range(4):
             for c in range(3):
-                v = buf[0:x_in, j, 7 + c : 7 + c + PITCH, :].reshape(n, 128).astype(BF16)
+                v = buf[0:x_in, j, 7 + c : 7 + c + pitch, :].reshape(n, 128).astype(BF16)
                 rows_ref[0:n, (j * 3 + c) * 128 : (j * 3 + c + 1) * 128] = v
                 if j == 0:
                     rows_ref[0:n, (12 + c) * 128 : (13 + c) * 128] = v
         x_out = x_in - 2
-        m = x_out * PITCH
+        m = x_out * pitch
         for p in range(4):
             t = jnp.dot(
                 rows_ref[0:n, 384 * p : 384 * p + 768], w_ref[w], preferred_element_type=F32
             )
-            o = t[0:m, 0:128] + t[PITCH : PITCH + m, 128:256] + t[2 * PITCH :, 256:384]
-            use(p, o.reshape(x_out, PITCH, 128))
+            o = t[0:m, 0:128] + t[pitch : pitch + m, 128:256] + t[2 * pitch :, 256:384]
+            use(p, o.reshape(x_out, pitch, 128))
 
     def hidden(p, h):
         t = jnp.tanh(h + bias_ref[...])
         act[:, p] = 1.0 - t * t
-        buf[0 : XB + 6, p, 8 : 8 + PITCH, :] = t
+        buf[0 : XB + 6, p, 8:end, :] = t
 
     def second(p, h):
-        buf[0 : XB + 4, p, 8 : 8 + PITCH, :] = h
+        buf[0 : XB + 4, p, 8:end, :] = h
 
     def back(p, g):
-        buf[0 : XB + 2, p, 8 : 8 + PITCH, :] = g * act[2 : XB + 4, (p + 1) % 4]
-
-    half = 0.5 * STEP
+        buf[0 : XB + 2, p, 8:end, :] = g * act[2 : XB + 4, (p + 1) % 4]
 
     def final(p, g):
-        buf[0:XB, p, 8 : 8 + PITCH, :] = g
+        buf[0:XB, p, 8:end, :] = g
         j = (p + 2) % 4
         for x in range(XB):
             q = q_of(x, j)
@@ -181,11 +214,23 @@
             if kind != "first":
                 mom = mom - half * force
             q = q + half * mom
-            mom = decay * mom + kick * r_ref[x // 2 * 4 + j, 2 + step_at, x % 2]
+            mom = decay * mom + kick * noise_of(x, j, step_at)
             q = q + half * mom
             qo_ref[x, j] = q
             po_ref[x, j] = mom
-            qb_ref[x, j] = q.astype(BF16)
+            if not wide:
+                qb_ref[x, j] = q.astype(BF16)
+                r, _ = ahead(coef, 2, q, mom, noise_of(x, j, step_at + 1))
+                rl_ref[x, j], rh_ref[x, j] = strips(r)
+                continue
+            c = (1 if kind == "first" else 2) * half * half * (1.0 + decay)
+            below, above = slice(lo - HALO, lo), slice(hi, hi + HALO)
+            for ref, at in ((zl_ref, below), (zh_ref, above)):
+                r = ref[x_all + x, j].astype(F32)
+                r = r + pltpu.roll(r, HALO, 0)
+                buf[x, p, at, :] = r[:HALO] - c * buf[x, p, at, :]
+            buf[x, p, lo:hi, :] = q
+            qb_ref[x, j] = buf[x, p, lo - HALO : hi + HALO, :].astype(BF16)
 
     conv(XB + 8, 0, hidden)
     conv(XB + 6, 1, second)
@@ -214,12 +259,18 @@
     decay = math.exp(-0.25)
     kick = math.sqrt(1.0 - decay * decay)
 
-    def halos(block):
+    def along_x(block):
         xl = lax.ppermute(block, "gX", x_shift(1))
         xh = lax.ppermute(block, "gX", x_shift(-1))
+        return xl, xh
+
+    def along_both(block, rl, rh):
+        xl, xh = along_x(block)
         whole = jnp.concatenate([xl, block, xh], axis=0)
-        zl = lax.ppermute(whole[:, :, ZB - HALO :], ("gs", "gy", "gz"), z_shift(1))
-        zh = lax.ppermute(whole[:, :, :HALO], ("gs", "gy", "gz"), z_shift(-1))
+        up = jnp.concatenate([whole[:, :, ZB - 2 * HALO :], rh], axis=0)
+        down = jnp.concatenate([whole[:, :, : 2 * HALO], rl], axis=0)
+        zl = lax.ppermute(up, ("gs", "gy", "gz"), z_shift(1))
+        zh = lax.ppermute(down, ("gs", "gy", "gz"), z_shift(-1))
         return xl, xh, zl, zh
 
     def body(position, momentum, noise, filter_in, filter_out, bias):
@@ -255,28 +306,36 @@
         )
         held = lax.all_to_all(spread, ("gs", "gy"), 0, 0, tiled=True)
 
-        start = held[:, 0].reshape(gs, gy, 2, ZB, 128).transpose(0, 2, 1, 3, 4)
-        block = start.reshape(XB, gy, ZB, 128).astype(BF16)
-
-        shape = jax.ShapeDtypeStruct(block.shape, F32)
-        scratch = (
-            VMEM((XB + 8, gy, PITCH + 16, 128), F32),
-            VMEM(((XB + 8) * PITCH, 15 * 128), BF16),
-            VMEM((XB + 6, gy, PITCH, 128), F32),
-        )
-        coef = (decay, kick)
+        coef = (decay, kick, 0.5 * STEP)
+        tall = (XB, gy, ZB, 128)
+        state32 = jax.ShapeDtypeStruct(tall, F32)
+        block16 = jax.ShapeDtypeStruct(tall, BF16)
+        grown16 = jax.ShapeDtypeStruct((XB, gy, ZB + 2 * HALO, 128), BF16)
+        strip16 = jax.ShapeDtypeStruct((XB, gy, 2 * HALO, 128), BF16)
+        block, *ends = kernel_call(
+            functools.partial(prepare_body, coef), [block16, strip16, strip16], (held,)
+        )
         state = ()
         for k in range(steps + 1):
             kind = "first" if k == 0 else "last" if k == steps else k
-            edges = halos(block)
-            args = (held, *state, *edges, weights, bias_row)
+            wide = k % 2 == 0
+            edges = along_both(block, *ends) if wide else (*along_x(block), block)
+            outs = [state32, state32, grown16] if wide else [state32, state32, block16, strip16, strip16]
             if kind == "last":
                 outs = [jax.ShapeDtypeStruct((gs, gy, 2, 2, ZB, 128), F32)]
-            else:
-                outs = [shape, shape, jax.ShapeDtypeStruct(block.shape, BF16)]
-            res = kernel_call(functools.partial(gradient_body, kind, coef), outs, args, scratch)
+            pitch = ZB + (4 if wide else 2) * HALO
+            res = kernel_call(
+                functools.partial(gradient_body, kind, wide, coef),
+                outs,
+                (held, *state, *edges, weights, bias_row),
+                (
+                    VMEM((XB + 8, gy, pitch + 16, 128), F32),
+                    VMEM(((XB + 8) * pitch, 15 * 128), BF16),
+                    VMEM((XB + 6, gy, pitch, 128), F32),
+                ),
+            )
             if kind != "last":
-                state, block = tuple(res[:2]), res[2]
+                state, block, ends = tuple(res[:2]), res[2], res[3:]
         back = lax.all_to_all(
             res[0].reshape(members, 2, 2, ZB, 128), ("gs", "gy"), 0, 0, tiled=True
         )

time: 197 us -> 191 us (0.970)
  starting transfers between devices: 108 us -> 95.3 us
  waiting for transfers between devices: 54.6 us -> 57.1 us
  Pallas kernels: 17.7 us -> 20.1 us
  blocking collectives: 10.4 us -> 12.6 us
    ppermute x16 -> x12, starting transfers between devices: 54.8 us -> 42.5 us  [the longest x4 20.7 us: along_x(): xh = lax.ppermute(block, 'gX', x_shift(-1))]
    ppermute x16 -> x12, waiting for transfers between devices: 24.5 us -> 27 us  [the longest x4 11.8 us: along_x(): xl = lax.ppermute(block, 'gX', x_shift(1))]
    pallas_call x7 -> x8, Pallas kernels: 17.7 us -> 20.1 us  [kernel_call(): pl.pallas_call(body, out_shape=outs if hbm_out else [VMEM(o.shape, o.dtyp...]
    all_to_all x1, blocking collectives: 10.4 us -> 12.6 us  [body(): lax.all_to_all(res[0].reshape(members, 2, 2, ZB, 128), ('gs', 'gy'), 0, 0...]
  transfers between devices with their start and end apart: 19 -> 15, of which waited for: 14 -> 13; matrix products, arithmetic and copies ran while one was open for 0% -> 0% of each run, Pallas kernels for 2% -> 2%
where the time goes in v2:
time: 191 us; the launch traced here: 190 us
  starting transfers between devices  95.3 us (50%)
  waiting for transfers between devices  57.1 us (30%)
  Pallas kernels  20.1 us (11%)
  blocking collectives  12.6 us (7%)
  local copies, waits for them, and re-layouts  3.91 us (2%)
    all_to_all x1, starting transfers between devices, body(): lax.all_to_all(jnp.broadcast_to(own, (gX, *own.shape)), 'gX', 0, 0, tiled...  44.6 us
    all_to_all x1, waiting for transfers between devices, body(): lax.all_to_all(jnp.broadcast_to(own, (gX, *own.shape)), 'gX', 0, 0, tiled...  21.1 us
    ppermute x4, starting transfers between devices, along_x(): xh = lax.ppermute(block, 'gX', x_shift(-1))  20.7 us
    pallas_call x8, Pallas kernels, kernel_call(): pl.pallas_call(body, out_shape=outs if hbm_out else [VMEM(o.shape, o.dtyp...  20.1 us
    all_to_all x1, blocking collectives, body(): lax.all_to_all(res[0].reshape(members, 2, 2, ZB, 128), ('gs', 'gy'), 0, 0...  12.6 us
    ppermute x4, waiting for transfers between devices, along_x(): xl = lax.ppermute(block, 'gX', x_shift(1))  11.8 us
    ppermute x4, starting transfers between devices, along_x(): xl = lax.ppermute(block, 'gX', x_shift(1))  10.4 us
    all_to_all x1, waiting for transfers between devices, body(): held = lax.all_to_all(spread, ('gs', 'gy'), 0, 0, tiled=True)  9.04 us
  transfers between devices with their start and end apart: 15, of which 13 were waited for; matrix products, arithmetic and copies ran while one was open for 0% of the time, Pallas kernels for 2%

profile of v2, /device:TPU:40, one launch (start us, length us, event | category | flops | bytes accessed | tf_op | source)
XLA Modules:
  0.0 190.1 jit_solution(16745898171223514187)
XLA Ops:
  0.6 0.7 copy.14
  1.3 0.1 reshape.29
  1.4 0.7 copy.13
  2.2 0.1 reshape.31
  2.2 0.1 fusion.2
  2.3 0.7 broadcast_in_dim.9
  3.0 44.6 %all-to-all-start.1 = ((bf16[16,2,896]{2,1,0:T(2,128)(2,1)}), bf16[16,2,896]{2,1,0:T(2,128)(2,1)S(1)}, u32[]{:S(2)}, u32[]{:S(2)}) async-start(bf16[16,2,896]{2,1,0:T(2,128)(2,1)} %broadcast_in_dim.9), calls=%async_computation.1 | async-start | bytes 114688 | tf_op jit(solution)/shard_map/all_to_all | solution.py:284
  47.6 2.5 %shard_map.77 = f32[8,5,2,16,128]{4,3,2,1,0:T(8,128)} custom-call(f32[64,2,2,128]{3,2,1,0:T(2,128)} %q_ref.1, f32[64,2,2,128]{3,2,1,0:T(2,128)} %p_ref.1, bf16[3,64,2,2,128]{4,3,2,1,0:T(2,128)(2,1)} %n_ref.1), custom_call_target="tpu_custom_call" | custom-call | tf_op jit(solution)/shard_map/pallas_call | solution.py:32
  50.1 21.1 %all-to-all-done.1 = bf16[16,2,896]{2,1,0:T(2,128)(2,1)S(1)} async-done(((bf16[16,2,896]{2,1,0:T(2,128)(2,1)}), bf16[16,2,896]{2,1,0:T(2,128)(2,1)S(1)}, u32[]{:S(2)}, u32[]{:S(2)}) %all-to-all-start.1) | async-done | bytes 57376 | tf_op jit(solution)/shard_map/all_to_all | solution.py:284
  71.2 4.6 %all-to-all-start = ((f32[8,5,2,16,128]{4,3,2,1,0:T(8,128)}), f32[8,5,2,16,128]{4,3,2,1,0:T(8,128)S(1)}, u32[]{:S(2)}, u32[]{:S(2)}) async-start(f32[8,5,2,16,128]{4,3,2,1,0:T(8,128)} %shard_map.77), calls=%async_computation | async-start | bytes 1310720 | tf_op jit(solution)/shard_map/all_to_all | solution.py:307
  75.8 9.0 %all-to-all-done.r_ref.refs_0_ = f32[8,5,2,16,128]{4,3,2,1,0:T(8,128)S(1)} async-done(((f32[8,5,2,16,128]{4,3,2,1,0:T(8,128)}), f32[8,5,2,16,128]{4,3,2,1,0:T(8,128)S(1)}, u32[]{:S(2)}, u32[]{:S(2)}) %all-to-all-start) | async-done | bytes 655392 | tf_op jit(solution)/shard_map/all_to_all | solution.py:307
  84.9 0.8 broadcast_in_dim.10
  85.7 3.7 %all-to-all-start.2 = ((bf16[8,32,896]{2,1,0:T(8,128)(2,1)}), bf16[8,32,896]{2,1,0:T(8,128)(2,1)S(1)}, u32[]{:S(2)}, u32[]{:S(2)}) async-start(bf16[8,32,896]{2,1,0:T(8,128)(2,1)} %broadcast_in_dim.10), calls=%async_computation.2 | async-start | bytes 917504 | tf_op jit(solution)/shard_map/all_to_all | solution.py:288
  89.4 0.1 shard_map.78
  89.4 4.4 %collective-permute-start = (bf16[4,4,16,128]{3,2,1,0:T(8,128)(2,1)S(1)}, bf16[4,4,16,128]{3,2,1,0:T(8,128)(2,1)S(1)}, u32[]{:S(2)}, u32[]{:S(2)}) collective-permute-start(bf16[4,4,16,128]{3,2,1,0:T(8,128)(2,1)S(1)} %get-tuple-element.16), channel_id=1, source_target_pairs={{0,16},{16,32},{32,48},{48,64},{64,80},{80,96},{96,112},{112,128},... | collective-permute-start | bytes 196616 | tf_op jit(solution)/shard_map/ppermute | solution.py:263
  93.8 3.6 %collective-permute-start.1 = (bf16[4,4,16,128]{3,2,1,0:T(8,128)(2,1)S(1)}, bf16[4,4,16,128]{3,2,1,0:T(8,128)(2,1)S(1)}, u32[]{:S(2)}, u32[]{:S(2)}) collective-permute-start(bf16[4,4,16,128]{3,2,1,0:T(8,128)(2,1)S(1)} %get-tuple-element.16), channel_id=1, source_target_pairs={{0,240},{16,0},{32,16},{48,32},{64,48},{80,64},{96,80},{112,96},{1... | collective-permute-start | bytes 196616 | tf_op jit(solution)/shard_map/ppermute | solution.py:264
  97.4 0.7 collective-permute-done.refs_1_
  98.2 2.7 %collective-permute-done.1.refs_2_ = bf16[4,4,16,128]{3,2,1,0:T(8,128)(2,1)S(1)} collective-permute-done((bf16[4,4,16,128]{3,2,1,0:T(8,128)(2,1)S(1)}, bf16[4,4,16,128]{3,2,1,0:T(8,128)(2,1)S(1)}, u32[]{:S(2)}, u32[]{:S(2)}) %collective-permute-start.1) | collective-permute-done | bytes 65568 | tf_op jit(solution)/shard_map/ppermute | solution.py:264
  101.0 3.7 %collective-permute-start.2 = (bf16[16,4,8,128]{3,2,1,0:T(8,128)(2,1)S(1)}, bf16[16,4,8,128]{3,2,1,0:T(8,128)(2,1)S(1)}, u32[]{:S(2)}, u32[]{:S(2)}) collective-permute-start(bf16[16,4,8,128]{3,2,1,0:T(8,128)(2,1)S(1)} %pad_maximum_fusion), channel_id=1, source_target_pairs={{0,2},{2,4},{4,6},{6,14},{14,12},{12,10},{10,8},{8,1},{1,3},{3,5},... | collective-permute-start | bytes 393224 | tf_op jit(solution)/shard_map/ppermute | solution.py:272
  104.7 2.0 %collective-permute-start.3 = (bf16[16,4,8,128]{3,2,1,0:T(8,128)(2,1)S(1)}, bf16[16,4,8,128]{3,2,1,0:T(8,128)(2,1)S(1)}, u32[]{:S(2)}, u32[]{:S(2)}) collective-permute-start(bf16[16,4,8,128]{3,2,1,0:T(8,128)(2,1)S(1)} %pad_maximum_fusion.1), channel_id=1, source_target_pairs={{0,9},{2,0},{4,2},{6,4},{14,6},{12,14},{10,12},{8,10},{1,8},{3,1},... | collective-permute-start | bytes 393224 | tf_op jit(solution)/shard_map/ppermute | solution.py:273
  106.7 0.1 maximum_bitcast_fusion.refs_6_.refs_7_.refs_8_
  106.7 0.2 reshape.33
  106.9 0.3 copy.10
  107.2 0.2 reshape.34.m_ref
  107.4 1.4 shard_map.79.refs_5_.refs_6_.refs_7_
  108.9 2.7 %collective-permute-done.3.refs_4_ = bf16[16,4,8,128]{3,2,1,0:T(8,128)(2,1)S(1)} collective-permute-done((bf16[16,4,8,128]{3,2,1,0:T(8,128)(2,1)S(1)}, bf16[16,4,8,128]{3,2,1,0:T(8,128)(2,1)S(1)}, u32[]{:S(2)}, u32[]{:S(2)}) %collective-permute-start.3) | collective-permute-done | bytes 131104 | tf_op jit(solution)/shard_map/ppermute | solution.py:273
  111.6 4.3 %shard_map.80 = (f32[4,4,16,128]{3,2,1,0:T(8,128)S(1)}, f32[4,4,16,128]{3,2,1,0:T(8,128)S(1)}, bf16[4,4,24,128]{3,2,1,0:T(8,128)(2,1)S(1)}) custom-call(f32[8,5,2,16,128]{4,3,2,1,0:T(8,128)S(1)} %all-to-all-done.r_ref.refs_0_, bf16[4,4,16,128]{3,2,1,0:T(8,128)(2,1)S(1)} %collective-permute-done.refs_1_, ...), custom_call_target="tpu_custom_call" | custom-call | tf_op jit(solution)/shard_map/pallas_call | solution.py:32
  115.9 4.8 %collective-permute-start.5 = (bf16[4,4,24,128]{3,2,1,0:T(8,128)(2,1)S(1)}, bf16[4,4,24,128]{3,2,1,0:T(8,128)(2,1)S(1)}, u32[]{:S(2)}, u32[]{:S(2)}) collective-permute-start(bf16[4,4,24,128]{3,2,1,0:T(8,128)(2,1)S(1)} %get-tuple-element.21.refs_5_), channel_id=1, source_target_pairs={{0,240},{16,0},{32,16},{48,32},{64,48},{80,64},{96,80},{112,96},{1... | collective-permute-start | bytes 294920 | tf_op jit(solution)/shard_map/ppermute | solution.py:264
  120.7 2.0 %collective-permute-start.4 = (bf16[4,4,24,128]{3,2,1,0:T(8,128)(2,1)S(1)}, bf16[4,4,24,128]{3,2,1,0:T(8,128)(2,1)S(1)}, u32[]{:S(2)}, u32[]{:S(2)}) collective-permute-start(bf16[4,4,24,128]{3,2,1,0:T(8,128)(2,1)S(1)} %get-tuple-element.21.refs_5_), channel_id=1, source_target_pairs={{0,16},{16,32},{32,48},{48,64},{64,80},{80,96},{96,112},{112,128},... | collective-permute-start | bytes 294920 | tf_op jit(solution)/shard_map/ppermute | solution.py:263
  122.7 2.7 %collective-permute-done.5.refs_4_ = bf16[4,4,24,128]{3,2,1,0:T(8,128)(2,1)S(1)} collective-permute-done((bf16[4,4,24,128]{3,2,1,0:T(8,128)(2,1)S(1)}, bf16[4,4,24,128]{3,2,1,0:T(8,128)(2,1)S(1)}, u32[]{:S(2)}, u32[]{:S(2)}) %collective-permute-start.5) | collective-permute-done | bytes 98336 | tf_op jit(solution)/shard_map/ppermute | solution.py:264
  125.4 4.2 %collective-permute-done.4.refs_3_ = bf16[4,4,24,128]{3,2,1,0:T(8,128)(2,1)S(1)} collective-permute-done((bf16[4,4,24,128]{3,2,1,0:T(8,128)(2,1)S(1)}, bf16[4,4,24,128]{3,2,1,0:T(8,128)(2,1)S(1)}, u32[]{:S(2)}, u32[]{:S(2)}) %collective-permute-start.4) | collective-permute-done | bytes 98336 | tf_op jit(solution)/shard_map/ppermute | solution.py:263
  129.7 3.3 %shard_map.81 = (f32[4,4,16,128]{3,2,1,0:T(8,128)S(1)}, f32[4,4,16,128]{3,2,1,0:T(8,128)S(1)}, bf16[4,4,16,128]{3,2,1,0:T(8,128)(2,1)S(1)}, bf16[4,4,8,128]{3,2,1,0:T(8,128)(2,1)S(1)}, bf16[4,4,8,128]{3,2,1,0:T(8,128)(2,1)S(1)}) custom-call(f32[8,5,2,16,128]{4,3,2,1,0:T(8,128)S(1)} %all-to-all-done.r_ref.refs_0_, ...), custom_call_target="tpu_custom_call" | custom-call | tf_op jit(solution)/shard_map/pallas_call | solution.py:32
  132.9 2.1 %collective-permute-start.6 = (bf16[4,4,16,128]{3,2,1,0:T(8,128)(2,1)S(1)}, bf16[4,4,16,128]{3,2,1,0:T(8,128)(2,1)S(1)}, u32[]{:S(2)}, u32[]{:S(2)}) collective-permute-start(bf16[4,4,16,128]{3,2,1,0:T(8,128)(2,1)S(1)} %get-tuple-element.24), channel_id=1, source_target_pairs={{0,16},{16,32},{32,48},{48,64},{64,80},{80,96},{96,112},{112,128},... | collective-permute-start | bytes 196616 | tf_op jit(solution)/shard_map/ppermute | solution.py:263
  135.1 5.9 %collective-permute-start.7 = (bf16[4,4,16,128]{3,2,1,0:T(8,128)(2,1)S(1)}, bf16[4,4,16,128]{3,2,1,0:T(8,128)(2,1)S(1)}, u32[]{:S(2)}, u32[]{:S(2)}) collective-permute-start(bf16[4,4,16,128]{3,2,1,0:T(8,128)(2,1)S(1)} %get-tuple-element.24), channel_id=1, source_target_pairs={{0,240},{16,0},{32,16},{48,32},{64,48},{80,64},{96,80},{112,96},{1... | collective-permute-start | bytes 196616 | tf_op jit(solution)/shard_map/ppermute | solution.py:264
  141.0 0.8 collective-permute-done.6.refs_3_
  141.8 1.7 collective-permute-done.7.refs_4_
  143.6 2.6 %collective-permute-start.8 = (bf16[16,4,8,128]{3,2,1,0:T(8,128)(2,1)S(1)}, bf16[16,4,8,128]{3,2,1,0:T(8,128)(2,1)S(1)}, u32[]{:S(2)}, u32[]{:S(2)}) collective-permute-start(bf16[16,4,8,128]{3,2,1,0:T(8,128)(2,1)S(1)} %pad_maximum_fusion.2), channel_id=1, source_target_pairs={{0,2},{2,4},{4,6},{6,14},{14,12},{12,10},{10,8},{8,1},{1,3},{3,5},... | collective-permute-start | bytes 393224 | tf_op jit(solution)/shard_map/ppermute | solution.py:272
  146.2 3.0 %collective-permute-start.9 = (bf16[16,4,8,128]{3,2,1,0:T(8,128)(2,1)S(1)}, bf16[16,4,8,128]{3,2,1,0:T(8,128)(2,1)S(1)}, u32[]{:S(2)}, u32[]{:S(2)}) collective-permute-start(bf16[16,4,8,128]{3,2,1,0:T(8,128)(2,1)S(1)} %pad_maximum_fusion.3), channel_id=1, source_target_pairs={{0,9},{2,0},{4,2},{6,4},{14,6},{12,14},{10,12},{8,10},{1,8},{3,1},... | collective-permute-start | bytes 393224 | tf_op jit(solution)/shard_map/ppermute | solution.py:273
  149.2 1.7 collective-permute-done.8.refs_5_
  151.0 2.2 %collective-permute-done.9.refs_6_ = bf16[16,4,8,128]{3,2,1,0:T(8,128)(2,1)S(1)} collective-permute-done((bf16[16,4,8,128]{3,2,1,0:T(8,128)(2,1)S(1)}, bf16[16,4,8,128]{3,2,1,0:T(8,128)(2,1)S(1)}, u32[]{:S(2)}, u32[]{:S(2)}) %collective-permute-start.9) | collective-permute-done | bytes 131104 | tf_op jit(solution)/shard_map/ppermute | solution.py:273
  153.1 4.3 %shard_map.82 = (f32[4,4,16,128]{3,2,1,0:T(8,128)S(1)}, f32[4,4,16,128]{3,2,1,0:T(8,128)S(1)}, bf16[4,4,24,128]{3,2,1,0:T(8,128)(2,1)S(1)}) custom-call(f32[8,5,2,16,128]{4,3,2,1,0:T(8,128)S(1)} %all-to-all-done.r_ref.refs_0_, f32[4,4,16,128]{3,2,1,0:T(8,128)S(1)} %get-tuple-element.22.refs_1_, f32[4,4,16,128]{3,2,1,0:T(8,128)S(1)} %get-tuple-element.23.refs_2_, ...), custom_call_target="tpu_custom_call" | custom-call | tf_op jit(solution)/shard_map/pallas_call | solution.py:32
  157.4 6.4 %collective-permute-start.11 = (bf16[4,4,24,128]{3,2,1,0:T(8,128)(2,1)S(1)}, bf16[4,4,24,128]{3,2,1,0:T(8,128)(2,1)S(1)}, u32[]{:S(2)}, u32[]{:S(2)}) collective-permute-start(bf16[4,4,24,128]{3,2,1,0:T(8,128)(2,1)S(1)} %get-tuple-element.29.refs_5_), channel_id=1, source_target_pairs={{0,240},{16,0},{32,16},{48,32},{64,48},{80,64},{96,80},{112,96},{1... | collective-permute-start | bytes 294920 | tf_op jit(solution)/shard_map/ppermute | solution.py:264
  163.9 2.0 %collective-permute-start.10 = (bf16[4,4,24,128]{3,2,1,0:T(8,128)(2,1)S(1)}, bf16[4,4,24,128]{3,2,1,0:T(8,128)(2,1)S(1)}, u32[]{:S(2)}, u32[]{:S(2)}) collective-permute-start(bf16[4,4,24,128]{3,2,1,0:T(8,128)(2,1)S(1)} %get-tuple-element.29.refs_5_), channel_id=1, source_target_pairs={{0,16},{16,32},{32,48},{48,64},{64,80},{80,96},{96,112},{112,128},... | collective-permute-start | bytes 294920 | tf_op jit(solution)/shard_map/ppermute | solution.py:263
  165.8 1.5 collective-permute-done.11.refs_4_
  167.3 6.1 %collective-permute-done.10.refs_3_ = bf16[4,4,24,128]{3,2,1,0:T(8,128)(2,1)S(1)} collective-permute-done((bf16[4,4,24,128]{3,2,1,0:T(8,128)(2,1)S(1)}, bf16[4,4,24,128]{3,2,1,0:T(8,128)(2,1)S(1)}, u32[]{:S(2)}, u32[]{:S(2)}) %collective-permute-start.10) | collective-permute-done | bytes 98336 | tf_op jit(solution)/shard_map/ppermute | solution.py:263
  173.4 3.3 %shard_map.83 = f32[2,4,2,2,16,128]{5,4,3,2,1,0:T(8,128)S(1)} custom-call(f32[8,5,2,16,128]{4,3,2,1,0:T(8,128)S(1)} %all-to-all-done.r_ref.refs_0_, f32[4,4,16,128]{3,2,1,0:T(8,128)S(1)} %get-tuple-element.27.refs_1_, f32[4,4,16,128]{3,2,1,0:T(8,128)S(1)} %get-tuple-element.28.refs_2_, bf16[4,4,24,128]{3,2,1,0:T(8,128)(2,1)S(1)} %collective-permute-done.10.refs_3_, ...), custom_call_target="tpu_custom_call" | custom-call | tf_op jit(solution)/shard_map/pallas_call | solution.py:32
  176.6 12.6 %all_to_all.20.in_ref = f32[8,2,2,16,128]{4,3,2,1,0:T(8,128)S(1)} all-to-all(f32[8,2,2,16,128]{4,3,2,1,0:T(8,128)S(1)} %bitcast.12), channel_id=1, replica_groups=mesh['grp'=2,'gX'=16,'gs'=2,'gy'=4,'gz'=2] {'gs','gy'}, dimensions={0} | all-to-all | bytes 524288 | tf_op jit(solution)/shard_map/all_to_all | solution.py:339
  189.2 0.9 shard_map.84
  (17 shorter events, 0.2 us)
Async XLA Ops:
  3.0 68.2 %all-to-all-start.1 = ((bf16[16,2,896]{2,1,0:T(2,128)(2,1)}), bf16[16,2,896]{2,1,0:T(2,128)(2,1)S(1)}, u32[]{:S(2)}, u32[]{:S(2)}) async-start(bf16[16,2,896]{2,1,0:T(2,128)(2,1)} %broadcast_in_dim.9), calls=%async_computation.1 | async-start | bytes 114688 | tf_op jit(solution)/shard_map/all_to_all | solution.py:284
  50.1 56.6 %copy-start = (f32[64]{0:T(128)S(1)}, f32[64]{0:T(128)}, u32[]{:S(2)}) copy-start(f32[64]{0:T(128)} %param.11) | copy-start | bytes 772
  71.2 13.7 %all-to-all-start = ((f32[8,5,2,16,128]{4,3,2,1,0:T(8,128)}), f32[8,5,2,16,128]{4,3,2,1,0:T(8,128)S(1)}, u32[]{:S(2)}, u32[]{:S(2)}) async-start(f32[8,5,2,16,128]{4,3,2,1,0:T(8,128)} %shard_map.77), calls=%async_computation | async-start | bytes 1310720 | tf_op jit(solution)/shard_map/all_to_all | solution.py:307
  85.7 21.1 %all-to-all-start.2 = ((bf16[8,32,896]{2,1,0:T(8,128)(2,1)}), bf16[8,32,896]{2,1,0:T(8,128)(2,1)S(1)}, u32[]{:S(2)}, u32[]{:S(2)}) async-start(bf16[8,32,896]{2,1,0:T(8,128)(2,1)} %broadcast_in_dim.10), calls=%async_computation.2 | async-start | bytes 917504 | tf_op jit(solution)/shard_map/all_to_all | solution.py:288
  89.4 8.8 %collective-permute-start = (bf16[4,4,16,128]{3,2,1,0:T(8,128)(2,1)S(1)}, bf16[4,4,16,128]{3,2,1,0:T(8,128)(2,1)S(1)}, u32[]{:S(2)}, u32[]{:S(2)}) collective-permute-start(bf16[4,4,16,128]{3,2,1,0:T(8,128)(2,1)S(1)} %get-tuple-element.16), channel_id=1, source_target_pairs={{0,16},{16,32},{32,48},{48,64},{64,80},{80,96},{96,112},{112,128},... | collective-permute-start | bytes 196616 | tf_op jit(solution)/shard_map/ppermute | solution.py:263
  93.8 7.1 %collective-permute-start.1 = (bf16[4,4,16,128]{3,2,1,0:T(8,128)(2,1)S(1)}, bf16[4,4,16,128]{3,2,1,0:T(8,128)(2,1)S(1)}, u32[]{:S(2)}, u32[]{:S(2)}) collective-permute-start(bf16[4,4,16,128]{3,2,1,0:T(8,128)(2,1)S(1)} %get-tuple-element.16), channel_id=1, source_target_pairs={{0,240},{16,0},{32,16},{48,32},{64,48},{80,64},{96,80},{112,96},{1... | collective-permute-start | bytes 196616 | tf_op jit(solution)/shard_map/ppermute | solution.py:264
  101.0 7.9 %collective-permute-start.2 = (bf16[16,4,8,128]{3,2,1,0:T(8,128)(2,1)S(1)}, bf16[16,4,8,128]{3,2,1,0:T(8,128)(2,1)S(1)}, u32[]{:S(2)}, u32[]{:S(2)}) collective-permute-start(bf16[16,4,8,128]{3,2,1,0:T(8,128)(2,1)S(1)} %pad_maximum_fusion), channel_id=1, source_target_pairs={{0,2},{2,4},{4,6},{6,14},{14,12},{12,10},{10,8},{8,1},{1,3},{3,5},... | collective-permute-start | bytes 393224 | tf_op jit(solution)/shard_map/ppermute | solution.py:272
  104.7 6.9 %collective-permute-start.3 = (bf16[16,4,8,128]{3,2,1,0:T(8,128)(2,1)S(1)}, bf16[16,4,8,128]{3,2,1,0:T(8,128)(2,1)S(1)}, u32[]{:S(2)}, u32[]{:S(2)}) collective-permute-start(bf16[16,4,8,128]{3,2,1,0:T(8,128)(2,1)S(1)} %pad_maximum_fusion.1), channel_id=1, source_target_pairs={{0,9},{2,0},{4,2},{6,4},{14,6},{12,14},{10,12},{8,10},{1,8},{3,1},... | collective-permute-start | bytes 393224 | tf_op jit(solution)/shard_map/ppermute | solution.py:273
  115.9 9.5 %collective-permute-start.5 = (bf16[4,4,24,128]{3,2,1,0:T(8,128)(2,1)S(1)}, bf16[4,4,24,128]{3,2,1,0:T(8,128)(2,1)S(1)}, u32[]{:S(2)}, u32[]{:S(2)}) collective-permute-start(bf16[4,4,24,128]{3,2,1,0:T(8,128)(2,1)S(1)} %get-tuple-element.21.refs_5_), channel_id=1, source_target_pairs={{0,240},{16,0},{32,16},{48,32},{64,48},{80,64},{96,80},{112,96},{1... | collective-permute-start | bytes 294920 | tf_op jit(solution)/shard_map/ppermute | solution.py:264
  120.7 8.9 %collective-permute-start.4 = (bf16[4,4,24,128]{3,2,1,0:T(8,128)(2,1)S(1)}, bf16[4,4,24,128]{3,2,1,0:T(8,128)(2,1)S(1)}, u32[]{:S(2)}, u32[]{:S(2)}) collective-permute-start(bf16[4,4,24,128]{3,2,1,0:T(8,128)(2,1)S(1)} %get-tuple-element.21.refs_5_), channel_id=1, source_target_pairs={{0,16},{16,32},{32,48},{48,64},{64,80},{80,96},{96,112},{112,128},... | collective-permute-start | bytes 294920 | tf_op jit(solution)/shard_map/ppermute | solution.py:263
  132.9 8.8 %collective-permute-start.6 = (bf16[4,4,16,128]{3,2,1,0:T(8,128)(2,1)S(1)}, bf16[4,4,16,128]{3,2,1,0:T(8,128)(2,1)S(1)}, u32[]{:S(2)}, u32[]{:S(2)}) collective-permute-start(bf16[4,4,16,128]{3,2,1,0:T(8,128)(2,1)S(1)} %get-tuple-element.24), channel_id=1, source_target_pairs={{0,16},{16,32},{32,48},{48,64},{64,80},{80,96},{96,112},{112,128},... | collective-permute-start | bytes 196616 | tf_op jit(solution)/shard_map/ppermute | solution.py:263
  135.1 8.4 %collective-permute-start.7 = (bf16[4,4,16,128]{3,2,1,0:T(8,128)(2,1)S(1)}, bf16[4,4,16,128]{3,2,1,0:T(8,128)(2,1)S(1)}, u32[]{:S(2)}, u32[]{:S(2)}) collective-permute-start(bf16[4,4,16,128]{3,2,1,0:T(8,128)(2,1)S(1)} %get-tuple-element.24), channel_id=1, source_target_pairs={{0,240},{16,0},{32,16},{48,32},{64,48},{80,64},{96,80},{112,96},{1... | collective-permute-start | bytes 196616 | tf_op jit(solution)/shard_map/ppermute | solution.py:264
  143.6 7.4 %collective-permute-start.8 = (bf16[16,4,8,128]{3,2,1,0:T(8,128)(2,1)S(1)}, bf16[16,4,8,128]{3,2,1,0:T(8,128)(2,1)S(1)}, u32[]{:S(2)}, u32[]{:S(2)}) collective-permute-start(bf16[16,4,8,128]{3,2,1,0:T(8,128)(2,1)S(1)} %pad_maximum_fusion.2), channel_id=1, source_target_pairs={{0,2},{2,4},{4,6},{6,14},{14,12},{12,10},{10,8},{8,1},{1,3},{3,5},... | collective-permute-start | bytes 393224 | tf_op jit(solution)/shard_map/ppermute | solution.py:272
  146.2 6.9 %collective-permute-start.9 = (bf16[16,4,8,128]{3,2,1,0:T(8,128)(2,1)S(1)}, bf16[16,4,8,128]{3,2,1,0:T(8,128)(2,1)S(1)}, u32[]{:S(2)}, u32[]{:S(2)}) collective-permute-start(bf16[16,4,8,128]{3,2,1,0:T(8,128)(2,1)S(1)} %pad_maximum_fusion.3), channel_id=1, source_target_pairs={{0,9},{2,0},{4,2},{6,4},{14,6},{12,14},{10,12},{8,10},{1,8},{3,1},... | collective-permute-start | bytes 393224 | tf_op jit(solution)/shard_map/ppermute | solution.py:273
  157.4 9.8 %collective-permute-start.11 = (bf16[4,4,24,128]{3,2,1,0:T(8,128)(2,1)S(1)}, bf16[4,4,24,128]{3,2,1,0:T(8,128)(2,1)S(1)}, u32[]{:S(2)}, u32[]{:S(2)}) collective-permute-start(bf16[4,4,24,128]{3,2,1,0:T(8,128)(2,1)S(1)} %get-tuple-element.29.refs_5_), channel_id=1, source_target_pairs={{0,240},{16,0},{32,16},{48,32},{64,48},{80,64},{96,80},{112,96},{1... | collective-permute-start | bytes 294920 | tf_op jit(solution)/shard_map/ppermute | solution.py:264
  163.9 9.5 %collective-permute-start.10 = (bf16[4,4,24,128]{3,2,1,0:T(8,128)(2,1)S(1)}, bf16[4,4,24,128]{3,2,1,0:T(8,128)(2,1)S(1)}, u32[]{:S(2)}, u32[]{:S(2)}) collective-permute-start(bf16[4,4,24,128]{3,2,1,0:T(8,128)(2,1)S(1)} %get-tuple-element.29.refs_5_), channel_id=1, source_target_pairs={{0,16},{16,32},{32,48},{48,64},{64,80},{80,96},{96,112},{112,128},... | collective-permute-start | bytes 294920 | tf_op jit(solution)/shard_map/ppermute | solution.py:263

commit v3 on v2

--- a/solution.py
+++ b/solution.py
@@ -40,16 +40,26 @@
 
 
 def spread_body(place, q_ref, p_ref, n_ref, out_ref):
-    for k in range(2 + n_ref.shape[0]):
-        for x in range(q_ref.shape[1]):
-            if k < 2:
-                ref = (q_ref, p_ref)[k]
-                parts = [ref[:, x, y, :] for y in range(ref.shape[2])]
-            else:
-                parts = [n_ref[k - 2, :, x, y, :].astype(F32) for y in range(n_ref.shape[3])]
-            flat = jnp.concatenate(parts, axis=0).T
-            for member, block in enumerate(place):
-                out_ref[member, k, x] = flat[block * ZB : (block + 1) * ZB, :]
+    def send(part, x, flat):
+        for member, block in enumerate(place):
+            out_ref[member, part, x] = flat[block * ZB : (block + 1) * ZB, :]
+
+    for x in range(q_ref.shape[1]):
+        for k, ref in enumerate((q_ref, p_ref)):
+            flat = jnp.concatenate([ref[:, x, y, :] for y in range(ref.shape[2])], axis=0).T
+            high = flat.astype(BF16)
+            send(2 * k, x, high)
+            send(2 * k + 1, x, (flat - high.astype(F32)).astype(BF16))
+        for k in range(n_ref.shape[0]):
+            parts = [n_ref[k, :, x, y, :].astype(F32) for y in range(n_ref.shape[3])]
+            send(4 + k, x, jnp.concatenate(parts, axis=0).T.astype(BF16))
+
+
+def held_at(r_ref, array, x, j):
+    pick = lambda part: r_ref[x // 2 * 4 + j, part, x % 2].astype(F32)
+    if array < 2:
+        return pick(2 * array) + pick(2 * array + 1)
+    return pick(2 + array)
 
 
 def collect_body(place, in_ref, q_ref, p_ref):
@@ -122,8 +132,8 @@
 def prepare_body(coef, r_ref, block_ref, rl_ref, rh_ref):
     for x in range(XB):
         for j in range(4):
-            q, p, n = (r_ref[x // 2 * 4 + j, k, x % 2] for k in range(3))
-            block_ref[x, j] = q.astype(BF16)
+            q, p, n = (held_at(r_ref, k, x, j) for k in range(3))
+            block_ref[x, j] = r_ref[x // 2 * 4 + j, 0, x % 2]
             rl_ref[x, j], rh_ref[x, j] = strips(ahead(coef, 1, q, p, n)[0])
 
 
@@ -132,14 +142,14 @@
     it = iter(refs)
     r_ref = next(it)
     if kind == "first":
-        q_of = lambda x, j: r_ref[x // 2 * 4 + j, 0, x % 2]
-        p_of = lambda x, j: r_ref[x // 2 * 4 + j, 1, x % 2]
+        q_of = lambda x, j: held_at(r_ref, 0, x, j)
+        p_of = lambda x, j: held_at(r_ref, 1, x, j)
     else:
         q_ref, p_ref = next(it), next(it)
         q_of = lambda x, j: q_ref[x, j]
         p_of = lambda x, j: p_ref[x, j]
     step_at = {"first": 0}.get(kind, kind)
-    noise_of = lambda x, j, k: r_ref[x // 2 * 4 + j, 2 + k, x % 2]
+    noise_of = lambda x, j, k: held_at(r_ref, 2 + k, x, j)
     if wide:
         xl_ref, xh_ref, zl_ref, zh_ref, w_ref, bias_ref = (next(it) for _ in range(6))
     else:
@@ -183,10 +193,14 @@
         x_out = x_in - 2
         m = x_out * pitch
         for p in range(4):
+            cols = slice(384 * p, 384 * p + 768)
             t = jnp.dot(
-                rows_ref[0:n, 384 * p : 384 * p + 768], w_ref[w], preferred_element_type=F32
+                rows_ref[0 : n - pitch, cols], w_ref[w, :, 0:256], preferred_element_type=F32
             )
-            o = t[0:m, 0:128] + t[pitch : pitch + m, 128:256] + t[2 * pitch :, 256:384]
+            o = t[0:m, 0:128] + t[pitch:, 128:256]
+            o = o + jnp.dot(
+                rows_ref[2 * pitch : n, cols], w_ref[w, :, 256:384], preferred_element_type=F32
+            )
             use(p, o.reshape(x_out, pitch, 128))
 
     def hidden(p, h):
@@ -299,7 +313,7 @@
 
         (spread,) = kernel_call(
             functools.partial(spread_body, place),
-            [jax.ShapeDtypeStruct((members, 2 + steps, 2, ZB, 128), F32)],
+            [jax.ShapeDtypeStruct((members, 4 + steps, 2, ZB, 128), BF16)],
             (position, momentum, noise),
             hbm_in=True,
             hbm_out=True,

time: 191 us -> 187 us (0.979)
  Pallas kernels: 20.1 us -> 18 us
    pallas_call x8, Pallas kernels: 20.1 us -> 18 us  [kernel_call(): pl.pallas_call(body, out_shape=outs if hbm_out else [VMEM(o.shape, o.dtyp...]
where the time goes in v3:
time: 187 us; the launch traced here: 186 us
  starting transfers between devices  96.1 us (51%)
  waiting for transfers between devices  55.6 us (30%)
  Pallas kernels  18 us (10%)
  blocking collectives  11.3 us (6%)
  local copies, waits for them, and re-layouts  3.92 us (2%)
    all_to_all x1, starting transfers between devices, body(): lax.all_to_all(jnp.broadcast_to(own, (gX, *own.shape)), 'gX', 0, 0, tiled...  44.6 us
    ppermute x4, starting transfers between devices, along_x(): xh = lax.ppermute(block, 'gX', x_shift(-1))  22.1 us
    all_to_all x1, waiting for transfers between devices, body(): lax.all_to_all(jnp.broadcast_to(own, (gX, *own.shape)), 'gX', 0, 0, tiled...  21.2 us
    pallas_call x8, Pallas kernels, kernel_call(): pl.pallas_call(body, out_shape=outs if hbm_out else [VMEM(o.shape, o.dtyp...  18 us
    ppermute x4, waiting for transfers between devices, along_x(): xl = lax.ppermute(block, 'gX', x_shift(1))  11.6 us
    all_to_all x1, blocking collectives, body(): lax.all_to_all(res[0].reshape(members, 2, 2, ZB, 128), ('gs', 'gy'), 0, 0...  11.3 us
    ppermute x4, starting transfers between devices, along_x(): xl = lax.ppermute(block, 'gX', x_shift(1))  9.68 us
    all_to_all x1, waiting for transfers between devices, body(): held = lax.all_to_all(spread, ('gs', 'gy'), 0, 0, tiled=True)  7.99 us
  transfers between devices with their start and end apart: 15, of which 13 were waited for; matrix products, arithmetic and copies ran while one was open for 0% of the time, Pallas kernels for 2%

profile of v3, /device:TPU:40, one launch (start us, length us, event | category | flops | bytes accessed | tf_op | source)
XLA Modules:
  0.0 186.1 jit_solution(7665487974208833748)
XLA Ops:
  0.6 0.7 copy.14
  1.3 0.1 reshape.29
  1.4 0.7 copy.13
  2.2 0.1 reshape.31
  2.2 0.1 fusion.2
  2.3 0.7 broadcast_in_dim.9
  3.0 44.6 %all-to-all-start.1 = ((bf16[16,2,896]{2,1,0:T(2,128)(2,1)}), bf16[16,2,896]{2,1,0:T(2,128)(2,1)S(1)}, u32[]{:S(2)}, u32[]{:S(2)}) async-start(bf16[16,2,896]{2,1,0:T(2,128)(2,1)} %broadcast_in_dim.9), calls=%async_computation.1 | async-start | bytes 114688 | tf_op jit(solution)/shard_map/all_to_all | solution.py:298
  47.6 2.5 %shard_map.77 = bf16[8,7,2,16,128]{4,3,2,1,0:T(8,128)(2,1)} custom-call(f32[64,2,2,128]{3,2,1,0:T(2,128)} %q_ref.1, f32[64,2,2,128]{3,2,1,0:T(2,128)} %p_ref.1, bf16[3,64,2,2,128]{4,3,2,1,0:T(2,128)(2,1)} %n_ref.1), custom_call_target="tpu_custom_call" | custom-call | tf_op jit(solution)/shard_map/pallas_call | solution.py:32
  50.0 21.2 %all-to-all-done.1 = bf16[16,2,896]{2,1,0:T(2,128)(2,1)S(1)} async-done(((bf16[16,2,896]{2,1,0:T(2,128)(2,1)}), bf16[16,2,896]{2,1,0:T(2,128)(2,1)S(1)}, u32[]{:S(2)}, u32[]{:S(2)}) %all-to-all-start.1) | async-done | bytes 57376 | tf_op jit(solution)/shard_map/all_to_all | solution.py:298
  71.2 4.6 %all-to-all-start = ((bf16[8,7,2,16,128]{4,3,2,1,0:T(8,128)(2,1)}), bf16[8,7,2,16,128]{4,3,2,1,0:T(8,128)(2,1)S(1)}, u32[]{:S(2)}, u32[]{:S(2)}) async-start(bf16[8,7,2,16,128]{4,3,2,1,0:T(8,128)(2,1)} %shard_map.77), calls=%async_computation | async-start | bytes 917504 | tf_op jit(solution)/shard_map/all_to_all | solution.py:321
  75.8 8.0 %all-to-all-done.r_ref.refs_0_ = bf16[8,7,2,16,128]{4,3,2,1,0:T(8,128)(2,1)S(1)} async-done(((bf16[8,7,2,16,128]{4,3,2,1,0:T(8,128)(2,1)}), bf16[8,7,2,16,128]{4,3,2,1,0:T(8,128)(2,1)S(1)}, u32[]{:S(2)}, u32[]{:S(2)}) %all-to-all-start) | async-done | bytes 458784 | tf_op jit(solution)/shard_map/all_to_all | solution.py:321
  83.8 0.8 broadcast_in_dim.10
  84.6 3.7 %all-to-all-start.2 = ((bf16[8,32,896]{2,1,0:T(8,128)(2,1)}), bf16[8,32,896]{2,1,0:T(8,128)(2,1)S(1)}, u32[]{:S(2)}, u32[]{:S(2)}) async-start(bf16[8,32,896]{2,1,0:T(8,128)(2,1)} %broadcast_in_dim.10), calls=%async_computation.2 | async-start | bytes 917504 | tf_op jit(solution)/shard_map/all_to_all | solution.py:302
  88.3 0.1 shard_map.78
  88.4 3.8 %collective-permute-start = (bf16[4,4,16,128]{3,2,1,0:T(8,128)(2,1)S(1)}, bf16[4,4,16,128]{3,2,1,0:T(8,128)(2,1)S(1)}, u32[]{:S(2)}, u32[]{:S(2)}) collective-permute-start(bf16[4,4,16,128]{3,2,1,0:T(8,128)(2,1)S(1)} %get-tuple-element.16), channel_id=1, source_target_pairs={{0,16},{16,32},{32,48},{48,64},{64,80},{80,96},{96,112},{112,128},... | collective-permute-start | bytes 196616 | tf_op jit(solution)/shard_map/ppermute | solution.py:277
  92.2 4.2 %collective-permute-start.1 = (bf16[4,4,16,128]{3,2,1,0:T(8,128)(2,1)S(1)}, bf16[4,4,16,128]{3,2,1,0:T(8,128)(2,1)S(1)}, u32[]{:S(2)}, u32[]{:S(2)}) collective-permute-start(bf16[4,4,16,128]{3,2,1,0:T(8,128)(2,1)S(1)} %get-tuple-element.16), channel_id=1, source_target_pairs={{0,240},{16,0},{32,16},{48,32},{64,48},{80,64},{96,80},{112,96},{1... | collective-permute-start | bytes 196616 | tf_op jit(solution)/shard_map/ppermute | solution.py:278
  96.4 0.3 collective-permute-done.refs_1_
  96.8 2.6 %collective-permute-done.1.refs_2_ = bf16[4,4,16,128]{3,2,1,0:T(8,128)(2,1)S(1)} collective-permute-done((bf16[4,4,16,128]{3,2,1,0:T(8,128)(2,1)S(1)}, bf16[4,4,16,128]{3,2,1,0:T(8,128)(2,1)S(1)}, u32[]{:S(2)}, u32[]{:S(2)}) %collective-permute-start.1) | collective-permute-done | bytes 65568 | tf_op jit(solution)/shard_map/ppermute | solution.py:278
  99.4 3.7 %collective-permute-start.2 = (bf16[16,4,8,128]{3,2,1,0:T(8,128)(2,1)S(1)}, bf16[16,4,8,128]{3,2,1,0:T(8,128)(2,1)S(1)}, u32[]{:S(2)}, u32[]{:S(2)}) collective-permute-start(bf16[16,4,8,128]{3,2,1,0:T(8,128)(2,1)S(1)} %pad_maximum_fusion), channel_id=1, source_target_pairs={{0,2},{2,4},{4,6},{6,14},{14,12},{12,10},{10,8},{8,1},{1,3},{3,5},... | collective-permute-start | bytes 393224 | tf_op jit(solution)/shard_map/ppermute | solution.py:286
  103.1 2.0 %collective-permute-start.3 = (bf16[16,4,8,128]{3,2,1,0:T(8,128)(2,1)S(1)}, bf16[16,4,8,128]{3,2,1,0:T(8,128)(2,1)S(1)}, u32[]{:S(2)}, u32[]{:S(2)}) collective-permute-start(bf16[16,4,8,128]{3,2,1,0:T(8,128)(2,1)S(1)} %pad_maximum_fusion.1), channel_id=1, source_target_pairs={{0,9},{2,0},{4,2},{6,4},{14,6},{12,14},{10,12},{8,10},{1,8},{3,1},... | collective-permute-start | bytes 393224 | tf_op jit(solution)/shard_map/ppermute | solution.py:287
  105.1 0.1 maximum_bitcast_fusion.refs_6_.refs_7_.refs_8_
  105.2 0.2 reshape.33
  105.3 0.3 copy.10
  105.7 0.2 reshape.34.m_ref
  105.8 1.4 shard_map.79.refs_5_.refs_6_.refs_7_
  107.3 2.7 %collective-permute-done.3.refs_4_ = bf16[16,4,8,128]{3,2,1,0:T(8,128)(2,1)S(1)} collective-permute-done((bf16[16,4,8,128]{3,2,1,0:T(8,128)(2,1)S(1)}, bf16[16,4,8,128]{3,2,1,0:T(8,128)(2,1)S(1)}, u32[]{:S(2)}, u32[]{:S(2)}) %collective-permute-start.3) | collective-permute-done | bytes 131104 | tf_op jit(solution)/shard_map/ppermute | solution.py:287
  110.0 3.7 %shard_map.80 = (f32[4,4,16,128]{3,2,1,0:T(8,128)S(1)}, f32[4,4,16,128]{3,2,1,0:T(8,128)S(1)}, bf16[4,4,24,128]{3,2,1,0:T(8,128)(2,1)S(1)}) custom-call(bf16[8,7,2,16,128]{4,3,2,1,0:T(8,128)(2,1)S(1)} %all-to-all-done.r_ref.refs_0_, bf16[4,4,16,128]{3,2,1,0:T(8,128)(2,1)S(1)} %collective-permute-done.refs_1_, ...), custom_call_target="tpu_custom_call" | custom-call | tf_op jit(solution)/shard_map/pallas_call | solution.py:32
  113.7 5.4 %collective-permute-start.5 = (bf16[4,4,24,128]{3,2,1,0:T(8,128)(2,1)S(1)}, bf16[4,4,24,128]{3,2,1,0:T(8,128)(2,1)S(1)}, u32[]{:S(2)}, u32[]{:S(2)}) collective-permute-start(bf16[4,4,24,128]{3,2,1,0:T(8,128)(2,1)S(1)} %get-tuple-element.21.refs_5_), channel_id=1, source_target_pairs={{0,240},{16,0},{32,16},{48,32},{64,48},{80,64},{96,80},{112,96},{1... | collective-permute-start | bytes 294920 | tf_op jit(solution)/shard_map/ppermute | solution.py:278
  119.1 2.0 %collective-permute-start.4 = (bf16[4,4,24,128]{3,2,1,0:T(8,128)(2,1)S(1)}, bf16[4,4,24,128]{3,2,1,0:T(8,128)(2,1)S(1)}, u32[]{:S(2)}, u32[]{:S(2)}) collective-permute-start(bf16[4,4,24,128]{3,2,1,0:T(8,128)(2,1)S(1)} %get-tuple-element.21.refs_5_), channel_id=1, source_target_pairs={{0,16},{16,32},{32,48},{48,64},{64,80},{80,96},{96,112},{112,128},... | collective-permute-start | bytes 294920 | tf_op jit(solution)/shard_map/ppermute | solution.py:277
  121.1 2.2 %collective-permute-done.5.refs_4_ = bf16[4,4,24,128]{3,2,1,0:T(8,128)(2,1)S(1)} collective-permute-done((bf16[4,4,24,128]{3,2,1,0:T(8,128)(2,1)S(1)}, bf16[4,4,24,128]{3,2,1,0:T(8,128)(2,1)S(1)}, u32[]{:S(2)}, u32[]{:S(2)}) %collective-permute-start.5) | collective-permute-done | bytes 98336 | tf_op jit(solution)/shard_map/ppermute | solution.py:278
  123.3 5.0 %collective-permute-done.4.refs_3_ = bf16[4,4,24,128]{3,2,1,0:T(8,128)(2,1)S(1)} collective-permute-done((bf16[4,4,24,128]{3,2,1,0:T(8,128)(2,1)S(1)}, bf16[4,4,24,128]{3,2,1,0:T(8,128)(2,1)S(1)}, u32[]{:S(2)}, u32[]{:S(2)}) %collective-permute-start.4) | collective-permute-done | bytes 98336 | tf_op jit(solution)/shard_map/ppermute | solution.py:277
  128.3 2.9 %shard_map.81 = (f32[4,4,16,128]{3,2,1,0:T(8,128)S(1)}, f32[4,4,16,128]{3,2,1,0:T(8,128)S(1)}, bf16[4,4,16,128]{3,2,1,0:T(8,128)(2,1)S(1)}, bf16[4,4,8,128]{3,2,1,0:T(8,128)(2,1)S(1)}, bf16[4,4,8,128]{3,2,1,0:T(8,128)(2,1)S(1)}) custom-call(bf16[8,7,2,16,128]{4,3,2,1,0:T(8,128)(2,1)S(1)} %all-to-all-done.r_ref.refs_0_, ...), custom_call_target="tpu_custom_call" | custom-call | tf_op jit(solution)/shard_map/pallas_call | solution.py:32
  131.2 2.0 %collective-permute-start.6 = (bf16[4,4,16,128]{3,2,1,0:T(8,128)(2,1)S(1)}, bf16[4,4,16,128]{3,2,1,0:T(8,128)(2,1)S(1)}, u32[]{:S(2)}, u32[]{:S(2)}) collective-permute-start(bf16[4,4,16,128]{3,2,1,0:T(8,128)(2,1)S(1)} %get-tuple-element.24), channel_id=1, source_target_pairs={{0,16},{16,32},{32,48},{48,64},{64,80},{80,96},{96,112},{112,128},... | collective-permute-start | bytes 196616 | tf_op jit(solution)/shard_map/ppermute | solution.py:277
  133.1 6.1 %collective-permute-start.7 = (bf16[4,4,16,128]{3,2,1,0:T(8,128)(2,1)S(1)}, bf16[4,4,16,128]{3,2,1,0:T(8,128)(2,1)S(1)}, u32[]{:S(2)}, u32[]{:S(2)}) collective-permute-start(bf16[4,4,16,128]{3,2,1,0:T(8,128)(2,1)S(1)} %get-tuple-element.24), channel_id=1, source_target_pairs={{0,240},{16,0},{32,16},{48,32},{64,48},{80,64},{96,80},{112,96},{1... | collective-permute-start | bytes 196616 | tf_op jit(solution)/shard_map/ppermute | solution.py:278
  139.2 0.7 collective-permute-done.6.refs_3_
  139.9 1.2 collective-permute-done.7.refs_4_
  141.2 3.0 %collective-permute-start.8 = (bf16[16,4,8,128]{3,2,1,0:T(8,128)(2,1)S(1)}, bf16[16,4,8,128]{3,2,1,0:T(8,128)(2,1)S(1)}, u32[]{:S(2)}, u32[]{:S(2)}) collective-permute-start(bf16[16,4,8,128]{3,2,1,0:T(8,128)(2,1)S(1)} %pad_maximum_fusion.2), channel_id=1, source_target_pairs={{0,2},{2,4},{4,6},{6,14},{14,12},{12,10},{10,8},{8,1},{1,3},{3,5},... | collective-permute-start | bytes 393224 | tf_op jit(solution)/shard_map/ppermute | solution.py:286
  144.2 2.8 %collective-permute-start.9 = (bf16[16,4,8,128]{3,2,1,0:T(8,128)(2,1)S(1)}, bf16[16,4,8,128]{3,2,1,0:T(8,128)(2,1)S(1)}, u32[]{:S(2)}, u32[]{:S(2)}) collective-permute-start(bf16[16,4,8,128]{3,2,1,0:T(8,128)(2,1)S(1)} %pad_maximum_fusion.3), channel_id=1, source_target_pairs={{0,9},{2,0},{4,2},{6,4},{14,6},{12,14},{10,12},{8,10},{1,8},{3,1},... | collective-permute-start | bytes 393224 | tf_op jit(solution)/shard_map/ppermute | solution.py:287
  147.0 1.8 collective-permute-done.8.refs_5_
  148.9 2.4 %collective-permute-done.9.refs_6_ = bf16[16,4,8,128]{3,2,1,0:T(8,128)(2,1)S(1)} collective-permute-done((bf16[16,4,8,128]{3,2,1,0:T(8,128)(2,1)S(1)}, bf16[16,4,8,128]{3,2,1,0:T(8,128)(2,1)S(1)}, u32[]{:S(2)}, u32[]{:S(2)}) %collective-permute-start.9) | collective-permute-done | bytes 131104 | tf_op jit(solution)/shard_map/ppermute | solution.py:287
  151.2 3.7 %shard_map.82 = (f32[4,4,16,128]{3,2,1,0:T(8,128)S(1)}, f32[4,4,16,128]{3,2,1,0:T(8,128)S(1)}, bf16[4,4,24,128]{3,2,1,0:T(8,128)(2,1)S(1)}) custom-call(bf16[8,7,2,16,128]{4,3,2,1,0:T(8,128)(2,1)S(1)} %all-to-all-done.r_ref.refs_0_, f32[4,4,16,128]{3,2,1,0:T(8,128)S(1)} %get-tuple-element.22.refs_1_, f32[4,4,16,128]{3,2,1,0:T(8,128)S(1)} %get-tuple-element.23.refs_2_, ...), custom_call_target="tpu_custom_call" | custom-call | tf_op jit(solution)/shard_map/pallas_call | solution.py:32
  154.9 6.5 %collective-permute-start.11 = (bf16[4,4,24,128]{3,2,1,0:T(8,128)(2,1)S(1)}, bf16[4,4,24,128]{3,2,1,0:T(8,128)(2,1)S(1)}, u32[]{:S(2)}, u32[]{:S(2)}) collective-permute-start(bf16[4,4,24,128]{3,2,1,0:T(8,128)(2,1)S(1)} %get-tuple-element.29.refs_5_), channel_id=1, source_target_pairs={{0,240},{16,0},{32,16},{48,32},{64,48},{80,64},{96,80},{112,96},{1... | collective-permute-start | bytes 294920 | tf_op jit(solution)/shard_map/ppermute | solution.py:278
  161.4 2.0 %collective-permute-start.10 = (bf16[4,4,24,128]{3,2,1,0:T(8,128)(2,1)S(1)}, bf16[4,4,24,128]{3,2,1,0:T(8,128)(2,1)S(1)}, u32[]{:S(2)}, u32[]{:S(2)}) collective-permute-start(bf16[4,4,24,128]{3,2,1,0:T(8,128)(2,1)S(1)} %get-tuple-element.29.refs_5_), channel_id=1, source_target_pairs={{0,16},{16,32},{32,48},{48,64},{64,80},{80,96},{96,112},{112,128},... | collective-permute-start | bytes 294920 | tf_op jit(solution)/shard_map/ppermute | solution.py:277
  163.4 1.9 %collective-permute-done.11.refs_4_ = bf16[4,4,24,128]{3,2,1,0:T(8,128)(2,1)S(1)} collective-permute-done((bf16[4,4,24,128]{3,2,1,0:T(8,128)(2,1)S(1)}, bf16[4,4,24,128]{3,2,1,0:T(8,128)(2,1)S(1)}, u32[]{:S(2)}, u32[]{:S(2)}) %collective-permute-start.11) | collective-permute-done | bytes 98336 | tf_op jit(solution)/shard_map/ppermute | solution.py:278
  165.3 5.7 %collective-permute-done.10.refs_3_ = bf16[4,4,24,128]{3,2,1,0:T(8,128)(2,1)S(1)} collective-permute-done((bf16[4,4,24,128]{3,2,1,0:T(8,128)(2,1)S(1)}, bf16[4,4,24,128]{3,2,1,0:T(8,128)(2,1)S(1)}, u32[]{:S(2)}, u32[]{:S(2)}) %collective-permute-start.10) | collective-permute-done | bytes 98336 | tf_op jit(solution)/shard_map/ppermute | solution.py:277
  171.0 2.9 %shard_map.83 = f32[2,4,2,2,16,128]{5,4,3,2,1,0:T(8,128)S(1)} custom-call(bf16[8,7,2,16,128]{4,3,2,1,0:T(8,128)(2,1)S(1)} %all-to-all-done.r_ref.refs_0_, f32[4,4,16,128]{3,2,1,0:T(8,128)S(1)} %get-tuple-element.27.refs_1_, f32[4,4,16,128]{3,2,1,0:T(8,128)S(1)} %get-tuple-element.28.refs_2_, bf16[4,4,24,128]{3,2,1,0:T(8,128)(2,1)S(1)} %collective-permute-done.10.refs_3_, ...), custom_call_target="tpu_custom_call" | custom-call | tf_op jit(solution)/shard_map/pallas_call | solution.py:32
  173.9 11.3 %all_to_all.20.in_ref = f32[8,2,2,16,128]{4,3,2,1,0:T(8,128)S(1)} all-to-all(f32[8,2,2,16,128]{4,3,2,1,0:T(8,128)S(1)} %bitcast.12), channel_id=1, replica_groups=mesh['grp'=2,'gX'=16,'gs'=2,'gy'=4,'gz'=2] {'gs','gy'}, dimensions={0} | all-to-all | bytes 524288 | tf_op jit(solution)/shard_map/all_to_all | solution.py:353
  185.2 0.9 shard_map.84
  (17 shorter events, 0.2 us)
Async XLA Ops:
  3.0 68.2 %all-to-all-start.1 = ((bf16[16,2,896]{2,1,0:T(2,128)(2,1)}), bf16[16,2,896]{2,1,0:T(2,128)(2,1)S(1)}, u32[]{:S(2)}, u32[]{:S(2)}) async-start(bf16[16,2,896]{2,1,0:T(2,128)(2,1)} %broadcast_in_dim.9), calls=%async_computation.1 | async-start | bytes 114688 | tf_op jit(solution)/shard_map/all_to_all | solution.py:298
  47.6 57.5 %copy-start = (f32[64]{0:T(128)S(1)}, f32[64]{0:T(128)}, u32[]{:S(2)}) copy-start(f32[64]{0:T(128)} %param.11) | copy-start | bytes 772
  71.2 12.6 %all-to-all-start = ((bf16[8,7,2,16,128]{4,3,2,1,0:T(8,128)(2,1)}), bf16[8,7,2,16,128]{4,3,2,1,0:T(8,128)(2,1)S(1)}, u32[]{:S(2)}, u32[]{:S(2)}) async-start(bf16[8,7,2,16,128]{4,3,2,1,0:T(8,128)(2,1)} %shard_map.77), calls=%async_computation | async-start | bytes 917504 | tf_op jit(solution)/shard_map/all_to_all | solution.py:321
  84.6 20.5 %all-to-all-start.2 = ((bf16[8,32,896]{2,1,0:T(8,128)(2,1)}), bf16[8,32,896]{2,1,0:T(8,128)(2,1)S(1)}, u32[]{:S(2)}, u32[]{:S(2)}) async-start(bf16[8,32,896]{2,1,0:T(8,128)(2,1)} %broadcast_in_dim.10), calls=%async_computation.2 | async-start | bytes 917504 | tf_op jit(solution)/shard_map/all_to_all | solution.py:302
  88.4 8.3 %collective-permute-start = (bf16[4,4,16,128]{3,2,1,0:T(8,128)(2,1)S(1)}, bf16[4,4,16,128]{3,2,1,0:T(8,128)(2,1)S(1)}, u32[]{:S(2)}, u32[]{:S(2)}) collective-permute-start(bf16[4,4,16,128]{3,2,1,0:T(8,128)(2,1)S(1)} %get-tuple-element.16), channel_id=1, source_target_pairs={{0,16},{16,32},{32,48},{48,64},{64,80},{80,96},{96,112},{112,128},... | collective-permute-start | bytes 196616 | tf_op jit(solution)/shard_map/ppermute | solution.py:277
  92.2 7.1 %collective-permute-start.1 = (bf16[4,4,16,128]{3,2,1,0:T(8,128)(2,1)S(1)}, bf16[4,4,16,128]{3,2,1,0:T(8,128)(2,1)S(1)}, u32[]{:S(2)}, u32[]{:S(2)}) collective-permute-start(bf16[4,4,16,128]{3,2,1,0:T(8,128)(2,1)S(1)} %get-tuple-element.16), channel_id=1, source_target_pairs={{0,240},{16,0},{32,16},{48,32},{64,48},{80,64},{96,80},{112,96},{1... | collective-permute-start | bytes 196616 | tf_op jit(solution)/shard_map/ppermute | solution.py:278
  99.4 7.9 %collective-permute-start.2 = (bf16[16,4,8,128]{3,2,1,0:T(8,128)(2,1)S(1)}, bf16[16,4,8,128]{3,2,1,0:T(8,128)(2,1)S(1)}, u32[]{:S(2)}, u32[]{:S(2)}) collective-permute-start(bf16[16,4,8,128]{3,2,1,0:T(8,128)(2,1)S(1)} %pad_maximum_fusion), channel_id=1, source_target_pairs={{0,2},{2,4},{4,6},{6,14},{14,12},{12,10},{10,8},{8,1},{1,3},{3,5},... | collective-permute-start | bytes 393224 | tf_op jit(solution)/shard_map/ppermute | solution.py:286
  103.1 6.9 %collective-permute-start.3 = (bf16[16,4,8,128]{3,2,1,0:T(8,128)(2,1)S(1)}, bf16[16,4,8,128]{3,2,1,0:T(8,128)(2,1)S(1)}, u32[]{:S(2)}, u32[]{:S(2)}) collective-permute-start(bf16[16,4,8,128]{3,2,1,0:T(8,128)(2,1)S(1)} %pad_maximum_fusion.1), channel_id=1, source_target_pairs={{0,9},{2,0},{4,2},{6,4},{14,6},{12,14},{10,12},{8,10},{1,8},{3,1},... | collective-permute-start | bytes 393224 | tf_op jit(solution)/shard_map/ppermute | solution.py:287
  113.7 9.6 %collective-permute-start.5 = (bf16[4,4,24,128]{3,2,1,0:T(8,128)(2,1)S(1)}, bf16[4,4,24,128]{3,2,1,0:T(8,128)(2,1)S(1)}, u32[]{:S(2)}, u32[]{:S(2)}) collective-permute-start(bf16[4,4,24,128]{3,2,1,0:T(8,128)(2,1)S(1)} %get-tuple-element.21.refs_5_), channel_id=1, source_target_pairs={{0,240},{16,0},{32,16},{48,32},{64,48},{80,64},{96,80},{112,96},{1... | collective-permute-start | bytes 294920 | tf_op jit(solution)/shard_map/ppermute | solution.py:278
  119.1 9.2 %collective-permute-start.4 = (bf16[4,4,24,128]{3,2,1,0:T(8,128)(2,1)S(1)}, bf16[4,4,24,128]{3,2,1,0:T(8,128)(2,1)S(1)}, u32[]{:S(2)}, u32[]{:S(2)}) collective-permute-start(bf16[4,4,24,128]{3,2,1,0:T(8,128)(2,1)S(1)} %get-tuple-element.21.refs_5_), channel_id=1, source_target_pairs={{0,16},{16,32},{32,48},{48,64},{64,80},{80,96},{96,112},{112,128},... | collective-permute-start | bytes 294920 | tf_op jit(solution)/shard_map/ppermute | solution.py:277
  131.2 8.7 %collective-permute-start.6 = (bf16[4,4,16,128]{3,2,1,0:T(8,128)(2,1)S(1)}, bf16[4,4,16,128]{3,2,1,0:T(8,128)(2,1)S(1)}, u32[]{:S(2)}, u32[]{:S(2)}) collective-permute-start(bf16[4,4,16,128]{3,2,1,0:T(8,128)(2,1)S(1)} %get-tuple-element.24), channel_id=1, source_target_pairs={{0,16},{16,32},{32,48},{48,64},{64,80},{80,96},{96,112},{112,128},... | collective-permute-start | bytes 196616 | tf_op jit(solution)/shard_map/ppermute | solution.py:277
  133.1 8.0 %collective-permute-start.7 = (bf16[4,4,16,128]{3,2,1,0:T(8,128)(2,1)S(1)}, bf16[4,4,16,128]{3,2,1,0:T(8,128)(2,1)S(1)}, u32[]{:S(2)}, u32[]{:S(2)}) collective-permute-start(bf16[4,4,16,128]{3,2,1,0:T(8,128)(2,1)S(1)} %get-tuple-element.24), channel_id=1, source_target_pairs={{0,240},{16,0},{32,16},{48,32},{64,48},{80,64},{96,80},{112,96},{1... | collective-permute-start | bytes 196616 | tf_op jit(solution)/shard_map/ppermute | solution.py:278
  141.2 7.7 %collective-permute-start.8 = (bf16[16,4,8,128]{3,2,1,0:T(8,128)(2,1)S(1)}, bf16[16,4,8,128]{3,2,1,0:T(8,128)(2,1)S(1)}, u32[]{:S(2)}, u32[]{:S(2)}) collective-permute-start(bf16[16,4,8,128]{3,2,1,0:T(8,128)(2,1)S(1)} %pad_maximum_fusion.2), channel_id=1, source_target_pairs={{0,2},{2,4},{4,6},{6,14},{14,12},{12,10},{10,8},{8,1},{1,3},{3,5},... | collective-permute-start | bytes 393224 | tf_op jit(solution)/shard_map/ppermute | solution.py:286
  144.2 7.0 %collective-permute-start.9 = (bf16[16,4,8,128]{3,2,1,0:T(8,128)(2,1)S(1)}, bf16[16,4,8,128]{3,2,1,0:T(8,128)(2,1)S(1)}, u32[]{:S(2)}, u32[]{:S(2)}) collective-permute-start(bf16[16,4,8,128]{3,2,1,0:T(8,128)(2,1)S(1)} %pad_maximum_fusion.3), channel_id=1, source_target_pairs={{0,9},{2,0},{4,2},{6,4},{14,6},{12,14},{10,12},{8,10},{1,8},{3,1},... | collective-permute-start | bytes 393224 | tf_op jit(solution)/shard_map/ppermute | solution.py:287
  154.9 10.4 %collective-permute-start.11 = (bf16[4,4,24,128]{3,2,1,0:T(8,128)(2,1)S(1)}, bf16[4,4,24,128]{3,2,1,0:T(8,128)(2,1)S(1)}, u32[]{:S(2)}, u32[]{:S(2)}) collective-permute-start(bf16[4,4,24,128]{3,2,1,0:T(8,128)(2,1)S(1)} %get-tuple-element.29.refs_5_), channel_id=1, source_target_pairs={{0,240},{16,0},{32,16},{48,32},{64,48},{80,64},{96,80},{112,96},{1... | collective-permute-start | bytes 294920 | tf_op jit(solution)/shard_map/ppermute | solution.py:278
  161.4 9.5 %collective-permute-start.10 = (bf16[4,4,24,128]{3,2,1,0:T(8,128)(2,1)S(1)}, bf16[4,4,24,128]{3,2,1,0:T(8,128)(2,1)S(1)}, u32[]{:S(2)}, u32[]{:S(2)}) collective-permute-start(bf16[4,4,24,128]{3,2,1,0:T(8,128)(2,1)S(1)} %get-tuple-element.29.refs_5_), channel_id=1, source_target_pairs={{0,16},{16,32},{32,48},{48,64},{64,80},{80,96},{96,112},{112,128},... | collective-permute-start | bytes 294920 | tf_op jit(solution)/shard_map/ppermute | solution.py:277

commit v4 on v3

--- a/solution.py
+++ b/solution.py
@@ -74,11 +74,19 @@
                 ref[:, x, y, :] = flat[y * chans : (y + 1) * chans, :]
 
 
-def weights_body(m_ref, out_ref, fwd_ref):
-    groups, chans, _ = m_ref.shape
+def weights_body(near, m_ref, out_ref, fwd_ref):
+    groups = near[1]
+    chans = near[0] * m_ref.shape[1]
     per = chans // groups
     taps = 27
-    turned = [m_ref[g].astype(F32).T.astype(BF16) for g in range(groups)]
+    at = lax.broadcasted_iota(jnp.int32, (chans, chans), 0)
+    row = at % (2 * near[0]) // 2 * (chans // near[0]) + at // (2 * near[0]) * 2 + at % 2
+    swap = (row == lax.broadcasted_iota(jnp.int32, (chans, chans), 1)).astype(BF16)
+    turned = []
+    for g in range(groups):
+        m = jnp.concatenate([m_ref[a * groups + g] for a in range(near[0])], axis=0)
+        m = jnp.dot(swap, m, preferred_element_type=F32)
+        turned.append(m.T.astype(BF16))
     for f in range(2):
         for tap in range(taps):
             at = (f * taps + tap) * per
@@ -160,7 +168,7 @@
         qo_ref, po_ref, qb_ref = (next(it) for _ in range(3))
         if not wide:
             rl_ref, rh_ref = next(it), next(it)
-    buf, rows_ref, act = (next(it) for _ in range(3))
+    buf, rows_a, rows_b, act = (next(it) for _ in range(4))
 
     pad = 2 * HALO if wide else HALO
     pitch = ZB + 2 * pad
@@ -182,26 +190,28 @@
         buf[HALO : HALO + XB, :, 8:end, :] = own_ref[...].astype(F32)
         buf[HALO + XB :, :, 8:end, :] = xh_ref[...].astype(F32)
 
-    def conv(x_in, w, use):
+    def build(j, x_in, rows):
         n = x_in * pitch
-        for j in range(4):
-            for c in range(3):
-                v = buf[0:x_in, j, 7 + c : 7 + c + pitch, :].reshape(n, 128).astype(BF16)
-                rows_ref[0:n, (j * 3 + c) * 128 : (j * 3 + c + 1) * 128] = v
-                if j == 0:
-                    rows_ref[0:n, (12 + c) * 128 : (13 + c) * 128] = v
+        for c in range(3):
+            v = buf[0:x_in, j, 7 + c : 7 + c + pitch, :].reshape(n, 128).astype(BF16)
+            rows[0:n, (j * 3 + c) * 128 : (j * 3 + c + 1) * 128] = v
+            if j == 0:
+                rows[0:n, (12 + c) * 128 : (13 + c) * 128] = v
+
+    def conv(x_in, w, use, rows, then=None):
+        n = x_in * pitch
         x_out = x_in - 2
         m = x_out * pitch
         for p in range(4):
             cols = slice(384 * p, 384 * p + 768)
-            t = jnp.dot(
-                rows_ref[0 : n - pitch, cols], w_ref[w, :, 0:256], preferred_element_type=F32
-            )
+            t = jnp.dot(rows[0 : n - pitch, cols], w_ref[w, :, 0:256], preferred_element_type=F32)
             o = t[0:m, 0:128] + t[pitch:, 128:256]
             o = o + jnp.dot(
-                rows_ref[2 * pitch : n, cols], w_ref[w, :, 256:384], preferred_element_type=F32
+                rows[2 * pitch : n, cols], w_ref[w, :, 256:384], preferred_element_type=F32
             )
             use(p, o.reshape(x_out, pitch, 128))
+            if then is not None:
+                build(p, x_out, then)
 
     def hidden(p, h):
         t = jnp.tanh(h + bias_ref[...])
@@ -246,10 +256,12 @@
             buf[x, p, lo:hi, :] = q
             qb_ref[x, j] = buf[x, p, lo - HALO : hi + HALO, :].astype(BF16)
 
-    conv(XB + 8, 0, hidden)
-    conv(XB + 6, 1, second)
-    conv(XB + 4, 3, back)
-    conv(XB + 2, 2, final)
+    for j in range(4):
+        build(j, XB + 8, rows_a)
+    conv(XB + 8, 0, hidden, rows_a, rows_b)
+    conv(XB + 6, 1, second, rows_b, rows_a)
+    conv(XB + 4, 3, back, rows_a, rows_b)
+    conv(XB + 2, 2, final, rows_b)
 
 
 def solution(mesh):
@@ -302,11 +314,10 @@
         near = lax.all_to_all(
             jnp.broadcast_to(far, (members, *far.shape)), ("gs", "gy"), 0, 0, tiled=True
         )
-        near = near.reshape(gs, gy, gX, *own.shape).transpose(1, 2, 0, 3, 4)
         (weights,) = kernel_call(
-            weights_body,
+            functools.partial(weights_body, (gs, gy)),
             [jax.ShapeDtypeStruct((4, 12 * chans, 6 * chans), BF16)],
-            (near.reshape(gy, chans, own.shape[1]),),
+            (near,),
             [VMEM((2, 27 * chans, chans), F32)],
         )
         bias_row = jnp.concatenate([bias, bias])[None, :]
@@ -345,6 +356,7 @@
                 (
                     VMEM((XB + 8, gy, pitch + 16, 128), F32),
                     VMEM(((XB + 8) * pitch, 15 * 128), BF16),
+                    VMEM(((XB + 6) * pitch, 15 * 128), BF16),
                     VMEM((XB + 6, gy, pitch, 128), F32),
                 ),
             )

time: 187 us -> 187 us (level)
  no operation moved by 1% of the time
where the time goes in v4:
time: 187 us; the launch traced here: 186 us
  starting transfers between devices  96.1 us (51%)
  waiting for transfers between devices  56.2 us (30%)
  Pallas kernels  17.9 us (10%)
  blocking collectives  11.3 us (6%)
  local copies, waits for them, and re-layouts  3.25 us (2%)
    all_to_all x1, starting transfers between devices, body(): lax.all_to_all(jnp.broadcast_to(own, (gX, *own.shape)), 'gX', 0, 0, tiled...  44.6 us
    ppermute x4, starting transfers between devices, along_x(): xh = lax.ppermute(block, 'gX', x_shift(-1))  22.1 us
    all_to_all x1, waiting for transfers between devices, body(): lax.all_to_all(jnp.broadcast_to(own, (gX, *own.shape)), 'gX', 0, 0, tiled...  21.2 us
    pallas_call x8, Pallas kernels, kernel_call(): pl.pallas_call(body, out_shape=outs if hbm_out else [VMEM(o.shape, o.dtyp...  17.9 us
    ppermute x4, waiting for transfers between devices, along_x(): xl = lax.ppermute(block, 'gX', x_shift(1))  11.6 us
    all_to_all x1, blocking collectives, body(): lax.all_to_all(res[0].reshape(members, 2, 2, ZB, 128), ('gs', 'gy'), 0, 0...  11.3 us
    ppermute x4, starting transfers between devices, along_x(): xl = lax.ppermute(block, 'gX', x_shift(1))  9.68 us
    all_to_all x1, waiting for transfers between devices, body(): held = lax.all_to_all(spread, ('gs', 'gy'), 0, 0, tiled=True)  7.99 us
  transfers between devices with their start and end apart: 15, of which 13 were waited for; matrix products, arithmetic and copies ran while one was open for 0% of the time, Pallas kernels for 2%

profile of v4, /device:TPU:40, one launch (start us, length us, event | category | flops | bytes accessed | tf_op | source)
XLA Modules:
  0.0 185.9 jit_solution(8586624644187188049)
XLA Ops:
  0.6 0.7 copy.13
  1.3 0.1 reshape.23
  1.4 0.7 copy.12
  2.2 0.1 reshape.25
  2.2 0.1 fusion.2
  2.3 0.7 broadcast_in_dim.9
  3.0 44.6 %all-to-all-start.1 = ((bf16[16,2,896]{2,1,0:T(2,128)(2,1)}), bf16[16,2,896]{2,1,0:T(2,128)(2,1)S(1)}, u32[]{:S(2)}, u32[]{:S(2)}) async-start(bf16[16,2,896]{2,1,0:T(2,128)(2,1)} %broadcast_in_dim.9), calls=%async_computation.1 | async-start | bytes 114688 | tf_op jit(solution)/shard_map/all_to_all | solution.py:310
  47.6 0.0 copy-start
  47.6 2.5 %shard_map.77 = bf16[8,7,2,16,128]{4,3,2,1,0:T(8,128)(2,1)} custom-call(f32[64,2,2,128]{3,2,1,0:T(2,128)} %q_ref.1, f32[64,2,2,128]{3,2,1,0:T(2,128)} %p_ref.1, bf16[3,64,2,2,128]{4,3,2,1,0:T(2,128)(2,1)} %n_ref.1), custom_call_target="tpu_custom_call" | custom-call | tf_op jit(solution)/shard_map/pallas_call | solution.py:32
  50.0 21.2 %all-to-all-done.1 = bf16[16,2,896]{2,1,0:T(2,128)(2,1)S(1)} async-done(((bf16[16,2,896]{2,1,0:T(2,128)(2,1)}), bf16[16,2,896]{2,1,0:T(2,128)(2,1)S(1)}, u32[]{:S(2)}, u32[]{:S(2)}) %all-to-all-start.1) | async-done | bytes 57376 | tf_op jit(solution)/shard_map/all_to_all | solution.py:310
  71.2 4.6 %all-to-all-start = ((bf16[8,7,2,16,128]{4,3,2,1,0:T(8,128)(2,1)}), bf16[8,7,2,16,128]{4,3,2,1,0:T(8,128)(2,1)S(1)}, u32[]{:S(2)}, u32[]{:S(2)}) async-start(bf16[8,7,2,16,128]{4,3,2,1,0:T(8,128)(2,1)} %shard_map.77), calls=%async_computation | async-start | bytes 917504 | tf_op jit(solution)/shard_map/all_to_all | solution.py:332
  75.8 8.0 %all-to-all-done.r_ref.refs_0_ = bf16[8,7,2,16,128]{4,3,2,1,0:T(8,128)(2,1)S(1)} async-done(((bf16[8,7,2,16,128]{4,3,2,1,0:T(8,128)(2,1)}), bf16[8,7,2,16,128]{4,3,2,1,0:T(8,128)(2,1)S(1)}, u32[]{:S(2)}, u32[]{:S(2)}) %all-to-all-start) | async-done | bytes 458784 | tf_op jit(solution)/shard_map/all_to_all | solution.py:332
  83.8 0.8 broadcast_in_dim.10
  84.6 3.7 %all-to-all-start.2 = ((bf16[8,32,896]{2,1,0:T(8,128)(2,1)}), bf16[8,32,896]{2,1,0:T(8,128)(2,1)S(1)}, u32[]{:S(2)}, u32[]{:S(2)}) async-start(bf16[8,32,896]{2,1,0:T(8,128)(2,1)} %broadcast_in_dim.10), calls=%async_computation.2 | async-start | bytes 917504 | tf_op jit(solution)/shard_map/all_to_all | solution.py:314
  88.3 0.1 shard_map.78
  88.4 3.8 %collective-permute-start = (bf16[4,4,16,128]{3,2,1,0:T(8,128)(2,1)S(1)}, bf16[4,4,16,128]{3,2,1,0:T(8,128)(2,1)S(1)}, u32[]{:S(2)}, u32[]{:S(2)}) collective-permute-start(bf16[4,4,16,128]{3,2,1,0:T(8,128)(2,1)S(1)} %get-tuple-element.16), channel_id=1, source_target_pairs={{0,16},{16,32},{32,48},{48,64},{64,80},{80,96},{96,112},{112,128},... | collective-permute-start | bytes 196616 | tf_op jit(solution)/shard_map/ppermute | solution.py:289
  92.2 4.2 %collective-permute-start.1 = (bf16[4,4,16,128]{3,2,1,0:T(8,128)(2,1)S(1)}, bf16[4,4,16,128]{3,2,1,0:T(8,128)(2,1)S(1)}, u32[]{:S(2)}, u32[]{:S(2)}) collective-permute-start(bf16[4,4,16,128]{3,2,1,0:T(8,128)(2,1)S(1)} %get-tuple-element.16), channel_id=1, source_target_pairs={{0,240},{16,0},{32,16},{48,32},{64,48},{80,64},{96,80},{112,96},{1... | collective-permute-start | bytes 196616 | tf_op jit(solution)/shard_map/ppermute | solution.py:290
  96.4 0.3 collective-permute-done.refs_1_
  96.8 2.6 %collective-permute-done.1.refs_2_ = bf16[4,4,16,128]{3,2,1,0:T(8,128)(2,1)S(1)} collective-permute-done((bf16[4,4,16,128]{3,2,1,0:T(8,128)(2,1)S(1)}, bf16[4,4,16,128]{3,2,1,0:T(8,128)(2,1)S(1)}, u32[]{:S(2)}, u32[]{:S(2)}) %collective-permute-start.1) | collective-permute-done | bytes 65568 | tf_op jit(solution)/shard_map/ppermute | solution.py:290
  99.4 3.7 %collective-permute-start.2 = (bf16[16,4,8,128]{3,2,1,0:T(8,128)(2,1)S(1)}, bf16[16,4,8,128]{3,2,1,0:T(8,128)(2,1)S(1)}, u32[]{:S(2)}, u32[]{:S(2)}) collective-permute-start(bf16[16,4,8,128]{3,2,1,0:T(8,128)(2,1)S(1)} %pad_maximum_fusion), channel_id=1, source_target_pairs={{0,2},{2,4},{4,6},{6,14},{14,12},{12,10},{10,8},{8,1},{1,3},{3,5},... | collective-permute-start | bytes 393224 | tf_op jit(solution)/shard_map/ppermute | solution.py:298
  103.1 2.0 %collective-permute-start.3 = (bf16[16,4,8,128]{3,2,1,0:T(8,128)(2,1)S(1)}, bf16[16,4,8,128]{3,2,1,0:T(8,128)(2,1)S(1)}, u32[]{:S(2)}, u32[]{:S(2)}) collective-permute-start(bf16[16,4,8,128]{3,2,1,0:T(8,128)(2,1)S(1)} %pad_maximum_fusion.1), channel_id=1, source_target_pairs={{0,9},{2,0},{4,2},{6,4},{14,6},{12,14},{10,12},{8,10},{1,8},{3,1},... | collective-permute-start | bytes 393224 | tf_op jit(solution)/shard_map/ppermute | solution.py:299
  105.1 0.1 maximum_bitcast_fusion.refs_6_.refs_7_.refs_8_
  105.2 0.0 all-to-all-done.2.m_ref
  105.2 1.5 shard_map.79.refs_5_.refs_6_.refs_7_
  106.7 0.0 collective-permute-done.2.refs_3_
  106.7 3.3 %collective-permute-done.3.refs_4_ = bf16[16,4,8,128]{3,2,1,0:T(8,128)(2,1)S(1)} collective-permute-done((bf16[16,4,8,128]{3,2,1,0:T(8,128)(2,1)S(1)}, bf16[16,4,8,128]{3,2,1,0:T(8,128)(2,1)S(1)}, u32[]{:S(2)}, u32[]{:S(2)}) %collective-permute-start.3) | collective-permute-done | bytes 131104 | tf_op jit(solution)/shard_map/ppermute | solution.py:299
  110.0 3.6 %shard_map.80 = (f32[4,4,16,128]{3,2,1,0:T(8,128)S(1)}, f32[4,4,16,128]{3,2,1,0:T(8,128)S(1)}, bf16[4,4,24,128]{3,2,1,0:T(8,128)(2,1)S(1)}) custom-call(bf16[8,7,2,16,128]{4,3,2,1,0:T(8,128)(2,1)S(1)} %all-to-all-done.r_ref.refs_0_, bf16[4,4,16,128]{3,2,1,0:T(8,128)(2,1)S(1)} %collective-permute-done.refs_1_, ...), custom_call_target="tpu_custom_call" | custom-call | tf_op jit(solution)/shard_map/pallas_call | solution.py:32
  113.6 5.4 %collective-permute-start.5 = (bf16[4,4,24,128]{3,2,1,0:T(8,128)(2,1)S(1)}, bf16[4,4,24,128]{3,2,1,0:T(8,128)(2,1)S(1)}, u32[]{:S(2)}, u32[]{:S(2)}) collective-permute-start(bf16[4,4,24,128]{3,2,1,0:T(8,128)(2,1)S(1)} %get-tuple-element.21.refs_5_), channel_id=1, source_target_pairs={{0,240},{16,0},{32,16},{48,32},{64,48},{80,64},{96,80},{112,96},{1... | collective-permute-start | bytes 294920 | tf_op jit(solution)/shard_map/ppermute | solution.py:290
  119.0 2.0 %collective-permute-start.4 = (bf16[4,4,24,128]{3,2,1,0:T(8,128)(2,1)S(1)}, bf16[4,4,24,128]{3,2,1,0:T(8,128)(2,1)S(1)}, u32[]{:S(2)}, u32[]{:S(2)}) collective-permute-start(bf16[4,4,24,128]{3,2,1,0:T(8,128)(2,1)S(1)} %get-tuple-element.21.refs_5_), channel_id=1, source_target_pairs={{0,16},{16,32},{32,48},{48,64},{64,80},{80,96},{96,112},{112,128},... | collective-permute-start | bytes 294920 | tf_op jit(solution)/shard_map/ppermute | solution.py:289
  121.0 2.2 %collective-permute-done.5.refs_4_ = bf16[4,4,24,128]{3,2,1,0:T(8,128)(2,1)S(1)} collective-permute-done((bf16[4,4,24,128]{3,2,1,0:T(8,128)(2,1)S(1)}, bf16[4,4,24,128]{3,2,1,0:T(8,128)(2,1)S(1)}, u32[]{:S(2)}, u32[]{:S(2)}) %collective-permute-start.5) | collective-permute-done | bytes 98336 | tf_op jit(solution)/shard_map/ppermute | solution.py:290
  123.2 5.0 %collective-permute-done.4.refs_3_ = bf16[4,4,24,128]{3,2,1,0:T(8,128)(2,1)S(1)} collective-permute-done((bf16[4,4,24,128]{3,2,1,0:T(8,128)(2,1)S(1)}, bf16[4,4,24,128]{3,2,1,0:T(8,128)(2,1)S(1)}, u32[]{:S(2)}, u32[]{:S(2)}) %collective-permute-start.4) | collective-permute-done | bytes 98336 | tf_op jit(solution)/shard_map/ppermute | solution.py:289
  128.2 2.9 %shard_map.81 = (f32[4,4,16,128]{3,2,1,0:T(8,128)S(1)}, f32[4,4,16,128]{3,2,1,0:T(8,128)S(1)}, bf16[4,4,16,128]{3,2,1,0:T(8,128)(2,1)S(1)}, bf16[4,4,8,128]{3,2,1,0:T(8,128)(2,1)S(1)}, bf16[4,4,8,128]{3,2,1,0:T(8,128)(2,1)S(1)}) custom-call(bf16[8,7,2,16,128]{4,3,2,1,0:T(8,128)(2,1)S(1)} %all-to-all-done.r_ref.refs_0_, ...), custom_call_target="tpu_custom_call" | custom-call | tf_op jit(solution)/shard_map/pallas_call | solution.py:32
  131.1 2.0 %collective-permute-start.6 = (bf16[4,4,16,128]{3,2,1,0:T(8,128)(2,1)S(1)}, bf16[4,4,16,128]{3,2,1,0:T(8,128)(2,1)S(1)}, u32[]{:S(2)}, u32[]{:S(2)}) collective-permute-start(bf16[4,4,16,128]{3,2,1,0:T(8,128)(2,1)S(1)} %get-tuple-element.24), channel_id=1, source_target_pairs={{0,16},{16,32},{32,48},{48,64},{64,80},{80,96},{96,112},{112,128},... | collective-permute-start | bytes 196616 | tf_op jit(solution)/shard_map/ppermute | solution.py:289
  133.0 6.1 %collective-permute-start.7 = (bf16[4,4,16,128]{3,2,1,0:T(8,128)(2,1)S(1)}, bf16[4,4,16,128]{3,2,1,0:T(8,128)(2,1)S(1)}, u32[]{:S(2)}, u32[]{:S(2)}) collective-permute-start(bf16[4,4,16,128]{3,2,1,0:T(8,128)(2,1)S(1)} %get-tuple-element.24), channel_id=1, source_target_pairs={{0,240},{16,0},{32,16},{48,32},{64,48},{80,64},{96,80},{112,96},{1... | collective-permute-start | bytes 196616 | tf_op jit(solution)/shard_map/ppermute | solution.py:290
  139.1 0.7 collective-permute-done.6.refs_3_
  139.8 1.2 collective-permute-done.7.refs_4_
  141.1 3.0 %collective-permute-start.8 = (bf16[16,4,8,128]{3,2,1,0:T(8,128)(2,1)S(1)}, bf16[16,4,8,128]{3,2,1,0:T(8,128)(2,1)S(1)}, u32[]{:S(2)}, u32[]{:S(2)}) collective-permute-start(bf16[16,4,8,128]{3,2,1,0:T(8,128)(2,1)S(1)} %pad_maximum_fusion.2), channel_id=1, source_target_pairs={{0,2},{2,4},{4,6},{6,14},{14,12},{12,10},{10,8},{8,1},{1,3},{3,5},... | collective-permute-start | bytes 393224 | tf_op jit(solution)/shard_map/ppermute | solution.py:298
  144.2 2.8 %collective-permute-start.9 = (bf16[16,4,8,128]{3,2,1,0:T(8,128)(2,1)S(1)}, bf16[16,4,8,128]{3,2,1,0:T(8,128)(2,1)S(1)}, u32[]{:S(2)}, u32[]{:S(2)}) collective-permute-start(bf16[16,4,8,128]{3,2,1,0:T(8,128)(2,1)S(1)} %pad_maximum_fusion.3), channel_id=1, source_target_pairs={{0,9},{2,0},{4,2},{6,4},{14,6},{12,14},{10,12},{8,10},{1,8},{3,1},... | collective-permute-start | bytes 393224 | tf_op jit(solution)/shard_map/ppermute | solution.py:299
  146.9 1.8 collective-permute-done.8.refs_5_
  148.8 2.4 %collective-permute-done.9.refs_6_ = bf16[16,4,8,128]{3,2,1,0:T(8,128)(2,1)S(1)} collective-permute-done((bf16[16,4,8,128]{3,2,1,0:T(8,128)(2,1)S(1)}, bf16[16,4,8,128]{3,2,1,0:T(8,128)(2,1)S(1)}, u32[]{:S(2)}, u32[]{:S(2)}) %collective-permute-start.9) | collective-permute-done | bytes 131104 | tf_op jit(solution)/shard_map/ppermute | solution.py:299
  151.1 3.6 %shard_map.82 = (f32[4,4,16,128]{3,2,1,0:T(8,128)S(1)}, f32[4,4,16,128]{3,2,1,0:T(8,128)S(1)}, bf16[4,4,24,128]{3,2,1,0:T(8,128)(2,1)S(1)}) custom-call(bf16[8,7,2,16,128]{4,3,2,1,0:T(8,128)(2,1)S(1)} %all-to-all-done.r_ref.refs_0_, f32[4,4,16,128]{3,2,1,0:T(8,128)S(1)} %get-tuple-element.22.refs_1_, f32[4,4,16,128]{3,2,1,0:T(8,128)S(1)} %get-tuple-element.23.refs_2_, ...), custom_call_target="tpu_custom_call" | custom-call | tf_op jit(solution)/shard_map/pallas_call | solution.py:32
  154.8 6.5 %collective-permute-start.11 = (bf16[4,4,24,128]{3,2,1,0:T(8,128)(2,1)S(1)}, bf16[4,4,24,128]{3,2,1,0:T(8,128)(2,1)S(1)}, u32[]{:S(2)}, u32[]{:S(2)}) collective-permute-start(bf16[4,4,24,128]{3,2,1,0:T(8,128)(2,1)S(1)} %get-tuple-element.29.refs_5_), channel_id=1, source_target_pairs={{0,240},{16,0},{32,16},{48,32},{64,48},{80,64},{96,80},{112,96},{1... | collective-permute-start | bytes 294920 | tf_op jit(solution)/shard_map/ppermute | solution.py:290
  161.3 2.0 %collective-permute-start.10 = (bf16[4,4,24,128]{3,2,1,0:T(8,128)(2,1)S(1)}, bf16[4,4,24,128]{3,2,1,0:T(8,128)(2,1)S(1)}, u32[]{:S(2)}, u32[]{:S(2)}) collective-permute-start(bf16[4,4,24,128]{3,2,1,0:T(8,128)(2,1)S(1)} %get-tuple-element.29.refs_5_), channel_id=1, source_target_pairs={{0,16},{16,32},{32,48},{48,64},{64,80},{80,96},{96,112},{112,128},... | collective-permute-start | bytes 294920 | tf_op jit(solution)/shard_map/ppermute | solution.py:289
  163.2 1.9 %collective-permute-done.11.refs_4_ = bf16[4,4,24,128]{3,2,1,0:T(8,128)(2,1)S(1)} collective-permute-done((bf16[4,4,24,128]{3,2,1,0:T(8,128)(2,1)S(1)}, bf16[4,4,24,128]{3,2,1,0:T(8,128)(2,1)S(1)}, u32[]{:S(2)}, u32[]{:S(2)}) %collective-permute-start.11) | collective-permute-done | bytes 98336 | tf_op jit(solution)/shard_map/ppermute | solution.py:290
  165.2 5.7 %collective-permute-done.10.refs_3_ = bf16[4,4,24,128]{3,2,1,0:T(8,128)(2,1)S(1)} collective-permute-done((bf16[4,4,24,128]{3,2,1,0:T(8,128)(2,1)S(1)}, bf16[4,4,24,128]{3,2,1,0:T(8,128)(2,1)S(1)}, u32[]{:S(2)}, u32[]{:S(2)}) %collective-permute-start.10) | collective-permute-done | bytes 98336 | tf_op jit(solution)/shard_map/ppermute | solution.py:289
  170.8 2.9 %shard_map.83 = f32[2,4,2,2,16,128]{5,4,3,2,1,0:T(8,128)S(1)} custom-call(bf16[8,7,2,16,128]{4,3,2,1,0:T(8,128)(2,1)S(1)} %all-to-all-done.r_ref.refs_0_, f32[4,4,16,128]{3,2,1,0:T(8,128)S(1)} %get-tuple-element.27.refs_1_, f32[4,4,16,128]{3,2,1,0:T(8,128)S(1)} %get-tuple-element.28.refs_2_, bf16[4,4,24,128]{3,2,1,0:T(8,128)(2,1)S(1)} %collective-permute-done.10.refs_3_, ...), custom_call_target="tpu_custom_call" | custom-call | tf_op jit(solution)/shard_map/pallas_call | solution.py:32
  173.7 11.3 %all_to_all.20.in_ref = f32[8,2,2,16,128]{4,3,2,1,0:T(8,128)S(1)} all-to-all(f32[8,2,2,16,128]{4,3,2,1,0:T(8,128)S(1)} %bitcast.11), channel_id=1, replica_groups=mesh['grp'=2,'gX'=16,'gs'=2,'gy'=4,'gz'=2] {'gs','gy'}, dimensions={0} | all-to-all | bytes 524288 | tf_op jit(solution)/shard_map/all_to_all | solution.py:365
  185.0 0.9 shard_map.84
  (14 shorter events, 0.2 us)
Async XLA Ops:
  3.0 68.2 %all-to-all-start.1 = ((bf16[16,2,896]{2,1,0:T(2,128)(2,1)}), bf16[16,2,896]{2,1,0:T(2,128)(2,1)S(1)}, u32[]{:S(2)}, u32[]{:S(2)}) async-start(bf16[16,2,896]{2,1,0:T(2,128)(2,1)} %broadcast_in_dim.9), calls=%async_computation.1 | async-start | bytes 114688 | tf_op jit(solution)/shard_map/all_to_all | solution.py:310
  47.6 57.5 %copy-start = (f32[64]{0:T(128)S(1)}, f32[64]{0:T(128)}, u32[]{:S(2)}) copy-start(f32[64]{0:T(128)} %param.11) | copy-start | bytes 772
  71.2 12.6 %all-to-all-start = ((bf16[8,7,2,16,128]{4,3,2,1,0:T(8,128)(2,1)}), bf16[8,7,2,16,128]{4,3,2,1,0:T(8,128)(2,1)S(1)}, u32[]{:S(2)}, u32[]{:S(2)}) async-start(bf16[8,7,2,16,128]{4,3,2,1,0:T(8,128)(2,1)} %shard_map.77), calls=%async_computation | async-start | bytes 917504 | tf_op jit(solution)/shard_map/all_to_all | solution.py:332
  84.6 20.5 %all-to-all-start.2 = ((bf16[8,32,896]{2,1,0:T(8,128)(2,1)}), bf16[8,32,896]{2,1,0:T(8,128)(2,1)S(1)}, u32[]{:S(2)}, u32[]{:S(2)}) async-start(bf16[8,32,896]{2,1,0:T(8,128)(2,1)} %broadcast_in_dim.10), calls=%async_computation.2 | async-start | bytes 917504 | tf_op jit(solution)/shard_map/all_to_all | solution.py:314
  88.4 8.3 %collective-permute-start = (bf16[4,4,16,128]{3,2,1,0:T(8,128)(2,1)S(1)}, bf16[4,4,16,128]{3,2,1,0:T(8,128)(2,1)S(1)}, u32[]{:S(2)}, u32[]{:S(2)}) collective-permute-start(bf16[4,4,16,128]{3,2,1,0:T(8,128)(2,1)S(1)} %get-tuple-element.16), channel_id=1, source_target_pairs={{0,16},{16,32},{32,48},{48,64},{64,80},{80,96},{96,112},{112,128},... | collective-permute-start | bytes 196616 | tf_op jit(solution)/shard_map/ppermute | solution.py:289
  92.2 7.1 %collective-permute-start.1 = (bf16[4,4,16,128]{3,2,1,0:T(8,128)(2,1)S(1)}, bf16[4,4,16,128]{3,2,1,0:T(8,128)(2,1)S(1)}, u32[]{:S(2)}, u32[]{:S(2)}) collective-permute-start(bf16[4,4,16,128]{3,2,1,0:T(8,128)(2,1)S(1)} %get-tuple-element.16), channel_id=1, source_target_pairs={{0,240},{16,0},{32,16},{48,32},{64,48},{80,64},{96,80},{112,96},{1... | collective-permute-start | bytes 196616 | tf_op jit(solution)/shard_map/ppermute | solution.py:290
  99.4 7.3 %collective-permute-start.2 = (bf16[16,4,8,128]{3,2,1,0:T(8,128)(2,1)S(1)}, bf16[16,4,8,128]{3,2,1,0:T(8,128)(2,1)S(1)}, u32[]{:S(2)}, u32[]{:S(2)}) collective-permute-start(bf16[16,4,8,128]{3,2,1,0:T(8,128)(2,1)S(1)} %pad_maximum_fusion), channel_id=1, source_target_pairs={{0,2},{2,4},{4,6},{6,14},{14,12},{12,10},{10,8},{8,1},{1,3},{3,5},... | collective-permute-start | bytes 393224 | tf_op jit(solution)/shard_map/ppermute | solution.py:298
  103.1 6.9 %collective-permute-start.3 = (bf16[16,4,8,128]{3,2,1,0:T(8,128)(2,1)S(1)}, bf16[16,4,8,128]{3,2,1,0:T(8,128)(2,1)S(1)}, u32[]{:S(2)}, u32[]{:S(2)}) collective-permute-start(bf16[16,4,8,128]{3,2,1,0:T(8,128)(2,1)S(1)} %pad_maximum_fusion.1), channel_id=1, source_target_pairs={{0,9},{2,0},{4,2},{6,4},{14,6},{12,14},{10,12},{8,10},{1,8},{3,1},... | collective-permute-start | bytes 393224 | tf_op jit(solution)/shard_map/ppermute | solution.py:299
  113.6 9.6 %collective-permute-start.5 = (bf16[4,4,24,128]{3,2,1,0:T(8,128)(2,1)S(1)}, bf16[4,4,24,128]{3,2,1,0:T(8,128)(2,1)S(1)}, u32[]{:S(2)}, u32[]{:S(2)}) collective-permute-start(bf16[4,4,24,128]{3,2,1,0:T(8,128)(2,1)S(1)} %get-tuple-element.21.refs_5_), channel_id=1, source_target_pairs={{0,240},{16,0},{32,16},{48,32},{64,48},{80,64},{96,80},{112,96},{1... | collective-permute-start | bytes 294920 | tf_op jit(solution)/shard_map/ppermute | solution.py:290
  119.0 9.2 %collective-permute-start.4 = (bf16[4,4,24,128]{3,2,1,0:T(8,128)(2,1)S(1)}, bf16[4,4,24,128]{3,2,1,0:T(8,128)(2,1)S(1)}, u32[]{:S(2)}, u32[]{:S(2)}) collective-permute-start(bf16[4,4,24,128]{3,2,1,0:T(8,128)(2,1)S(1)} %get-tuple-element.21.refs_5_), channel_id=1, source_target_pairs={{0,16},{16,32},{32,48},{48,64},{64,80},{80,96},{96,112},{112,128},... | collective-permute-start | bytes 294920 | tf_op jit(solution)/shard_map/ppermute | solution.py:289
  131.1 8.7 %collective-permute-start.6 = (bf16[4,4,16,128]{3,2,1,0:T(8,128)(2,1)S(1)}, bf16[4,4,16,128]{3,2,1,0:T(8,128)(2,1)S(1)}, u32[]{:S(2)}, u32[]{:S(2)}) collective-permute-start(bf16[4,4,16,128]{3,2,1,0:T(8,128)(2,1)S(1)} %get-tuple-element.24), channel_id=1, source_target_pairs={{0,16},{16,32},{32,48},{48,64},{64,80},{80,96},{96,112},{112,128},... | collective-permute-start | bytes 196616 | tf_op jit(solution)/shard_map/ppermute | solution.py:289
  133.0 8.0 %collective-permute-start.7 = (bf16[4,4,16,128]{3,2,1,0:T(8,128)(2,1)S(1)}, bf16[4,4,16,128]{3,2,1,0:T(8,128)(2,1)S(1)}, u32[]{:S(2)}, u32[]{:S(2)}) collective-permute-start(bf16[4,4,16,128]{3,2,1,0:T(8,128)(2,1)S(1)} %get-tuple-element.24), channel_id=1, source_target_pairs={{0,240},{16,0},{32,16},{48,32},{64,48},{80,64},{96,80},{112,96},{1... | collective-permute-start | bytes 196616 | tf_op jit(solution)/shard_map/ppermute | solution.py:290
  141.1 7.7 %collective-permute-start.8 = (bf16[16,4,8,128]{3,2,1,0:T(8,128)(2,1)S(1)}, bf16[16,4,8,128]{3,2,1,0:T(8,128)(2,1)S(1)}, u32[]{:S(2)}, u32[]{:S(2)}) collective-permute-start(bf16[16,4,8,128]{3,2,1,0:T(8,128)(2,1)S(1)} %pad_maximum_fusion.2), channel_id=1, source_target_pairs={{0,2},{2,4},{4,6},{6,14},{14,12},{12,10},{10,8},{8,1},{1,3},{3,5},... | collective-permute-start | bytes 393224 | tf_op jit(solution)/shard_map/ppermute | solution.py:298
  144.2 7.0 %collective-permute-start.9 = (bf16[16,4,8,128]{3,2,1,0:T(8,128)(2,1)S(1)}, bf16[16,4,8,128]{3,2,1,0:T(8,128)(2,1)S(1)}, u32[]{:S(2)}, u32[]{:S(2)}) collective-permute-start(bf16[16,4,8,128]{3,2,1,0:T(8,128)(2,1)S(1)} %pad_maximum_fusion.3), channel_id=1, source_target_pairs={{0,9},{2,0},{4,2},{6,4},{14,6},{12,14},{10,12},{8,10},{1,8},{3,1},... | collective-permute-start | bytes 393224 | tf_op jit(solution)/shard_map/ppermute | solution.py:299
  154.8 10.4 %collective-permute-start.11 = (bf16[4,4,24,128]{3,2,1,0:T(8,128)(2,1)S(1)}, bf16[4,4,24,128]{3,2,1,0:T(8,128)(2,1)S(1)}, u32[]{:S(2)}, u32[]{:S(2)}) collective-permute-start(bf16[4,4,24,128]{3,2,1,0:T(8,128)(2,1)S(1)} %get-tuple-element.29.refs_5_), channel_id=1, source_target_pairs={{0,240},{16,0},{32,16},{48,32},{64,48},{80,64},{96,80},{112,96},{1... | collective-permute-start | bytes 294920 | tf_op jit(solution)/shard_map/ppermute | solution.py:290
  161.3 9.5 %collective-permute-start.10 = (bf16[4,4,24,128]{3,2,1,0:T(8,128)(2,1)S(1)}, bf16[4,4,24,128]{3,2,1,0:T(8,128)(2,1)S(1)}, u32[]{:S(2)}, u32[]{:S(2)}) collective-permute-start(bf16[4,4,24,128]{3,2,1,0:T(8,128)(2,1)S(1)} %get-tuple-element.29.refs_5_), channel_id=1, source_target_pairs={{0,16},{16,32},{32,48},{48,64},{64,80},{80,96},{96,112},{112,128},... | collective-permute-start | bytes 294920 | tf_op jit(solution)/shard_map/ppermute | solution.py:289

commit v5 on v4

--- a/solution.py
+++ b/solution.py
@@ -25,7 +25,7 @@
     return path + [(a, 0) for a in range(rows - 1, 0, -1)]
 
 
-def kernel_call(body, outs, args, scratch=(), hbm_in=False, hbm_out=False):
+def kernel_call(body, outs, args, scratch=(), hbm_in=False, hbm_out=False, out_space=VMEM):
     spec = pl.BlockSpec(memory_space=VMEM)
     space = pltpu.HBM if hbm_in else VMEM
     args = [pltpu.with_memory_space_constraint(v, space) for v in args]
@@ -33,26 +33,38 @@
         body,
         out_shape=outs if hbm_out else [VMEM(o.shape, o.dtype) for o in outs],
         in_specs=[spec] * len(args),
-        out_specs=[spec] * len(outs),
+        out_specs=[pl.BlockSpec(memory_space=out_space)] * len(outs),
         scratch_shapes=list(scratch),
         compiler_params=pltpu.CompilerParams(vmem_limit_bytes=LIMIT),
     )(*args)
 
 
-def spread_body(place, q_ref, p_ref, n_ref, out_ref):
-    def send(part, x, flat):
+def spread_body(place, q_ref, p_ref, n_ref, out_ref, made, sems):
+    copies = []
+
+    def keep(part, x, flat):
         for member, block in enumerate(place):
-            out_ref[member, part, x] = flat[block * ZB : (block + 1) * ZB, :]
-
-    for x in range(q_ref.shape[1]):
-        for k, ref in enumerate((q_ref, p_ref)):
+            made[member, part, x] = flat[block * ZB : (block + 1) * ZB, :]
+
+    def send(part):
+        copies.append(pltpu.make_async_copy(made.at[:, part], out_ref.at[:, part], sems.at[part]))
+        copies[-1].start()
+
+    for k, ref in enumerate((q_ref, p_ref)):
+        for x in range(ref.shape[1]):
             flat = jnp.concatenate([ref[:, x, y, :] for y in range(ref.shape[2])], axis=0).T
             high = flat.astype(BF16)
-            send(2 * k, x, high)
-            send(2 * k + 1, x, (flat - high.astype(F32)).astype(BF16))
-        for k in range(n_ref.shape[0]):
+            keep(2 * k, x, high)
+            keep(2 * k + 1, x, (flat - high.astype(F32)).astype(BF16))
+        send(2 * k)
+        send(2 * k + 1)
+    for k in range(n_ref.shape[0]):
+        for x in range(n_ref.shape[2]):
             parts = [n_ref[k, :, x, y, :].astype(F32) for y in range(n_ref.shape[3])]
-            send(4 + k, x, jnp.concatenate(parts, axis=0).T.astype(BF16))
+            keep(4 + k, x, jnp.concatenate(parts, axis=0).T.astype(BF16))
+        send(4 + k)
+    for copy in copies:
+        copy.wait()
 
 
 def held_at(r_ref, array, x, j):
@@ -74,7 +86,7 @@
                 ref[:, x, y, :] = flat[y * chans : (y + 1) * chans, :]
 
 
-def weights_body(near, m_ref, out_ref, fwd_ref):
+def weights_body(near, m_ref, out_ref, top_ref, fwd_ref):
     groups = near[1]
     chans = near[0] * m_ref.shape[1]
     per = chans // groups
@@ -96,21 +108,29 @@
                 ].astype(F32)
     zero = jnp.zeros((chans, chans), BF16)
 
+    def store(w, a, row, u, block):
+        row = row * chans
+        if a < 2:
+            col = (a * 2 + u) * chans
+            out_ref[w, row : row + chans, col : col + chans] = block
+            return
+        for pair in range(2):
+            at, col = row + pair * 6 * chans, (pair * 2 + u) * chans
+            top_ref[w, at : at + chans, col : col + chans] = block
+
     def place(w, tap, block):
         a, b, c = tap // 9, tap // 3 % 3, tap % 3
         for u in range(2):
             t = b + u
-            row = ((t // 2 * 3 + c) * 2 + t % 2) * chans
-            col = (a * 2 + u) * chans
-            out_ref[w, row : row + chans, col : col + chans] = block
+            store(w, a, (t // 2 * 3 + c) * 2 + t % 2, u, block)
 
     for w in range(4):
+        top_ref[w, 0 : 6 * chans, 2 * chans :] = jnp.zeros((6 * chans, 2 * chans), BF16)
+        top_ref[w, 12 * chans :, 0 : 2 * chans] = jnp.zeros((6 * chans, 2 * chans), BF16)
         for c in range(3):
             for a in range(3):
                 for t, u in ((3, 0), (0, 1)):
-                    row = ((t // 2 * 3 + c) * 2 + t % 2) * chans
-                    col = (a * 2 + u) * chans
-                    out_ref[w, row : row + chans, col : col + chans] = zero
+                    store(w, a, (t // 2 * 3 + c) * 2 + t % 2, u, zero)
     for f in range(2):
         for tap in range(0, taps, 2):
             n = min(2, taps - tap)
@@ -159,9 +179,9 @@
     step_at = {"first": 0}.get(kind, kind)
     noise_of = lambda x, j, k: held_at(r_ref, 2 + k, x, j)
     if wide:
-        xl_ref, xh_ref, zl_ref, zh_ref, w_ref, bias_ref = (next(it) for _ in range(6))
+        xl_ref, xh_ref, zl_ref, zh_ref, w_ref, w2_ref, bias_ref = (next(it) for _ in range(7))
     else:
-        xl_ref, xh_ref, own_ref, w_ref, bias_ref = (next(it) for _ in range(5))
+        xl_ref, xh_ref, own_ref, w_ref, w2_ref, bias_ref = (next(it) for _ in range(6))
     if kind == "last":
         out_ref = next(it)
     else:
@@ -204,11 +224,11 @@
         m = x_out * pitch
         for p in range(4):
             cols = slice(384 * p, 384 * p + 768)
-            t = jnp.dot(rows[0 : n - pitch, cols], w_ref[w, :, 0:256], preferred_element_type=F32)
-            o = t[0:m, 0:128] + t[pitch:, 128:256]
-            o = o + jnp.dot(
-                rows[2 * pitch : n, cols], w_ref[w, :, 256:384], preferred_element_type=F32
-            )
+            t = jnp.dot(rows[0 : n - pitch, cols], w_ref[w], preferred_element_type=F32)
+            if p % 2 == 0:
+                cols = slice(384 * p, 384 * p + 1152)
+                top = jnp.dot(rows[2 * pitch : n, cols], w2_ref[w], preferred_element_type=F32)
+            o = t[0:m, 0:128] + t[pitch:, 128:256] + top[:, p % 2 * 128 : p % 2 * 128 + 128]
             use(p, o.reshape(x_out, pitch, 128))
             if then is not None:
                 build(p, x_out, then)
@@ -314,9 +334,12 @@
         near = lax.all_to_all(
             jnp.broadcast_to(far, (members, *far.shape)), ("gs", "gy"), 0, 0, tiled=True
         )
-        (weights,) = kernel_call(
+        weights = kernel_call(
             functools.partial(weights_body, (gs, gy)),
-            [jax.ShapeDtypeStruct((4, 12 * chans, 6 * chans), BF16)],
+            [
+                jax.ShapeDtypeStruct((4, 12 * chans, 4 * chans), BF16),
+                jax.ShapeDtypeStruct((4, 18 * chans, 4 * chans), BF16),
+            ],
             (near,),
             [VMEM((2, 27 * chans, chans), F32)],
         )
@@ -326,8 +349,13 @@
             functools.partial(spread_body, place),
             [jax.ShapeDtypeStruct((members, 4 + steps, 2, ZB, 128), BF16)],
             (position, momentum, noise),
+            [
+                VMEM((members, 4 + steps, 2, ZB, 128), BF16),
+                pltpu.SemaphoreType.DMA((4 + steps,)),
+            ],
             hbm_in=True,
             hbm_out=True,
+            out_space=pl.ANY,
         )
         held = lax.all_to_all(spread, ("gs", "gy"), 0, 0, tiled=True)
 
@@ -352,7 +380,7 @@
             res = kernel_call(
                 functools.partial(gradient_body, kind, wide, coef),
                 outs,
-                (held, *state, *edges, weights, bias_row),
+                (held, *state, *edges, *weights, bias_row),
                 (
                     VMEM((XB + 8, gy, pitch + 16, 128), F32),
                     VMEM(((XB + 8) * pitch, 15 * 128), BF16),

time: 187 us -> 186 us (level)
  no operation moved by 1% of the time
where the time goes in v5:
time: 186 us; the launch traced here: 185 us
  starting transfers between devices  96.1 us (52%)
  waiting for transfers between devices  56 us (30%)
  Pallas kernels  17 us (9%)
  blocking collectives  11.3 us (6%)
  local copies, waits for them, and re-layouts  3.25 us (2%)
    all_to_all x1, starting transfers between devices, body(): lax.all_to_all(jnp.broadcast_to(own, (gX, *own.shape)), 'gX', 0, 0, tiled...  44.6 us
    ppermute x4, starting transfers between devices, along_x(): xh = lax.ppermute(block, 'gX', x_shift(-1))  22.1 us
    all_to_all x1, waiting for transfers between devices, body(): lax.all_to_all(jnp.broadcast_to(own, (gX, *own.shape)), 'gX', 0, 0, tiled...  21.2 us
    pallas_call x8, Pallas kernels, kernel_call(): pl.pallas_call(body, out_shape=outs if hbm_out else [VMEM(o.shape, o.dtyp...  17 us
    ppermute x4, waiting for transfers between devices, along_x(): xl = lax.ppermute(block, 'gX', x_shift(1))  11.7 us
    all_to_all x1, blocking collectives, body(): lax.all_to_all(res[0].reshape(members, 2, 2, ZB, 128), ('gs', 'gy'), 0, 0...  11.3 us
    ppermute x4, starting transfers between devices, along_x(): xl = lax.ppermute(block, 'gX', x_shift(1))  9.68 us
    ppermute x4, waiting for transfers between devices, along_x(): xh = lax.ppermute(block, 'gX', x_shift(-1))  8.39 us
  transfers between devices with their start and end apart: 15, of which 13 were waited for; matrix products, arithmetic and copies ran while one was open for 0% of the time, Pallas kernels for 2%

profile of v5, /device:TPU:40, one launch (start us, length us, event | category | flops | bytes accessed | tf_op | source)
XLA Modules:
  0.0 184.7 jit_solution(9552387284831969528)
XLA Ops:
  0.6 0.7 copy.13
  1.3 0.1 reshape.23
  1.4 0.7 copy.12
  2.2 0.1 reshape.25
  2.2 0.1 fusion.2
  2.3 0.7 broadcast_in_dim.9
  3.0 44.6 %all-to-all-start.1 = ((bf16[16,2,896]{2,1,0:T(2,128)(2,1)}), bf16[16,2,896]{2,1,0:T(2,128)(2,1)S(1)}, u32[]{:S(2)}, u32[]{:S(2)}) async-start(bf16[16,2,896]{2,1,0:T(2,128)(2,1)} %broadcast_in_dim.9), calls=%async_computation.1 | async-start | bytes 114688 | tf_op jit(solution)/shard_map/all_to_all | solution.py:330
  47.6 0.0 copy-start
  47.6 2.4 %shard_map.77 = bf16[8,7,2,16,128]{4,3,2,1,0:T(8,128)(2,1)} custom-call(f32[64,2,2,128]{3,2,1,0:T(2,128)} %q_ref.1, f32[64,2,2,128]{3,2,1,0:T(2,128)} %p_ref.1, bf16[3,64,2,2,128]{4,3,2,1,0:T(2,128)(2,1)} %n_ref.1), custom_call_target="tpu_custom_call" | custom-call | tf_op jit(solution)/shard_map/pallas_call | solution.py:32
  50.0 21.2 %all-to-all-done.1 = bf16[16,2,896]{2,1,0:T(2,128)(2,1)S(1)} async-done(((bf16[16,2,896]{2,1,0:T(2,128)(2,1)}), bf16[16,2,896]{2,1,0:T(2,128)(2,1)S(1)}, u32[]{:S(2)}, u32[]{:S(2)}) %all-to-all-start.1) | async-done | bytes 57376 | tf_op jit(solution)/shard_map/all_to_all | solution.py:330
  71.2 4.6 %all-to-all-start = ((bf16[8,7,2,16,128]{4,3,2,1,0:T(8,128)(2,1)}), bf16[8,7,2,16,128]{4,3,2,1,0:T(8,128)(2,1)S(1)}, u32[]{:S(2)}, u32[]{:S(2)}) async-start(bf16[8,7,2,16,128]{4,3,2,1,0:T(8,128)(2,1)} %shard_map.77), calls=%async_computation | async-start | bytes 917504 | tf_op jit(solution)/shard_map/all_to_all | solution.py:360
  75.8 8.0 %all-to-all-done.r_ref.refs_0_ = bf16[8,7,2,16,128]{4,3,2,1,0:T(8,128)(2,1)S(1)} async-done(((bf16[8,7,2,16,128]{4,3,2,1,0:T(8,128)(2,1)}), bf16[8,7,2,16,128]{4,3,2,1,0:T(8,128)(2,1)S(1)}, u32[]{:S(2)}, u32[]{:S(2)}) %all-to-all-start) | async-done | bytes 458784 | tf_op jit(solution)/shard_map/all_to_all | solution.py:360
  83.8 0.8 broadcast_in_dim.10
  84.6 3.7 %all-to-all-start.2 = ((bf16[8,32,896]{2,1,0:T(8,128)(2,1)}), bf16[8,32,896]{2,1,0:T(8,128)(2,1)S(1)}, u32[]{:S(2)}, u32[]{:S(2)}) async-start(bf16[8,32,896]{2,1,0:T(8,128)(2,1)} %broadcast_in_dim.10), calls=%async_computation.2 | async-start | bytes 917504 | tf_op jit(solution)/shard_map/all_to_all | solution.py:334
  88.3 0.1 shard_map.78
  88.4 3.8 %collective-permute-start = (bf16[4,4,16,128]{3,2,1,0:T(8,128)(2,1)S(1)}, bf16[4,4,16,128]{3,2,1,0:T(8,128)(2,1)S(1)}, u32[]{:S(2)}, u32[]{:S(2)}) collective-permute-start(bf16[4,4,16,128]{3,2,1,0:T(8,128)(2,1)S(1)} %get-tuple-element.18), channel_id=1, source_target_pairs={{0,16},{16,32},{32,48},{48,64},{64,80},{80,96},{96,112},{112,128},... | collective-permute-start | bytes 196616 | tf_op jit(solution)/shard_map/ppermute | solution.py:309
  92.2 4.2 %collective-permute-start.1 = (bf16[4,4,16,128]{3,2,1,0:T(8,128)(2,1)S(1)}, bf16[4,4,16,128]{3,2,1,0:T(8,128)(2,1)S(1)}, u32[]{:S(2)}, u32[]{:S(2)}) collective-permute-start(bf16[4,4,16,128]{3,2,1,0:T(8,128)(2,1)S(1)} %get-tuple-element.18), channel_id=1, source_target_pairs={{0,240},{16,0},{32,16},{48,32},{64,48},{80,64},{96,80},{112,96},{1... | collective-permute-start | bytes 196616 | tf_op jit(solution)/shard_map/ppermute | solution.py:310
  96.4 0.3 collective-permute-done.refs_1_
  96.8 2.6 %collective-permute-done.1.refs_2_ = bf16[4,4,16,128]{3,2,1,0:T(8,128)(2,1)S(1)} collective-permute-done((bf16[4,4,16,128]{3,2,1,0:T(8,128)(2,1)S(1)}, bf16[4,4,16,128]{3,2,1,0:T(8,128)(2,1)S(1)}, u32[]{:S(2)}, u32[]{:S(2)}) %collective-permute-start.1) | collective-permute-done | bytes 65568 | tf_op jit(solution)/shard_map/ppermute | solution.py:310
  99.4 3.7 %collective-permute-start.2 = (bf16[16,4,8,128]{3,2,1,0:T(8,128)(2,1)S(1)}, bf16[16,4,8,128]{3,2,1,0:T(8,128)(2,1)S(1)}, u32[]{:S(2)}, u32[]{:S(2)}) collective-permute-start(bf16[16,4,8,128]{3,2,1,0:T(8,128)(2,1)S(1)} %pad_maximum_fusion), channel_id=1, source_target_pairs={{0,2},{2,4},{4,6},{6,14},{14,12},{12,10},{10,8},{8,1},{1,3},{3,5},... | collective-permute-start | bytes 393224 | tf_op jit(solution)/shard_map/ppermute | solution.py:318
  103.1 2.0 %collective-permute-start.3 = (bf16[16,4,8,128]{3,2,1,0:T(8,128)(2,1)S(1)}, bf16[16,4,8,128]{3,2,1,0:T(8,128)(2,1)S(1)}, u32[]{:S(2)}, u32[]{:S(2)}) collective-permute-start(bf16[16,4,8,128]{3,2,1,0:T(8,128)(2,1)S(1)} %pad_maximum_fusion.1), channel_id=1, source_target_pairs={{0,9},{2,0},{4,2},{6,4},{14,6},{12,14},{10,12},{8,10},{1,8},{3,1},... | collective-permute-start | bytes 393224 | tf_op jit(solution)/shard_map/ppermute | solution.py:319
  105.1 0.1 maximum_bitcast_fusion.refs_7_.refs_8_.refs_9_
  105.2 0.0 all-to-all-done.2.m_ref
  105.2 1.7 shard_map.79
  106.9 0.0 collective-permute-done.2.refs_3_
  106.9 3.1 %collective-permute-done.3.refs_4_ = bf16[16,4,8,128]{3,2,1,0:T(8,128)(2,1)S(1)} collective-permute-done((bf16[16,4,8,128]{3,2,1,0:T(8,128)(2,1)S(1)}, bf16[16,4,8,128]{3,2,1,0:T(8,128)(2,1)S(1)}, u32[]{:S(2)}, u32[]{:S(2)}) %collective-permute-start.3) | collective-permute-done | bytes 131104 | tf_op jit(solution)/shard_map/ppermute | solution.py:319
  110.0 3.3 %shard_map.80 = (f32[4,4,16,128]{3,2,1,0:T(8,128)S(1)}, f32[4,4,16,128]{3,2,1,0:T(8,128)S(1)}, bf16[4,4,24,128]{3,2,1,0:T(8,128)(2,1)S(1)}) custom-call(bf16[8,7,2,16,128]{4,3,2,1,0:T(8,128)(2,1)S(1)} %all-to-all-done.r_ref.refs_0_, bf16[4,4,16,128]{3,2,1,0:T(8,128)(2,1)S(1)} %collective-permute-done.refs_1_, ...), custom_call_target="tpu_custom_call" | custom-call | tf_op jit(solution)/shard_map/pallas_call | solution.py:32
  113.3 5.4 %collective-permute-start.5 = (bf16[4,4,24,128]{3,2,1,0:T(8,128)(2,1)S(1)}, bf16[4,4,24,128]{3,2,1,0:T(8,128)(2,1)S(1)}, u32[]{:S(2)}, u32[]{:S(2)}) collective-permute-start(bf16[4,4,24,128]{3,2,1,0:T(8,128)(2,1)S(1)} %get-tuple-element.25.refs_5_), channel_id=1, source_target_pairs={{0,240},{16,0},{32,16},{48,32},{64,48},{80,64},{96,80},{112,96},{1... | collective-permute-start | bytes 294920 | tf_op jit(solution)/shard_map/ppermute | solution.py:310
  118.7 2.0 %collective-permute-start.4 = (bf16[4,4,24,128]{3,2,1,0:T(8,128)(2,1)S(1)}, bf16[4,4,24,128]{3,2,1,0:T(8,128)(2,1)S(1)}, u32[]{:S(2)}, u32[]{:S(2)}) collective-permute-start(bf16[4,4,24,128]{3,2,1,0:T(8,128)(2,1)S(1)} %get-tuple-element.25.refs_5_), channel_id=1, source_target_pairs={{0,16},{16,32},{32,48},{48,64},{64,80},{80,96},{96,112},{112,128},... | collective-permute-start | bytes 294920 | tf_op jit(solution)/shard_map/ppermute | solution.py:309
  120.7 2.2 %collective-permute-done.5.refs_4_ = bf16[4,4,24,128]{3,2,1,0:T(8,128)(2,1)S(1)} collective-permute-done((bf16[4,4,24,128]{3,2,1,0:T(8,128)(2,1)S(1)}, bf16[4,4,24,128]{3,2,1,0:T(8,128)(2,1)S(1)}, u32[]{:S(2)}, u32[]{:S(2)}) %collective-permute-start.5) | collective-permute-done | bytes 98336 | tf_op jit(solution)/shard_map/ppermute | solution.py:310
  122.9 5.0 %collective-permute-done.4.refs_3_ = bf16[4,4,24,128]{3,2,1,0:T(8,128)(2,1)S(1)} collective-permute-done((bf16[4,4,24,128]{3,2,1,0:T(8,128)(2,1)S(1)}, bf16[4,4,24,128]{3,2,1,0:T(8,128)(2,1)S(1)}, u32[]{:S(2)}, u32[]{:S(2)}) %collective-permute-start.4) | collective-permute-done | bytes 98336 | tf_op jit(solution)/shard_map/ppermute | solution.py:309
  127.9 2.6 %shard_map.81 = (f32[4,4,16,128]{3,2,1,0:T(8,128)S(1)}, f32[4,4,16,128]{3,2,1,0:T(8,128)S(1)}, bf16[4,4,16,128]{3,2,1,0:T(8,128)(2,1)S(1)}, bf16[4,4,8,128]{3,2,1,0:T(8,128)(2,1)S(1)}, bf16[4,4,8,128]{3,2,1,0:T(8,128)(2,1)S(1)}) custom-call(bf16[8,7,2,16,128]{4,3,2,1,0:T(8,128)(2,1)S(1)} %all-to-all-done.r_ref.refs_0_, ...), custom_call_target="tpu_custom_call" | custom-call | tf_op jit(solution)/shard_map/pallas_call | solution.py:32
  130.5 2.0 %collective-permute-start.6 = (bf16[4,4,16,128]{3,2,1,0:T(8,128)(2,1)S(1)}, bf16[4,4,16,128]{3,2,1,0:T(8,128)(2,1)S(1)}, u32[]{:S(2)}, u32[]{:S(2)}) collective-permute-start(bf16[4,4,16,128]{3,2,1,0:T(8,128)(2,1)S(1)} %get-tuple-element.28), channel_id=1, source_target_pairs={{0,16},{16,32},{32,48},{48,64},{64,80},{80,96},{96,112},{112,128},... | collective-permute-start | bytes 196616 | tf_op jit(solution)/shard_map/ppermute | solution.py:309
  132.5 6.1 %collective-permute-start.7 = (bf16[4,4,16,128]{3,2,1,0:T(8,128)(2,1)S(1)}, bf16[4,4,16,128]{3,2,1,0:T(8,128)(2,1)S(1)}, u32[]{:S(2)}, u32[]{:S(2)}) collective-permute-start(bf16[4,4,16,128]{3,2,1,0:T(8,128)(2,1)S(1)} %get-tuple-element.28), channel_id=1, source_target_pairs={{0,240},{16,0},{32,16},{48,32},{64,48},{80,64},{96,80},{112,96},{1... | collective-permute-start | bytes 196616 | tf_op jit(solution)/shard_map/ppermute | solution.py:310
  138.5 0.6 collective-permute-done.6.refs_3_
  139.1 1.8 collective-permute-done.7.refs_4_
  141.0 2.5 %collective-permute-start.8 = (bf16[16,4,8,128]{3,2,1,0:T(8,128)(2,1)S(1)}, bf16[16,4,8,128]{3,2,1,0:T(8,128)(2,1)S(1)}, u32[]{:S(2)}, u32[]{:S(2)}) collective-permute-start(bf16[16,4,8,128]{3,2,1,0:T(8,128)(2,1)S(1)} %pad_maximum_fusion.2), channel_id=1, source_target_pairs={{0,2},{2,4},{4,6},{6,14},{14,12},{12,10},{10,8},{8,1},{1,3},{3,5},... | collective-permute-start | bytes 393224 | tf_op jit(solution)/shard_map/ppermute | solution.py:318
  143.6 3.3 %collective-permute-start.9 = (bf16[16,4,8,128]{3,2,1,0:T(8,128)(2,1)S(1)}, bf16[16,4,8,128]{3,2,1,0:T(8,128)(2,1)S(1)}, u32[]{:S(2)}, u32[]{:S(2)}) collective-permute-start(bf16[16,4,8,128]{3,2,1,0:T(8,128)(2,1)S(1)} %pad_maximum_fusion.3), channel_id=1, source_target_pairs={{0,9},{2,0},{4,2},{6,4},{14,6},{12,14},{10,12},{8,10},{1,8},{3,1},... | collective-permute-start | bytes 393224 | tf_op jit(solution)/shard_map/ppermute | solution.py:319
  146.9 0.5 collective-permute-done.8.refs_5_
  147.3 3.2 %collective-permute-done.9.refs_6_ = bf16[16,4,8,128]{3,2,1,0:T(8,128)(2,1)S(1)} collective-permute-done((bf16[16,4,8,128]{3,2,1,0:T(8,128)(2,1)S(1)}, bf16[16,4,8,128]{3,2,1,0:T(8,128)(2,1)S(1)}, u32[]{:S(2)}, u32[]{:S(2)}) %collective-permute-start.9) | collective-permute-done | bytes 131104 | tf_op jit(solution)/shard_map/ppermute | solution.py:319
  150.5 3.3 %shard_map.82 = (f32[4,4,16,128]{3,2,1,0:T(8,128)S(1)}, f32[4,4,16,128]{3,2,1,0:T(8,128)S(1)}, bf16[4,4,24,128]{3,2,1,0:T(8,128)(2,1)S(1)}) custom-call(bf16[8,7,2,16,128]{4,3,2,1,0:T(8,128)(2,1)S(1)} %all-to-all-done.r_ref.refs_0_, f32[4,4,16,128]{3,2,1,0:T(8,128)S(1)} %get-tuple-element.26.refs_1_, f32[4,4,16,128]{3,2,1,0:T(8,128)S(1)} %get-tuple-element.27.refs_2_, ...), custom_call_target="tpu_custom_call" | custom-call | tf_op jit(solution)/shard_map/pallas_call | solution.py:32
  153.9 6.5 %collective-permute-start.11 = (bf16[4,4,24,128]{3,2,1,0:T(8,128)(2,1)S(1)}, bf16[4,4,24,128]{3,2,1,0:T(8,128)(2,1)S(1)}, u32[]{:S(2)}, u32[]{:S(2)}) collective-permute-start(bf16[4,4,24,128]{3,2,1,0:T(8,128)(2,1)S(1)} %get-tuple-element.33.refs_5_), channel_id=1, source_target_pairs={{0,240},{16,0},{32,16},{48,32},{64,48},{80,64},{96,80},{112,96},{1... | collective-permute-start | bytes 294920 | tf_op jit(solution)/shard_map/ppermute | solution.py:310
  160.4 2.0 %collective-permute-start.10 = (bf16[4,4,24,128]{3,2,1,0:T(8,128)(2,1)S(1)}, bf16[4,4,24,128]{3,2,1,0:T(8,128)(2,1)S(1)}, u32[]{:S(2)}, u32[]{:S(2)}) collective-permute-start(bf16[4,4,24,128]{3,2,1,0:T(8,128)(2,1)S(1)} %get-tuple-element.33.refs_5_), channel_id=1, source_target_pairs={{0,16},{16,32},{32,48},{48,64},{64,80},{80,96},{96,112},{112,128},... | collective-permute-start | bytes 294920 | tf_op jit(solution)/shard_map/ppermute | solution.py:309
  162.3 1.8 collective-permute-done.11.refs_4_
  164.1 5.8 %collective-permute-done.10.refs_3_ = bf16[4,4,24,128]{3,2,1,0:T(8,128)(2,1)S(1)} collective-permute-done((bf16[4,4,24,128]{3,2,1,0:T(8,128)(2,1)S(1)}, bf16[4,4,24,128]{3,2,1,0:T(8,128)(2,1)S(1)}, u32[]{:S(2)}, u32[]{:S(2)}) %collective-permute-start.10) | collective-permute-done | bytes 98336 | tf_op jit(solution)/shard_map/ppermute | solution.py:309
  169.9 2.6 %shard_map.83 = f32[2,4,2,2,16,128]{5,4,3,2,1,0:T(8,128)S(1)} custom-call(bf16[8,7,2,16,128]{4,3,2,1,0:T(8,128)(2,1)S(1)} %all-to-all-done.r_ref.refs_0_, f32[4,4,16,128]{3,2,1,0:T(8,128)S(1)} %get-tuple-element.31.refs_1_, f32[4,4,16,128]{3,2,1,0:T(8,128)S(1)} %get-tuple-element.32.refs_2_, bf16[4,4,24,128]{3,2,1,0:T(8,128)(2,1)S(1)} %collective-permute-done.10.refs_3_, ...), custom_call_target="tpu_custom_call" | custom-call | tf_op jit(solution)/shard_map/pallas_call | solution.py:32
  172.6 11.3 %all_to_all.20.in_ref = f32[8,2,2,16,128]{4,3,2,1,0:T(8,128)S(1)} all-to-all(f32[8,2,2,16,128]{4,3,2,1,0:T(8,128)S(1)} %bitcast.11), channel_id=1, replica_groups=mesh['grp'=2,'gX'=16,'gs'=2,'gy'=4,'gz'=2] {'gs','gy'}, dimensions={0} | all-to-all | bytes 524288 | tf_op jit(solution)/shard_map/all_to_all | solution.py:393
  183.9 0.9 shard_map.84
  (14 shorter events, 0.2 us)
Async XLA Ops:
  3.0 68.2 %all-to-all-start.1 = ((bf16[16,2,896]{2,1,0:T(2,128)(2,1)}), bf16[16,2,896]{2,1,0:T(2,128)(2,1)S(1)}, u32[]{:S(2)}, u32[]{:S(2)}) async-start(bf16[16,2,896]{2,1,0:T(2,128)(2,1)} %broadcast_in_dim.9), calls=%async_computation.1 | async-start | bytes 114688 | tf_op jit(solution)/shard_map/all_to_all | solution.py:330
  47.6 57.5 %copy-start = (f32[64]{0:T(128)S(1)}, f32[64]{0:T(128)}, u32[]{:S(2)}) copy-start(f32[64]{0:T(128)} %param.11) | copy-start | bytes 772
  71.2 12.6 %all-to-all-start = ((bf16[8,7,2,16,128]{4,3,2,1,0:T(8,128)(2,1)}), bf16[8,7,2,16,128]{4,3,2,1,0:T(8,128)(2,1)S(1)}, u32[]{:S(2)}, u32[]{:S(2)}) async-start(bf16[8,7,2,16,128]{4,3,2,1,0:T(8,128)(2,1)} %shard_map.77), calls=%async_computation | async-start | bytes 917504 | tf_op jit(solution)/shard_map/all_to_all | solution.py:360
  84.6 20.5 %all-to-all-start.2 = ((bf16[8,32,896]{2,1,0:T(8,128)(2,1)}), bf16[8,32,896]{2,1,0:T(8,128)(2,1)S(1)}, u32[]{:S(2)}, u32[]{:S(2)}) async-start(bf16[8,32,896]{2,1,0:T(8,128)(2,1)} %broadcast_in_dim.10), calls=%async_computation.2 | async-start | bytes 917504 | tf_op jit(solution)/shard_map/all_to_all | solution.py:334
  88.4 8.3 %collective-permute-start = (bf16[4,4,16,128]{3,2,1,0:T(8,128)(2,1)S(1)}, bf16[4,4,16,128]{3,2,1,0:T(8,128)(2,1)S(1)}, u32[]{:S(2)}, u32[]{:S(2)}) collective-permute-start(bf16[4,4,16,128]{3,2,1,0:T(8,128)(2,1)S(1)} %get-tuple-element.18), channel_id=1, source_target_pairs={{0,16},{16,32},{32,48},{48,64},{64,80},{80,96},{96,112},{112,128},... | collective-permute-start | bytes 196616 | tf_op jit(solution)/shard_map/ppermute | solution.py:309
  92.2 7.1 %collective-permute-start.1 = (bf16[4,4,16,128]{3,2,1,0:T(8,128)(2,1)S(1)}, bf16[4,4,16,128]{3,2,1,0:T(8,128)(2,1)S(1)}, u32[]{:S(2)}, u32[]{:S(2)}) collective-permute-start(bf16[4,4,16,128]{3,2,1,0:T(8,128)(2,1)S(1)} %get-tuple-element.18), channel_id=1, source_target_pairs={{0,240},{16,0},{32,16},{48,32},{64,48},{80,64},{96,80},{112,96},{1... | collective-permute-start | bytes 196616 | tf_op jit(solution)/shard_map/ppermute | solution.py:310
  99.4 7.5 %collective-permute-start.2 = (bf16[16,4,8,128]{3,2,1,0:T(8,128)(2,1)S(1)}, bf16[16,4,8,128]{3,2,1,0:T(8,128)(2,1)S(1)}, u32[]{:S(2)}, u32[]{:S(2)}) collective-permute-start(bf16[16,4,8,128]{3,2,1,0:T(8,128)(2,1)S(1)} %pad_maximum_fusion), channel_id=1, source_target_pairs={{0,2},{2,4},{4,6},{6,14},{14,12},{12,10},{10,8},{8,1},{1,3},{3,5},... | collective-permute-start | bytes 393224 | tf_op jit(solution)/shard_map/ppermute | solution.py:318
  103.1 6.9 %collective-permute-start.3 = (bf16[16,4,8,128]{3,2,1,0:T(8,128)(2,1)S(1)}, bf16[16,4,8,128]{3,2,1,0:T(8,128)(2,1)S(1)}, u32[]{:S(2)}, u32[]{:S(2)}) collective-permute-start(bf16[16,4,8,128]{3,2,1,0:T(8,128)(2,1)S(1)} %pad_maximum_fusion.1), channel_id=1, source_target_pairs={{0,9},{2,0},{4,2},{6,4},{14,6},{12,14},{10,12},{8,10},{1,8},{3,1},... | collective-permute-start | bytes 393224 | tf_op jit(solution)/shard_map/ppermute | solution.py:319
  113.3 9.6 %collective-permute-start.5 = (bf16[4,4,24,128]{3,2,1,0:T(8,128)(2,1)S(1)}, bf16[4,4,24,128]{3,2,1,0:T(8,128)(2,1)S(1)}, u32[]{:S(2)}, u32[]{:S(2)}) collective-permute-start(bf16[4,4,24,128]{3,2,1,0:T(8,128)(2,1)S(1)} %get-tuple-element.25.refs_5_), channel_id=1, source_target_pairs={{0,240},{16,0},{32,16},{48,32},{64,48},{80,64},{96,80},{112,96},{1... | collective-permute-start | bytes 294920 | tf_op jit(solution)/shard_map/ppermute | solution.py:310
  118.7 9.2 %collective-permute-start.4 = (bf16[4,4,24,128]{3,2,1,0:T(8,128)(2,1)S(1)}, bf16[4,4,24,128]{3,2,1,0:T(8,128)(2,1)S(1)}, u32[]{:S(2)}, u32[]{:S(2)}) collective-permute-start(bf16[4,4,24,128]{3,2,1,0:T(8,128)(2,1)S(1)} %get-tuple-element.25.refs_5_), channel_id=1, source_target_pairs={{0,16},{16,32},{32,48},{48,64},{64,80},{80,96},{96,112},{112,128},... | collective-permute-start | bytes 294920 | tf_op jit(solution)/shard_map/ppermute | solution.py:309
  130.5 8.6 %collective-permute-start.6 = (bf16[4,4,16,128]{3,2,1,0:T(8,128)(2,1)S(1)}, bf16[4,4,16,128]{3,2,1,0:T(8,128)(2,1)S(1)}, u32[]{:S(2)}, u32[]{:S(2)}) collective-permute-start(bf16[4,4,16,128]{3,2,1,0:T(8,128)(2,1)S(1)} %get-tuple-element.28), channel_id=1, source_target_pairs={{0,16},{16,32},{32,48},{48,64},{64,80},{80,96},{96,112},{112,128},... | collective-permute-start | bytes 196616 | tf_op jit(solution)/shard_map/ppermute | solution.py:309
  132.5 8.5 %collective-permute-start.7 = (bf16[4,4,16,128]{3,2,1,0:T(8,128)(2,1)S(1)}, bf16[4,4,16,128]{3,2,1,0:T(8,128)(2,1)S(1)}, u32[]{:S(2)}, u32[]{:S(2)}) collective-permute-start(bf16[4,4,16,128]{3,2,1,0:T(8,128)(2,1)S(1)} %get-tuple-element.28), channel_id=1, source_target_pairs={{0,240},{16,0},{32,16},{48,32},{64,48},{80,64},{96,80},{112,96},{1... | collective-permute-start | bytes 196616 | tf_op jit(solution)/shard_map/ppermute | solution.py:310
  141.0 6.3 %collective-permute-start.8 = (bf16[16,4,8,128]{3,2,1,0:T(8,128)(2,1)S(1)}, bf16[16,4,8,128]{3,2,1,0:T(8,128)(2,1)S(1)}, u32[]{:S(2)}, u32[]{:S(2)}) collective-permute-start(bf16[16,4,8,128]{3,2,1,0:T(8,128)(2,1)S(1)} %pad_maximum_fusion.2), channel_id=1, source_target_pairs={{0,2},{2,4},{4,6},{6,14},{14,12},{12,10},{10,8},{8,1},{1,3},{3,5},... | collective-permute-start | bytes 393224 | tf_op jit(solution)/shard_map/ppermute | solution.py:318
  143.6 7.0 %collective-permute-start.9 = (bf16[16,4,8,128]{3,2,1,0:T(8,128)(2,1)S(1)}, bf16[16,4,8,128]{3,2,1,0:T(8,128)(2,1)S(1)}, u32[]{:S(2)}, u32[]{:S(2)}) collective-permute-start(bf16[16,4,8,128]{3,2,1,0:T(8,128)(2,1)S(1)} %pad_maximum_fusion.3), channel_id=1, source_target_pairs={{0,9},{2,0},{4,2},{6,4},{14,6},{12,14},{10,12},{8,10},{1,8},{3,1},... | collective-permute-start | bytes 393224 | tf_op jit(solution)/shard_map/ppermute | solution.py:319
  153.9 10.2 %collective-permute-start.11 = (bf16[4,4,24,128]{3,2,1,0:T(8,128)(2,1)S(1)}, bf16[4,4,24,128]{3,2,1,0:T(8,128)(2,1)S(1)}, u32[]{:S(2)}, u32[]{:S(2)}) collective-permute-start(bf16[4,4,24,128]{3,2,1,0:T(8,128)(2,1)S(1)} %get-tuple-element.33.refs_5_), channel_id=1, source_target_pairs={{0,240},{16,0},{32,16},{48,32},{64,48},{80,64},{96,80},{112,96},{1... | collective-permute-start | bytes 294920 | tf_op jit(solution)/shard_map/ppermute | solution.py:310
  160.4 9.6 %collective-permute-start.10 = (bf16[4,4,24,128]{3,2,1,0:T(8,128)(2,1)S(1)}, bf16[4,4,24,128]{3,2,1,0:T(8,128)(2,1)S(1)}, u32[]{:S(2)}, u32[]{:S(2)}) collective-permute-start(bf16[4,4,24,128]{3,2,1,0:T(8,128)(2,1)S(1)} %get-tuple-element.33.refs_5_), channel_id=1, source_target_pairs={{0,16},{16,32},{32,48},{48,64},{64,80},{80,96},{96,112},{112,128},... | collective-permute-start | bytes 294920 | tf_op jit(solution)/shard_map/ppermute | solution.py:309

commit v6 on v5

--- a/solution.py
+++ b/solution.py
@@ -295,28 +295,32 @@
     place = [walk.index((a, b)) for a in range(gs) for b in range(gy)]
     ring = [(a * gy + b) * gz + c for c in range(gz) for a, b in walk]
 
-    def x_shift(d):
-        return [(i, (i + d) % gX) for i in range(gX)]
-
-    def z_shift(d):
+    def swaps(ring, first):
         n = len(ring)
-        return [(ring[i], ring[(i + d) % n]) for i in range(n)]
+        pairs = [(ring[i], ring[(i + 1) % n]) for i in range(0 if first else 1, n, 2)]
+        return [pair for i, j in pairs for pair in ((i, j), (j, i))]
+
+    def exchange(up, down, axes, ring, even):
+        one = up if up is down else jnp.where(even, up, down)
+        two = up if up is down else jnp.where(even, down, up)
+        one = lax.ppermute(one, axes, swaps(ring, True))
+        two = lax.ppermute(two, axes, swaps(ring, False))
+        return jnp.where(even, two, one), jnp.where(even, one, two)
 
     decay = math.exp(-0.25)
     kick = math.sqrt(1.0 - decay * decay)
 
     def along_x(block):
-        xl = lax.ppermute(block, "gX", x_shift(1))
-        xh = lax.ppermute(block, "gX", x_shift(-1))
-        return xl, xh
+        even = lax.axis_index("gX") % 2 == 0
+        return exchange(block, block, "gX", list(range(gX)), even)
 
     def along_both(block, rl, rh):
         xl, xh = along_x(block)
         whole = jnp.concatenate([xl, block, xh], axis=0)
         up = jnp.concatenate([whole[:, :, ZB - 2 * HALO :], rh], axis=0)
         down = jnp.concatenate([whole[:, :, : 2 * HALO], rl], axis=0)
-        zl = lax.ppermute(up, ("gs", "gy", "gz"), z_shift(1))
-        zh = lax.ppermute(down, ("gs", "gy", "gz"), z_shift(-1))
+        even = (lax.axis_index("gs") + lax.axis_index("gy")) % 2 == 0
+        zl, zh = exchange(up, down, ("gs", "gy", "gz"), ring, even)
         return xl, xh, zl, zh
 
     def body(position, momentum, noise, filter_in, filter_out, bias):

time: 186 us -> 186 us (level)
  starting transfers between devices: 96.1 us -> 92.8 us
  waiting for transfers between devices: 56 us -> 58.4 us
    ppermute x12, starting transfers between devices: 43.2 us -> 40 us  [the longest x6 20.4 us: exchange(): two = lax.ppermute(two, axes, swaps(ring, False))]
    ppermute x12, waiting for transfers between devices: 26.9 us -> 29.2 us  [the longest x6 22.1 us: exchange(): two = lax.ppermute(two, axes, swaps(ring, False))]
  transfers between devices with their start and end apart: 15 -> 15, of which waited for: 13 -> 13; matrix products, arithmetic and copies ran while one was open for 0% -> 0% of each run, Pallas kernels for 2% -> 1%
where the time goes in v6:
time: 186 us; the launch traced here: 185 us
  starting transfers between devices  92.8 us (50%)
  waiting for transfers between devices  58.4 us (31%)
  Pallas kernels  17 us (9%)
  blocking collectives  12.1 us (7%)
  local copies, waits for them, and re-layouts  3.19 us (2%)
    all_to_all x1, starting transfers between devices, body(): lax.all_to_all(jnp.broadcast_to(own, (gX, *own.shape)), 'gX', 0, 0, tiled...  44.6 us
    ppermute x6, waiting for transfers between devices, exchange(): two = lax.ppermute(two, axes, swaps(ring, False))  22.1 us
    all_to_all x1, waiting for transfers between devices, body(): lax.all_to_all(jnp.broadcast_to(own, (gX, *own.shape)), 'gX', 0, 0, tiled...  21.2 us
    ppermute x6, starting transfers between devices, exchange(): two = lax.ppermute(two, axes, swaps(ring, False))  20.4 us
    ppermute x6, starting transfers between devices, exchange(): one = lax.ppermute(one, axes, swaps(ring, True))  19.5 us
    pallas_call x8, Pallas kernels, kernel_call(): pl.pallas_call(body, out_shape=outs if hbm_out else [VMEM(o.shape, o.dtyp...  17 us
    all_to_all x1, blocking collectives, body(): lax.all_to_all(res[0].reshape(members, 2, 2, ZB, 128), ('gs', 'gy'), 0, 0...  12.1 us
    all_to_all x1, waiting for transfers between devices, body(): held = lax.all_to_all(spread, ('gs', 'gy'), 0, 0, tiled=True)  7.99 us
  transfers between devices with their start and end apart: 15, of which 13 were waited for; matrix products, arithmetic and copies ran while one was open for 0% of the time, Pallas kernels for 1%

profile of v6, /device:TPU:40, one launch (start us, length us, event | category | flops | bytes accessed | tf_op | source)
XLA Modules:
  0.0 184.7 jit_solution(13822946712968542020)
XLA Ops:
  0.6 0.7 copy.13
  1.3 0.1 reshape.23
  1.4 0.7 copy.12
  2.2 0.1 reshape.25
  2.2 0.1 fusion.2
  2.3 0.7 broadcast_in_dim.9
  3.0 44.6 %all-to-all-start.1 = ((bf16[16,2,896]{2,1,0:T(2,128)(2,1)}), bf16[16,2,896]{2,1,0:T(2,128)(2,1)S(1)}, u32[]{:S(2)}, u32[]{:S(2)}) async-start(bf16[16,2,896]{2,1,0:T(2,128)(2,1)} %broadcast_in_dim.9), calls=%async_computation.1 | async-start | bytes 114688 | tf_op jit(solution)/shard_map/all_to_all | solution.py:334
  47.6 2.4 %shard_map.77 = bf16[8,7,2,16,128]{4,3,2,1,0:T(8,128)(2,1)} custom-call(f32[64,2,2,128]{3,2,1,0:T(2,128)} %q_ref.1, f32[64,2,2,128]{3,2,1,0:T(2,128)} %p_ref.1, bf16[3,64,2,2,128]{4,3,2,1,0:T(2,128)(2,1)} %n_ref.1), custom_call_target="tpu_custom_call" | custom-call | tf_op jit(solution)/shard_map/pallas_call | solution.py:32
  50.0 0.0 copy-start
  50.0 21.2 %all-to-all-done.1 = bf16[16,2,896]{2,1,0:T(2,128)(2,1)S(1)} async-done(((bf16[16,2,896]{2,1,0:T(2,128)(2,1)}), bf16[16,2,896]{2,1,0:T(2,128)(2,1)S(1)}, u32[]{:S(2)}, u32[]{:S(2)}) %all-to-all-start.1) | async-done | bytes 57376 | tf_op jit(solution)/shard_map/all_to_all | solution.py:334
  71.2 4.6 %all-to-all-start = ((bf16[8,7,2,16,128]{4,3,2,1,0:T(8,128)(2,1)}), bf16[8,7,2,16,128]{4,3,2,1,0:T(8,128)(2,1)S(1)}, u32[]{:S(2)}, u32[]{:S(2)}) async-start(bf16[8,7,2,16,128]{4,3,2,1,0:T(8,128)(2,1)} %shard_map.77), calls=%async_computation | async-start | bytes 917504 | tf_op jit(solution)/shard_map/all_to_all | solution.py:364
  75.8 8.0 %all-to-all-done.r_ref.refs_0_ = bf16[8,7,2,16,128]{4,3,2,1,0:T(8,128)(2,1)S(1)} async-done(((bf16[8,7,2,16,128]{4,3,2,1,0:T(8,128)(2,1)}), bf16[8,7,2,16,128]{4,3,2,1,0:T(8,128)(2,1)S(1)}, u32[]{:S(2)}, u32[]{:S(2)}) %all-to-all-start) | async-done | bytes 458784 | tf_op jit(solution)/shard_map/all_to_all | solution.py:364
  83.8 0.8 broadcast_in_dim.10
  84.6 3.7 %all-to-all-start.2 = ((bf16[8,32,896]{2,1,0:T(8,128)(2,1)}), bf16[8,32,896]{2,1,0:T(8,128)(2,1)S(1)}, u32[]{:S(2)}, u32[]{:S(2)}) async-start(bf16[8,32,896]{2,1,0:T(8,128)(2,1)} %broadcast_in_dim.10), calls=%async_computation.2 | async-start | bytes 917504 | tf_op jit(solution)/shard_map/all_to_all | solution.py:338
  88.3 0.1 shard_map.78
  88.4 3.8 %collective-permute-start.1 = (bf16[4,4,16,128]{3,2,1,0:T(8,128)(2,1)S(1)}, bf16[4,4,16,128]{3,2,1,0:T(8,128)(2,1)S(1)}, u32[]{:S(2)}, u32[]{:S(2)}) collective-permute-start(bf16[4,4,16,128]{3,2,1,0:T(8,128)(2,1)S(1)} %get-tuple-element.18), channel_id=1, source_target_pairs={{0,16},{16,0},{32,48},{48,32},{64,80},{80,64},{96,112},{112,96},{1... | collective-permute-start | bytes 196616 | tf_op jit(solution)/shard_map/ppermute | solution.py:306
  92.2 3.1 %collective-permute-start = (bf16[4,4,16,128]{3,2,1,0:T(8,128)(2,1)S(1)}, bf16[4,4,16,128]{3,2,1,0:T(8,128)(2,1)S(1)}, u32[]{:S(2)}, u32[]{:S(2)}) collective-permute-start(bf16[4,4,16,128]{3,2,1,0:T(8,128)(2,1)S(1)} %get-tuple-element.18), channel_id=1, source_target_pairs={{16,32},{32,16},{48,64},{64,48},{80,96},{96,80},{112,128},{128,112... | collective-permute-start | bytes 196616 | tf_op jit(solution)/shard_map/ppermute | solution.py:307
  95.3 0.2 collective-permute-done.1
  95.6 5.0 %collective-permute-done = bf16[4,4,16,128]{3,2,1,0:T(8,128)(2,1)S(1)} collective-permute-done((bf16[4,4,16,128]{3,2,1,0:T(8,128)(2,1)S(1)}, bf16[4,4,16,128]{3,2,1,0:T(8,128)(2,1)S(1)}, u32[]{:S(2)}, u32[]{:S(2)}) %collective-permute-start) | collective-permute-done | bytes 65568 | tf_op jit(solution)/shard_map/ppermute | solution.py:307
  100.7 3.7 %collective-permute-start.3 = (bf16[16,4,8,128]{3,2,1,0:T(8,128)(2,1)S(1)}, bf16[16,4,8,128]{3,2,1,0:T(8,128)(2,1)S(1)}, u32[]{:S(2)}, u32[]{:S(2)}) collective-permute-start(bf16[16,4,8,128]{3,2,1,0:T(8,128)(2,1)S(1)} %get-tuple-element.40), channel_id=1, source_target_pairs={{0,2},{2,0},{4,6},{6,4},{14,12},{12,14},{10,8},{8,10},{1,3},{3,1},... | collective-permute-start | bytes 393224 | tf_op jit(solution)/shard_map/ppermute | solution.py:306
  104.4 2.0 %collective-permute-start.2 = (bf16[16,4,8,128]{3,2,1,0:T(8,128)(2,1)S(1)}, bf16[16,4,8,128]{3,2,1,0:T(8,128)(2,1)S(1)}, u32[]{:S(2)}, u32[]{:S(2)}) collective-permute-start(bf16[16,4,8,128]{3,2,1,0:T(8,128)(2,1)S(1)} %get-tuple-element.41), channel_id=1, source_target_pairs={{2,4},{4,2},{6,14},{14,6},{12,10},{10,12},{8,1},{1,8},{3,5},{5,3},... | collective-permute-start | bytes 393224 | tf_op jit(solution)/shard_map/ppermute | solution.py:307
  106.4 0.1 maximum_bitcast_fusion.refs_7_.refs_8_.refs_9_
  106.4 1.2 collective-permute-done.3
  107.6 3.9 %collective-permute-done.2 = bf16[16,4,8,128]{3,2,1,0:T(8,128)(2,1)S(1)} collective-permute-done((bf16[16,4,8,128]{3,2,1,0:T(8,128)(2,1)S(1)}, bf16[16,4,8,128]{3,2,1,0:T(8,128)(2,1)S(1)}, u32[]{:S(2)}, u32[]{:S(2)}) %collective-permute-start.2) | collective-permute-done | bytes 131104 | tf_op jit(solution)/shard_map/ppermute | solution.py:307
  111.5 0.0 all-to-all-done.2.m_ref
  111.5 1.7 shard_map.79
  113.2 3.3 %shard_map.80 = (f32[4,4,16,128]{3,2,1,0:T(8,128)S(1)}, f32[4,4,16,128]{3,2,1,0:T(8,128)S(1)}, bf16[4,4,24,128]{3,2,1,0:T(8,128)(2,1)S(1)}) custom-call(bf16[8,7,2,16,128]{4,3,2,1,0:T(8,128)(2,1)S(1)} %all-to-all-done.r_ref.refs_0_, bf16[4,4,16,128]{3,2,1,0:T(8,128)(2,1)S(1)} %get-tuple-element.53.refs_1_, ...), custom_call_target="tpu_custom_call" | custom-call | tf_op jit(solution)/shard_map/pallas_call | solution.py:32
  116.5 3.5 %collective-permute-start.5 = (bf16[4,4,24,128]{3,2,1,0:T(8,128)(2,1)S(1)}, bf16[4,4,24,128]{3,2,1,0:T(8,128)(2,1)S(1)}, u32[]{:S(2)}, u32[]{:S(2)}) collective-permute-start(bf16[4,4,24,128]{3,2,1,0:T(8,128)(2,1)S(1)} %get-tuple-element.25.refs_5_), channel_id=1, source_target_pairs={{0,16},{16,0},{32,48},{48,32},{64,80},{80,64},{96,112},{112,96},{1... | collective-permute-start | bytes 294920 | tf_op jit(solution)/shard_map/ppermute | solution.py:306
  120.0 4.3 %collective-permute-start.4 = (bf16[4,4,24,128]{3,2,1,0:T(8,128)(2,1)S(1)}, bf16[4,4,24,128]{3,2,1,0:T(8,128)(2,1)S(1)}, u32[]{:S(2)}, u32[]{:S(2)}) collective-permute-start(bf16[4,4,24,128]{3,2,1,0:T(8,128)(2,1)S(1)} %get-tuple-element.25.refs_5_), channel_id=1, source_target_pairs={{16,32},{32,16},{48,64},{64,48},{80,96},{96,80},{112,128},{128,112... | collective-permute-start | bytes 294920 | tf_op jit(solution)/shard_map/ppermute | solution.py:307
  124.3 1.4 collective-permute-done.5
  125.7 3.0 %collective-permute-done.4 = bf16[4,4,24,128]{3,2,1,0:T(8,128)(2,1)S(1)} collective-permute-done((bf16[4,4,24,128]{3,2,1,0:T(8,128)(2,1)S(1)}, bf16[4,4,24,128]{3,2,1,0:T(8,128)(2,1)S(1)}, u32[]{:S(2)}, u32[]{:S(2)}) %collective-permute-start.4) | collective-permute-done | bytes 98336 | tf_op jit(solution)/shard_map/ppermute | solution.py:307
  128.7 2.6 %shard_map.81 = (f32[4,4,16,128]{3,2,1,0:T(8,128)S(1)}, f32[4,4,16,128]{3,2,1,0:T(8,128)S(1)}, bf16[4,4,16,128]{3,2,1,0:T(8,128)(2,1)S(1)}, bf16[4,4,8,128]{3,2,1,0:T(8,128)(2,1)S(1)}, bf16[4,4,8,128]{3,2,1,0:T(8,128)(2,1)S(1)}) custom-call(bf16[8,7,2,16,128]{4,3,2,1,0:T(8,128)(2,1)S(1)} %all-to-all-done.r_ref.refs_0_, ...), custom_call_target="tpu_custom_call" | custom-call | tf_op jit(solution)/shard_map/pallas_call | solution.py:32
  131.3 4.7 %collective-permute-start.7 = (bf16[4,4,16,128]{3,2,1,0:T(8,128)(2,1)S(1)}, bf16[4,4,16,128]{3,2,1,0:T(8,128)(2,1)S(1)}, u32[]{:S(2)}, u32[]{:S(2)}) collective-permute-start(bf16[4,4,16,128]{3,2,1,0:T(8,128)(2,1)S(1)} %get-tuple-element.28), channel_id=1, source_target_pairs={{0,16},{16,0},{32,48},{48,32},{64,80},{80,64},{96,112},{112,96},{1... | collective-permute-start | bytes 196616 | tf_op jit(solution)/shard_map/ppermute | solution.py:306
  136.0 3.2 %collective-permute-start.6 = (bf16[4,4,16,128]{3,2,1,0:T(8,128)(2,1)S(1)}, bf16[4,4,16,128]{3,2,1,0:T(8,128)(2,1)S(1)}, u32[]{:S(2)}, u32[]{:S(2)}) collective-permute-start(bf16[4,4,16,128]{3,2,1,0:T(8,128)(2,1)S(1)} %get-tuple-element.28), channel_id=1, source_target_pairs={{16,32},{32,16},{48,64},{64,48},{80,96},{96,80},{112,128},{128,112... | collective-permute-start | bytes 196616 | tf_op jit(solution)/shard_map/ppermute | solution.py:307
  139.2 0.0 collective-permute-done.7
  139.2 5.1 %collective-permute-done.6 = bf16[4,4,16,128]{3,2,1,0:T(8,128)(2,1)S(1)} collective-permute-done((bf16[4,4,16,128]{3,2,1,0:T(8,128)(2,1)S(1)}, bf16[4,4,16,128]{3,2,1,0:T(8,128)(2,1)S(1)}, u32[]{:S(2)}, u32[]{:S(2)}) %collective-permute-start.6) | collective-permute-done | bytes 65568 | tf_op jit(solution)/shard_map/ppermute | solution.py:307
  144.4 2.0 %collective-permute-start.9 = (bf16[16,4,8,128]{3,2,1,0:T(8,128)(2,1)S(1)}, bf16[16,4,8,128]{3,2,1,0:T(8,128)(2,1)S(1)}, u32[]{:S(2)}, u32[]{:S(2)}) collective-permute-start(bf16[16,4,8,128]{3,2,1,0:T(8,128)(2,1)S(1)} %get-tuple-element.36), channel_id=1, source_target_pairs={{0,2},{2,0},{4,6},{6,4},{14,12},{12,14},{10,8},{8,10},{1,3},{3,1},... | collective-permute-start | bytes 393224 | tf_op jit(solution)/shard_map/ppermute | solution.py:306
  146.4 2.1 %collective-permute-start.8 = (bf16[16,4,8,128]{3,2,1,0:T(8,128)(2,1)S(1)}, bf16[16,4,8,128]{3,2,1,0:T(8,128)(2,1)S(1)}, u32[]{:S(2)}, u32[]{:S(2)}) collective-permute-start(bf16[16,4,8,128]{3,2,1,0:T(8,128)(2,1)S(1)} %get-tuple-element.37), channel_id=1, source_target_pairs={{2,4},{4,2},{6,14},{14,6},{12,10},{10,12},{8,1},{1,8},{3,5},{5,3},... | collective-permute-start | bytes 393224 | tf_op jit(solution)/shard_map/ppermute | solution.py:307
  148.5 2.8 %collective-permute-done.9 = bf16[16,4,8,128]{3,2,1,0:T(8,128)(2,1)S(1)} collective-permute-done((bf16[16,4,8,128]{3,2,1,0:T(8,128)(2,1)S(1)}, bf16[16,4,8,128]{3,2,1,0:T(8,128)(2,1)S(1)}, u32[]{:S(2)}, u32[]{:S(2)}) %collective-permute-start.9) | collective-permute-done | bytes 131104 | tf_op jit(solution)/shard_map/ppermute | solution.py:306
  151.3 2.6 %collective-permute-done.8 = bf16[16,4,8,128]{3,2,1,0:T(8,128)(2,1)S(1)} collective-permute-done((bf16[16,4,8,128]{3,2,1,0:T(8,128)(2,1)S(1)}, bf16[16,4,8,128]{3,2,1,0:T(8,128)(2,1)S(1)}, u32[]{:S(2)}, u32[]{:S(2)}) %collective-permute-start.8) | collective-permute-done | bytes 131104 | tf_op jit(solution)/shard_map/ppermute | solution.py:307
  154.0 3.3 %shard_map.82 = (f32[4,4,16,128]{3,2,1,0:T(8,128)S(1)}, f32[4,4,16,128]{3,2,1,0:T(8,128)S(1)}, bf16[4,4,24,128]{3,2,1,0:T(8,128)(2,1)S(1)}) custom-call(bf16[8,7,2,16,128]{4,3,2,1,0:T(8,128)(2,1)S(1)} %all-to-all-done.r_ref.refs_0_, f32[4,4,16,128]{3,2,1,0:T(8,128)S(1)} %get-tuple-element.26.refs_1_, f32[4,4,16,128]{3,2,1,0:T(8,128)S(1)} %get-tuple-element.27.refs_2_, ...), custom_call_target="tpu_custom_call" | custom-call | tf_op jit(solution)/shard_map/pallas_call | solution.py:32
  157.3 2.0 %collective-permute-start.11 = (bf16[4,4,24,128]{3,2,1,0:T(8,128)(2,1)S(1)}, bf16[4,4,24,128]{3,2,1,0:T(8,128)(2,1)S(1)}, u32[]{:S(2)}, u32[]{:S(2)}) collective-permute-start(bf16[4,4,24,128]{3,2,1,0:T(8,128)(2,1)S(1)} %get-tuple-element.33.refs_5_), channel_id=1, source_target_pairs={{0,16},{16,0},{32,48},{48,32},{64,80},{80,64},{96,112},{112,96},{1... | collective-permute-start | bytes 294920 | tf_op jit(solution)/shard_map/ppermute | solution.py:306
  159.3 5.8 %collective-permute-start.10 = (bf16[4,4,24,128]{3,2,1,0:T(8,128)(2,1)S(1)}, bf16[4,4,24,128]{3,2,1,0:T(8,128)(2,1)S(1)}, u32[]{:S(2)}, u32[]{:S(2)}) collective-permute-start(bf16[4,4,24,128]{3,2,1,0:T(8,128)(2,1)S(1)} %get-tuple-element.33.refs_5_), channel_id=1, source_target_pairs={{16,32},{32,16},{48,64},{64,48},{80,96},{96,80},{112,128},{128,112... | collective-permute-start | bytes 294920 | tf_op jit(solution)/shard_map/ppermute | solution.py:307
  165.1 1.5 collective-permute-done.11
  166.6 2.5 %collective-permute-done.10 = bf16[4,4,24,128]{3,2,1,0:T(8,128)(2,1)S(1)} collective-permute-done((bf16[4,4,24,128]{3,2,1,0:T(8,128)(2,1)S(1)}, bf16[4,4,24,128]{3,2,1,0:T(8,128)(2,1)S(1)}, u32[]{:S(2)}, u32[]{:S(2)}) %collective-permute-start.10) | collective-permute-done | bytes 98336 | tf_op jit(solution)/shard_map/ppermute | solution.py:307
  169.1 2.6 %shard_map.83 = f32[2,4,2,2,16,128]{5,4,3,2,1,0:T(8,128)S(1)} custom-call(bf16[8,7,2,16,128]{4,3,2,1,0:T(8,128)(2,1)S(1)} %all-to-all-done.r_ref.refs_0_, f32[4,4,16,128]{3,2,1,0:T(8,128)S(1)} %get-tuple-element.31.refs_1_, f32[4,4,16,128]{3,2,1,0:T(8,128)S(1)} %get-tuple-element.32.refs_2_, bf16[4,4,24,128]{3,2,1,0:T(8,128)(2,1)S(1)} %get-tuple-element.43.refs_3_, ...), custom_call_target="tpu_custom_call" | custom-call | tf_op jit(solution)/shard_map/pallas_call | solution.py:32
  171.7 12.1 %all_to_all.20.in_ref = f32[8,2,2,16,128]{4,3,2,1,0:T(8,128)S(1)} all-to-all(f32[8,2,2,16,128]{4,3,2,1,0:T(8,128)S(1)} %bitcast.11), channel_id=1, replica_groups=mesh['grp'=2,'gX'=16,'gs'=2,'gy'=4,'gz'=2] {'gs','gy'}, dimensions={0} | all-to-all | bytes 524288 | tf_op jit(solution)/shard_map/all_to_all | solution.py:397
  183.9 0.9 shard_map.84
  (14 shorter events, 0.3 us)
Async XLA Ops:
  3.0 68.2 %all-to-all-start.1 = ((bf16[16,2,896]{2,1,0:T(2,128)(2,1)}), bf16[16,2,896]{2,1,0:T(2,128)(2,1)S(1)}, u32[]{:S(2)}, u32[]{:S(2)}) async-start(bf16[16,2,896]{2,1,0:T(2,128)(2,1)} %broadcast_in_dim.9), calls=%async_computation.1 | async-start | bytes 114688 | tf_op jit(solution)/shard_map/all_to_all | solution.py:334
  50.0 56.4 %copy-start = (f32[64]{0:T(128)S(1)}, f32[64]{0:T(128)}, u32[]{:S(2)}) copy-start(f32[64]{0:T(128)} %param.11) | copy-start | bytes 772
  71.2 12.6 %all-to-all-start = ((bf16[8,7,2,16,128]{4,3,2,1,0:T(8,128)(2,1)}), bf16[8,7,2,16,128]{4,3,2,1,0:T(8,128)(2,1)S(1)}, u32[]{:S(2)}, u32[]{:S(2)}) async-start(bf16[8,7,2,16,128]{4,3,2,1,0:T(8,128)(2,1)} %shard_map.77), calls=%async_computation | async-start | bytes 917504 | tf_op jit(solution)/shard_map/all_to_all | solution.py:364
  84.6 26.9 %all-to-all-start.2 = ((bf16[8,32,896]{2,1,0:T(8,128)(2,1)}), bf16[8,32,896]{2,1,0:T(8,128)(2,1)S(1)}, u32[]{:S(2)}, u32[]{:S(2)}) async-start(bf16[8,32,896]{2,1,0:T(8,128)(2,1)} %broadcast_in_dim.10), calls=%async_computation.2 | async-start | bytes 917504 | tf_op jit(solution)/shard_map/all_to_all | solution.py:338
  88.4 7.2 %collective-permute-start.1 = (bf16[4,4,16,128]{3,2,1,0:T(8,128)(2,1)S(1)}, bf16[4,4,16,128]{3,2,1,0:T(8,128)(2,1)S(1)}, u32[]{:S(2)}, u32[]{:S(2)}) collective-permute-start(bf16[4,4,16,128]{3,2,1,0:T(8,128)(2,1)S(1)} %get-tuple-element.18), channel_id=1, source_target_pairs={{0,16},{16,0},{32,48},{48,32},{64,80},{80,64},{96,112},{112,96},{1... | collective-permute-start | bytes 196616 | tf_op jit(solution)/shard_map/ppermute | solution.py:306
  92.2 8.3 %collective-permute-start = (bf16[4,4,16,128]{3,2,1,0:T(8,128)(2,1)S(1)}, bf16[4,4,16,128]{3,2,1,0:T(8,128)(2,1)S(1)}, u32[]{:S(2)}, u32[]{:S(2)}) collective-permute-start(bf16[4,4,16,128]{3,2,1,0:T(8,128)(2,1)S(1)} %get-tuple-element.18), channel_id=1, source_target_pairs={{16,32},{32,16},{48,64},{64,48},{80,96},{96,80},{112,128},{128,112... | collective-permute-start | bytes 196616 | tf_op jit(solution)/shard_map/ppermute | solution.py:307
  100.7 6.9 %collective-permute-start.3 = (bf16[16,4,8,128]{3,2,1,0:T(8,128)(2,1)S(1)}, bf16[16,4,8,128]{3,2,1,0:T(8,128)(2,1)S(1)}, u32[]{:S(2)}, u32[]{:S(2)}) collective-permute-start(bf16[16,4,8,128]{3,2,1,0:T(8,128)(2,1)S(1)} %get-tuple-element.40), channel_id=1, source_target_pairs={{0,2},{2,0},{4,6},{6,4},{14,12},{12,14},{10,8},{8,10},{1,3},{3,1},... | collective-permute-start | bytes 393224 | tf_op jit(solution)/shard_map/ppermute | solution.py:306
  104.4 7.1 %collective-permute-start.2 = (bf16[16,4,8,128]{3,2,1,0:T(8,128)(2,1)S(1)}, bf16[16,4,8,128]{3,2,1,0:T(8,128)(2,1)S(1)}, u32[]{:S(2)}, u32[]{:S(2)}) collective-permute-start(bf16[16,4,8,128]{3,2,1,0:T(8,128)(2,1)S(1)} %get-tuple-element.41), channel_id=1, source_target_pairs={{2,4},{4,2},{6,14},{14,6},{12,10},{10,12},{8,1},{1,8},{3,5},{5,3},... | collective-permute-start | bytes 393224 | tf_op jit(solution)/shard_map/ppermute | solution.py:307
  116.5 9.2 %collective-permute-start.5 = (bf16[4,4,24,128]{3,2,1,0:T(8,128)(2,1)S(1)}, bf16[4,4,24,128]{3,2,1,0:T(8,128)(2,1)S(1)}, u32[]{:S(2)}, u32[]{:S(2)}) collective-permute-start(bf16[4,4,24,128]{3,2,1,0:T(8,128)(2,1)S(1)} %get-tuple-element.25.refs_5_), channel_id=1, source_target_pairs={{0,16},{16,0},{32,48},{48,32},{64,80},{80,64},{96,112},{112,96},{1... | collective-permute-start | bytes 294920 | tf_op jit(solution)/shard_map/ppermute | solution.py:306
  120.0 8.7 %collective-permute-start.4 = (bf16[4,4,24,128]{3,2,1,0:T(8,128)(2,1)S(1)}, bf16[4,4,24,128]{3,2,1,0:T(8,128)(2,1)S(1)}, u32[]{:S(2)}, u32[]{:S(2)}) collective-permute-start(bf16[4,4,24,128]{3,2,1,0:T(8,128)(2,1)S(1)} %get-tuple-element.25.refs_5_), channel_id=1, source_target_pairs={{16,32},{32,16},{48,64},{64,48},{80,96},{96,80},{112,128},{128,112... | collective-permute-start | bytes 294920 | tf_op jit(solution)/shard_map/ppermute | solution.py:307
  131.3 7.9 %collective-permute-start.7 = (bf16[4,4,16,128]{3,2,1,0:T(8,128)(2,1)S(1)}, bf16[4,4,16,128]{3,2,1,0:T(8,128)(2,1)S(1)}, u32[]{:S(2)}, u32[]{:S(2)}) collective-permute-start(bf16[4,4,16,128]{3,2,1,0:T(8,128)(2,1)S(1)} %get-tuple-element.28), channel_id=1, source_target_pairs={{0,16},{16,0},{32,48},{48,32},{64,80},{80,64},{96,112},{112,96},{1... | collective-permute-start | bytes 196616 | tf_op jit(solution)/shard_map/ppermute | solution.py:306
  136.0 8.3 %collective-permute-start.6 = (bf16[4,4,16,128]{3,2,1,0:T(8,128)(2,1)S(1)}, bf16[4,4,16,128]{3,2,1,0:T(8,128)(2,1)S(1)}, u32[]{:S(2)}, u32[]{:S(2)}) collective-permute-start(bf16[4,4,16,128]{3,2,1,0:T(8,128)(2,1)S(1)} %get-tuple-element.28), channel_id=1, source_target_pairs={{16,32},{32,16},{48,64},{64,48},{80,96},{96,80},{112,128},{128,112... | collective-permute-start | bytes 196616 | tf_op jit(solution)/shard_map/ppermute | solution.py:307
  144.4 6.9 %collective-permute-start.9 = (bf16[16,4,8,128]{3,2,1,0:T(8,128)(2,1)S(1)}, bf16[16,4,8,128]{3,2,1,0:T(8,128)(2,1)S(1)}, u32[]{:S(2)}, u32[]{:S(2)}) collective-permute-start(bf16[16,4,8,128]{3,2,1,0:T(8,128)(2,1)S(1)} %get-tuple-element.36), channel_id=1, source_target_pairs={{0,2},{2,0},{4,6},{6,4},{14,12},{12,14},{10,8},{8,10},{1,3},{3,1},... | collective-permute-start | bytes 393224 | tf_op jit(solution)/shard_map/ppermute | solution.py:306
  146.4 7.6 %collective-permute-start.8 = (bf16[16,4,8,128]{3,2,1,0:T(8,128)(2,1)S(1)}, bf16[16,4,8,128]{3,2,1,0:T(8,128)(2,1)S(1)}, u32[]{:S(2)}, u32[]{:S(2)}) collective-permute-start(bf16[16,4,8,128]{3,2,1,0:T(8,128)(2,1)S(1)} %get-tuple-element.37), channel_id=1, source_target_pairs={{2,4},{4,2},{6,14},{14,6},{12,10},{10,12},{8,1},{1,8},{3,5},{5,3},... | collective-permute-start | bytes 393224 | tf_op jit(solution)/shard_map/ppermute | solution.py:307
  157.3 9.2 %collective-permute-start.11 = (bf16[4,4,24,128]{3,2,1,0:T(8,128)(2,1)S(1)}, bf16[4,4,24,128]{3,2,1,0:T(8,128)(2,1)S(1)}, u32[]{:S(2)}, u32[]{:S(2)}) collective-permute-start(bf16[4,4,24,128]{3,2,1,0:T(8,128)(2,1)S(1)} %get-tuple-element.33.refs_5_), channel_id=1, source_target_pairs={{0,16},{16,0},{32,48},{48,32},{64,80},{80,64},{96,112},{112,96},{1... | collective-permute-start | bytes 294920 | tf_op jit(solution)/shard_map/ppermute | solution.py:306
  159.3 9.8 %collective-permute-start.10 = (bf16[4,4,24,128]{3,2,1,0:T(8,128)(2,1)S(1)}, bf16[4,4,24,128]{3,2,1,0:T(8,128)(2,1)S(1)}, u32[]{:S(2)}, u32[]{:S(2)}) collective-permute-start(bf16[4,4,24,128]{3,2,1,0:T(8,128)(2,1)S(1)} %get-tuple-element.33.refs_5_), channel_id=1, source_target_pairs={{16,32},{32,16},{48,64},{64,48},{80,96},{96,80},{112,128},{128,112... | collective-permute-start | bytes 294920 | tf_op jit(solution)/shard_map/ppermute | solution.py:307

commit v7 on v5

--- a/solution.py
+++ b/solution.py
@@ -310,6 +310,16 @@
         xh = lax.ppermute(block, "gX", x_shift(-1))
         return xl, xh
 
+    def swapped_along_x(block):
+        def swaps(first):
+            pairs = [(i, (i + 1) % gX) for i in range(0 if first else 1, gX, 2)]
+            return [pair for i, j in pairs for pair in ((i, j), (j, i))]
+
+        one = lax.ppermute(block, "gX", swaps(True))
+        two = lax.ppermute(block, "gX", swaps(False))
+        even = lax.axis_index("gX") % 2 == 0
+        return jnp.where(even, two, one), jnp.where(even, one, two)
+
     def along_both(block, rl, rh):
         xl, xh = along_x(block)
         whole = jnp.concatenate([xl, block, xh], axis=0)
@@ -372,7 +382,11 @@
         for k in range(steps + 1):
             kind = "first" if k == 0 else "last" if k == steps else k
             wide = k % 2 == 0
-            edges = along_both(block, *ends) if wide else (*along_x(block), block)
+            if wide:
+                edges = along_both(block, *ends)
+            else:
+                swap = swapped_along_x if kind == "last" else along_x
+                edges = (*swap(block), block)
             outs = [state32, state32, grown16] if wide else [state32, state32, block16, strip16, strip16]
             if kind == "last":
                 outs = [jax.ShapeDtypeStruct((gs, gy, 2, 2, ZB, 128), F32)]

time: 186 us -> 185 us (level)
  waiting for transfers between devices: 56 us -> 49.9 us
    ppermute x4 -> x3, waiting for transfers between devices: 11.7 us -> 2.06 us  [along_x(): xl = lax.ppermute(block, 'gX', x_shift(1))]
    ppermute x4 -> x3, starting transfers between devices: 22.1 us -> 13.7 us  [along_x(): xh = lax.ppermute(block, 'gX', x_shift(-1))]
    ppermute x0 -> x2, starting transfers between devices: none -> 8.12 us  [the longest x1 6.17 us: swapped_along_x(): two = lax.ppermute(block, 'gX', swaps(False))]
    ppermute x0 -> x2, waiting for transfers between devices: none -> 6.45 us  [the longest x1 5.28 us: swapped_along_x(): one = lax.ppermute(block, 'gX', swaps(True))]
    ppermute x2, waiting for transfers between devices: 6.31 us -> 0.77 us  [along_both(): zh = lax.ppermute(down, ('gs', 'gy', 'gz'), z_shift(-1))]
    ppermute x2, waiting for transfers between devices: 0.48 us -> 4.73 us  [along_both(): zl = lax.ppermute(up, ('gs', 'gy', 'gz'), z_shift(1))]
    ppermute x2, starting transfers between devices: 6.18 us -> 8.07 us  [along_both(): zl = lax.ppermute(up, ('gs', 'gy', 'gz'), z_shift(1))]
    ppermute x4 -> x3, waiting for transfers between devices: 8.39 us -> 6.74 us  [along_x(): xh = lax.ppermute(block, 'gX', x_shift(-1))]
  transfers between devices with their start and end apart: 15 -> 15, of which waited for: 13 -> 13; matrix products, arithmetic and copies ran while one was open for 0% -> 1% of each run, Pallas kernels for 2% -> 2%
where the time goes in v7:
time: 185 us; the launch traced here: 184 us
  starting transfers between devices  97.1 us (52%)
  waiting for transfers between devices  49.9 us (27%)
  Pallas kernels  17.5 us (9%)
  blocking collectives  12.4 us (7%)
  local copies, waits for them, and re-layouts  4.68 us (3%)
    all_to_all x1, starting transfers between devices, body(): lax.all_to_all(jnp.broadcast_to(own, (gX, *own.shape)), 'gX', 0, 0, tiled...  44.6 us
    all_to_all x1, waiting for transfers between devices, body(): lax.all_to_all(jnp.broadcast_to(own, (gX, *own.shape)), 'gX', 0, 0, tiled...  21.2 us
    pallas_call x8, Pallas kernels, kernel_call(): pl.pallas_call(body, out_shape=outs if hbm_out else [VMEM(o.shape, o.dtyp...  17.5 us
    ppermute x3, starting transfers between devices, along_x(): xh = lax.ppermute(block, 'gX', x_shift(-1))  13.7 us
    all_to_all x1, blocking collectives, body(): lax.all_to_all(res[0].reshape(members, 2, 2, ZB, 128), ('gs', 'gy'), 0, 0...  12.4 us
    ppermute x3, starting transfers between devices, along_x(): xl = lax.ppermute(block, 'gX', x_shift(1))  10.4 us
    ppermute x2, starting transfers between devices, along_both(): zl = lax.ppermute(up, ('gs', 'gy', 'gz'), z_shift(1))  8.07 us
    all_to_all x1, waiting for transfers between devices, body(): held = lax.all_to_all(spread, ('gs', 'gy'), 0, 0, tiled=True)  7.99 us
  transfers between devices with their start and end apart: 15, of which 13 were waited for; matrix products, arithmetic and copies ran while one was open for 1% of the time, Pallas kernels for 2%

profile of v7, /device:TPU:40, one launch (start us, length us, event | category | flops | bytes accessed | tf_op | source)
XLA Modules:
  0.0 184.0 jit_solution(12826995278488590027)
XLA Ops:
  0.6 0.7 copy.13
  1.3 0.1 reshape.23
  1.4 0.7 copy.12
  2.2 0.1 reshape.25
  2.2 0.1 fusion.2
  2.3 0.7 broadcast_in_dim.9
  3.0 44.6 %all-to-all-start.1 = ((bf16[16,2,896]{2,1,0:T(2,128)(2,1)}), bf16[16,2,896]{2,1,0:T(2,128)(2,1)S(1)}, u32[]{:S(2)}, u32[]{:S(2)}) async-start(bf16[16,2,896]{2,1,0:T(2,128)(2,1)} %broadcast_in_dim.9), calls=%async_computation.1 | async-start | bytes 114688 | tf_op jit(solution)/shard_map/all_to_all | solution.py:340
  47.6 2.4 %shard_map.77 = bf16[8,7,2,16,128]{4,3,2,1,0:T(8,128)(2,1)} custom-call(f32[64,2,2,128]{3,2,1,0:T(2,128)} %q_ref.1, f32[64,2,2,128]{3,2,1,0:T(2,128)} %p_ref.1, bf16[3,64,2,2,128]{4,3,2,1,0:T(2,128)(2,1)} %n_ref.1), custom_call_target="tpu_custom_call" | custom-call | tf_op jit(solution)/shard_map/pallas_call | solution.py:32
  50.0 21.2 %all-to-all-done.1 = bf16[16,2,896]{2,1,0:T(2,128)(2,1)S(1)} async-done(((bf16[16,2,896]{2,1,0:T(2,128)(2,1)}), bf16[16,2,896]{2,1,0:T(2,128)(2,1)S(1)}, u32[]{:S(2)}, u32[]{:S(2)}) %all-to-all-start.1) | async-done | bytes 57376 | tf_op jit(solution)/shard_map/all_to_all | solution.py:340
  71.2 4.6 %all-to-all-start = ((bf16[8,7,2,16,128]{4,3,2,1,0:T(8,128)(2,1)}), bf16[8,7,2,16,128]{4,3,2,1,0:T(8,128)(2,1)S(1)}, u32[]{:S(2)}, u32[]{:S(2)}) async-start(bf16[8,7,2,16,128]{4,3,2,1,0:T(8,128)(2,1)} %shard_map.77), calls=%async_computation | async-start | bytes 917504 | tf_op jit(solution)/shard_map/all_to_all | solution.py:370
  75.8 8.0 %all-to-all-done.r_ref.refs_0_ = bf16[8,7,2,16,128]{4,3,2,1,0:T(8,128)(2,1)S(1)} async-done(((bf16[8,7,2,16,128]{4,3,2,1,0:T(8,128)(2,1)}), bf16[8,7,2,16,128]{4,3,2,1,0:T(8,128)(2,1)S(1)}, u32[]{:S(2)}, u32[]{:S(2)}) %all-to-all-start) | async-done | bytes 458784 | tf_op jit(solution)/shard_map/all_to_all | solution.py:370
  83.8 0.8 broadcast_in_dim.10
  84.6 3.7 %all-to-all-start.2 = ((bf16[8,32,896]{2,1,0:T(8,128)(2,1)}), bf16[8,32,896]{2,1,0:T(8,128)(2,1)S(1)}, u32[]{:S(2)}, u32[]{:S(2)}) async-start(bf16[8,32,896]{2,1,0:T(8,128)(2,1)} %broadcast_in_dim.10), calls=%async_computation.2 | async-start | bytes 917504 | tf_op jit(solution)/shard_map/all_to_all | solution.py:344
  88.3 0.1 shard_map.78
  88.4 3.8 %collective-permute-start = (bf16[4,4,16,128]{3,2,1,0:T(8,128)(2,1)S(1)}, bf16[4,4,16,128]{3,2,1,0:T(8,128)(2,1)S(1)}, u32[]{:S(2)}, u32[]{:S(2)}) collective-permute-start(bf16[4,4,16,128]{3,2,1,0:T(8,128)(2,1)S(1)} %get-tuple-element.18), channel_id=1, source_target_pairs={{0,16},{16,32},{32,48},{48,64},{64,80},{80,96},{96,112},{112,128},... | collective-permute-start | bytes 196616 | tf_op jit(solution)/shard_map/ppermute | solution.py:309
  92.3 4.2 %collective-permute-start.1 = (bf16[4,4,16,128]{3,2,1,0:T(8,128)(2,1)S(1)}, bf16[4,4,16,128]{3,2,1,0:T(8,128)(2,1)S(1)}, u32[]{:S(2)}, u32[]{:S(2)}) collective-permute-start(bf16[4,4,16,128]{3,2,1,0:T(8,128)(2,1)S(1)} %get-tuple-element.18), channel_id=1, source_target_pairs={{0,240},{16,0},{32,16},{48,32},{64,48},{80,64},{96,80},{112,96},{1... | collective-permute-start | bytes 196616 | tf_op jit(solution)/shard_map/ppermute | solution.py:310
  96.4 0.3 collective-permute-done.refs_1_
  96.8 2.6 %collective-permute-done.1.refs_2_ = bf16[4,4,16,128]{3,2,1,0:T(8,128)(2,1)S(1)} collective-permute-done((bf16[4,4,16,128]{3,2,1,0:T(8,128)(2,1)S(1)}, bf16[4,4,16,128]{3,2,1,0:T(8,128)(2,1)S(1)}, u32[]{:S(2)}, u32[]{:S(2)}) %collective-permute-start.1) | collective-permute-done | bytes 65568 | tf_op jit(solution)/shard_map/ppermute | solution.py:310
  99.4 0.7 pad_maximum_fusion.1
  100.1 1.9 %collective-permute-start.3 = (bf16[16,4,8,128]{3,2,1,0:T(8,128)(2,1)}, bf16[16,4,8,128]{3,2,1,0:T(8,128)(2,1)S(1)}, u32[]{:S(2)}, u32[]{:S(2)}) collective-permute-start(bf16[16,4,8,128]{3,2,1,0:T(8,128)(2,1)} %pad_maximum_fusion.1), channel_id=1, source_target_pairs={{0,9},{2,0},{4,2},{6,4},{14,6},{12,14},{10,12},{8,10},{1,8},{3,1},... | collective-permute-start | bytes 393224 | tf_op jit(solution)/shard_map/ppermute | solution.py:329
  102.0 0.7 pad_maximum_fusion
  102.7 3.9 %collective-permute-start.2 = (bf16[16,4,8,128]{3,2,1,0:T(8,128)(2,1)}, bf16[16,4,8,128]{3,2,1,0:T(8,128)(2,1)}, u32[]{:S(2)}, u32[]{:S(2)}) collective-permute-start(bf16[16,4,8,128]{3,2,1,0:T(8,128)(2,1)} %pad_maximum_fusion), channel_id=1, source_target_pairs={{0,2},{2,4},{4,6},{6,14},{14,12},{12,10},{10,8},{8,1},{1,3},{3,5},... | collective-permute-start | bytes 393224 | tf_op jit(solution)/shard_map/ppermute | solution.py:328
  106.6 0.1 maximum_bitcast_fusion.refs_7_.refs_8_.refs_9_
  106.7 1.7 shard_map.79
  108.4 2.3 %collective-permute-done.2.refs_3_ = bf16[16,4,8,128]{3,2,1,0:T(8,128)(2,1)} collective-permute-done((bf16[16,4,8,128]{3,2,1,0:T(8,128)(2,1)}, bf16[16,4,8,128]{3,2,1,0:T(8,128)(2,1)}, u32[]{:S(2)}, u32[]{:S(2)}) %collective-permute-start.2) | collective-permute-done | bytes 131104 | tf_op jit(solution)/shard_map/ppermute | solution.py:328
  110.7 4.1 %shard_map.80 = (f32[4,4,16,128]{3,2,1,0:T(8,128)S(1)}, f32[4,4,16,128]{3,2,1,0:T(8,128)S(1)}, bf16[4,4,24,128]{3,2,1,0:T(8,128)(2,1)S(1)}) custom-call(bf16[8,7,2,16,128]{4,3,2,1,0:T(8,128)(2,1)S(1)} %all-to-all-done.r_ref.refs_0_, bf16[4,4,16,128]{3,2,1,0:T(8,128)(2,1)S(1)} %collective-permute-done.refs_1_, ...), custom_call_target="tpu_custom_call" | custom-call | tf_op jit(solution)/shard_map/pallas_call | solution.py:32
  114.8 3.1 %collective-permute-start.4 = (bf16[4,4,24,128]{3,2,1,0:T(8,128)(2,1)S(1)}, bf16[4,4,24,128]{3,2,1,0:T(8,128)(2,1)S(1)}, u32[]{:S(2)}, u32[]{:S(2)}) collective-permute-start(bf16[4,4,24,128]{3,2,1,0:T(8,128)(2,1)S(1)} %get-tuple-element.25.refs_5_), channel_id=1, source_target_pairs={{0,16},{16,32},{32,48},{48,64},{64,80},{80,96},{96,112},{112,128},... | collective-permute-start | bytes 294920 | tf_op jit(solution)/shard_map/ppermute | solution.py:309
  118.0 4.9 %collective-permute-start.5 = (bf16[4,4,24,128]{3,2,1,0:T(8,128)(2,1)S(1)}, bf16[4,4,24,128]{3,2,1,0:T(8,128)(2,1)S(1)}, u32[]{:S(2)}, u32[]{:S(2)}) collective-permute-start(bf16[4,4,24,128]{3,2,1,0:T(8,128)(2,1)S(1)} %get-tuple-element.25.refs_5_), channel_id=1, source_target_pairs={{0,240},{16,0},{32,16},{48,32},{64,48},{80,64},{96,80},{112,96},{1... | collective-permute-start | bytes 294920 | tf_op jit(solution)/shard_map/ppermute | solution.py:310
  122.9 1.5 collective-permute-done.4.refs_3_
  124.4 2.0 %collective-permute-done.5.refs_4_ = bf16[4,4,24,128]{3,2,1,0:T(8,128)(2,1)S(1)} collective-permute-done((bf16[4,4,24,128]{3,2,1,0:T(8,128)(2,1)S(1)}, bf16[4,4,24,128]{3,2,1,0:T(8,128)(2,1)S(1)}, u32[]{:S(2)}, u32[]{:S(2)}) %collective-permute-start.5) | collective-permute-done | bytes 98336 | tf_op jit(solution)/shard_map/ppermute | solution.py:310
  126.4 2.5 %shard_map.81 = (f32[4,4,16,128]{3,2,1,0:T(8,128)S(1)}, f32[4,4,16,128]{3,2,1,0:T(8,128)S(1)}, bf16[4,4,16,128]{3,2,1,0:T(8,128)(2,1)S(1)}, bf16[4,4,8,128]{3,2,1,0:T(8,128)(2,1)S(1)}, bf16[4,4,8,128]{3,2,1,0:T(8,128)(2,1)S(1)}) custom-call(bf16[8,7,2,16,128]{4,3,2,1,0:T(8,128)(2,1)S(1)} %all-to-all-done.r_ref.refs_0_, ...), custom_call_target="tpu_custom_call" | custom-call | tf_op jit(solution)/shard_map/pallas_call | solution.py:32
  128.9 3.5 %collective-permute-start.6 = (bf16[4,4,16,128]{3,2,1,0:T(8,128)(2,1)S(1)}, bf16[4,4,16,128]{3,2,1,0:T(8,128)(2,1)S(1)}, u32[]{:S(2)}, u32[]{:S(2)}) collective-permute-start(bf16[4,4,16,128]{3,2,1,0:T(8,128)(2,1)S(1)} %get-tuple-element.28), channel_id=1, source_target_pairs={{0,16},{16,32},{32,48},{48,64},{64,80},{80,96},{96,112},{112,128},... | collective-permute-start | bytes 196616 | tf_op jit(solution)/shard_map/ppermute | solution.py:309
  132.4 4.7 %collective-permute-start.7 = (bf16[4,4,16,128]{3,2,1,0:T(8,128)(2,1)S(1)}, bf16[4,4,16,128]{3,2,1,0:T(8,128)(2,1)S(1)}, u32[]{:S(2)}, u32[]{:S(2)}) collective-permute-start(bf16[4,4,16,128]{3,2,1,0:T(8,128)(2,1)S(1)} %get-tuple-element.28), channel_id=1, source_target_pairs={{0,240},{16,0},{32,16},{48,32},{64,48},{80,64},{96,80},{112,96},{1... | collective-permute-start | bytes 196616 | tf_op jit(solution)/shard_map/ppermute | solution.py:310
  137.1 0.3 collective-permute-done.6.refs_3_
  137.4 2.1 %collective-permute-done.7.refs_4_ = bf16[4,4,16,128]{3,2,1,0:T(8,128)(2,1)S(1)} collective-permute-done((bf16[4,4,16,128]{3,2,1,0:T(8,128)(2,1)S(1)}, bf16[4,4,16,128]{3,2,1,0:T(8,128)(2,1)S(1)}, u32[]{:S(2)}, u32[]{:S(2)}) %collective-permute-start.7) | collective-permute-done | bytes 65568 | tf_op jit(solution)/shard_map/ppermute | solution.py:310
  139.6 2.0 %collective-permute-start.9 = (bf16[16,4,8,128]{3,2,1,0:T(8,128)(2,1)S(1)}, bf16[16,4,8,128]{3,2,1,0:T(8,128)(2,1)S(1)}, u32[]{:S(2)}, u32[]{:S(2)}) collective-permute-start(bf16[16,4,8,128]{3,2,1,0:T(8,128)(2,1)S(1)} %pad_maximum_fusion.3), channel_id=1, source_target_pairs={{0,9},{2,0},{4,2},{6,4},{14,6},{12,14},{10,12},{8,10},{1,8},{3,1},... | collective-permute-start | bytes 393224 | tf_op jit(solution)/shard_map/ppermute | solution.py:329
  141.6 4.1 %collective-permute-start.8 = (bf16[16,4,8,128]{3,2,1,0:T(8,128)(2,1)S(1)}, bf16[16,4,8,128]{3,2,1,0:T(8,128)(2,1)S(1)}, u32[]{:S(2)}, u32[]{:S(2)}) collective-permute-start(bf16[16,4,8,128]{3,2,1,0:T(8,128)(2,1)S(1)} %pad_maximum_fusion.2), channel_id=1, source_target_pairs={{0,2},{2,4},{4,6},{6,14},{14,12},{12,10},{10,8},{8,1},{1,3},{3,5},... | collective-permute-start | bytes 393224 | tf_op jit(solution)/shard_map/ppermute | solution.py:328
  145.7 0.8 collective-permute-done.9.refs_6_
  146.5 2.5 %collective-permute-done.8.refs_5_ = bf16[16,4,8,128]{3,2,1,0:T(8,128)(2,1)S(1)} collective-permute-done((bf16[16,4,8,128]{3,2,1,0:T(8,128)(2,1)S(1)}, bf16[16,4,8,128]{3,2,1,0:T(8,128)(2,1)S(1)}, u32[]{:S(2)}, u32[]{:S(2)}) %collective-permute-start.8) | collective-permute-done | bytes 131104 | tf_op jit(solution)/shard_map/ppermute | solution.py:328
  149.0 3.2 %shard_map.82 = (f32[4,4,16,128]{3,2,1,0:T(8,128)S(1)}, f32[4,4,16,128]{3,2,1,0:T(8,128)S(1)}, bf16[4,4,24,128]{3,2,1,0:T(8,128)(2,1)S(1)}) custom-call(bf16[8,7,2,16,128]{4,3,2,1,0:T(8,128)(2,1)S(1)} %all-to-all-done.r_ref.refs_0_, f32[4,4,16,128]{3,2,1,0:T(8,128)S(1)} %get-tuple-element.26.refs_1_, f32[4,4,16,128]{3,2,1,0:T(8,128)S(1)} %get-tuple-element.27.refs_2_, ...), custom_call_target="tpu_custom_call" | custom-call | tf_op jit(solution)/shard_map/pallas_call | solution.py:32
  152.2 6.2 %collective-permute-start.10 = (bf16[4,4,24,128]{3,2,1,0:T(8,128)(2,1)S(1)}, bf16[4,4,24,128]{3,2,1,0:T(8,128)(2,1)S(1)}, u32[]{:S(2)}, u32[]{:S(2)}) collective-permute-start(bf16[4,4,24,128]{3,2,1,0:T(8,128)(2,1)S(1)} %get-tuple-element.33.refs_5_), channel_id=1, source_target_pairs={{16,32},{32,16},{48,64},{64,48},{80,96},{96,80},{112,128},{128,112... | collective-permute-start | bytes 294920 | tf_op jit(solution)/shard_map/ppermute | solution.py:319
  158.4 2.0 %collective-permute-start.11 = (bf16[4,4,24,128]{3,2,1,0:T(8,128)(2,1)S(1)}, bf16[4,4,24,128]{3,2,1,0:T(8,128)(2,1)S(1)}, u32[]{:S(2)}, u32[]{:S(2)}) collective-permute-start(bf16[4,4,24,128]{3,2,1,0:T(8,128)(2,1)S(1)} %get-tuple-element.33.refs_5_), channel_id=1, source_target_pairs={{0,16},{16,0},{32,48},{48,32},{64,80},{80,64},{96,112},{112,96},{1... | collective-permute-start | bytes 294920 | tf_op jit(solution)/shard_map/ppermute | solution.py:318
  160.3 1.2 collective-permute-done.10
  161.5 5.3 %collective-permute-done.11 = bf16[4,4,24,128]{3,2,1,0:T(8,128)(2,1)S(1)} collective-permute-done((bf16[4,4,24,128]{3,2,1,0:T(8,128)(2,1)S(1)}, bf16[4,4,24,128]{3,2,1,0:T(8,128)(2,1)S(1)}, u32[]{:S(2)}, u32[]{:S(2)}) %collective-permute-start.11) | collective-permute-done | bytes 98336 | tf_op jit(solution)/shard_map/ppermute | solution.py:318
  166.8 1.4 copy-done.1
  168.2 2.5 %shard_map.83 = f32[2,4,2,2,16,128]{5,4,3,2,1,0:T(8,128)S(1)} custom-call(bf16[8,7,2,16,128]{4,3,2,1,0:T(8,128)(2,1)S(1)} %all-to-all-done.r_ref.refs_0_, f32[4,4,16,128]{3,2,1,0:T(8,128)S(1)} %get-tuple-element.31.refs_1_, f32[4,4,16,128]{3,2,1,0:T(8,128)S(1)} %get-tuple-element.32.refs_2_, bf16[4,4,24,128]{3,2,1,0:T(8,128)(2,1)S(1)} %get-tuple-element.35.refs_3_, ...), custom_call_target="tpu_custom_call" | custom-call | tf_op jit(solution)/shard_map/pallas_call | solution.py:32
  170.7 12.4 %all_to_all.20.in_ref = f32[8,2,2,16,128]{4,3,2,1,0:T(8,128)S(1)} all-to-all(f32[8,2,2,16,128]{4,3,2,1,0:T(8,128)S(1)} %bitcast.11), channel_id=1, replica_groups=mesh['grp'=2,'gX'=16,'gs'=2,'gy'=4,'gz'=2] {'gs','gy'}, dimensions={0} | all-to-all | bytes 524288 | tf_op jit(solution)/shard_map/all_to_all | solution.py:407
  183.1 0.9 shard_map.84
  (19 shorter events, 0.2 us)
Async XLA Ops:
  3.0 68.2 %all-to-all-start.1 = ((bf16[16,2,896]{2,1,0:T(2,128)(2,1)}), bf16[16,2,896]{2,1,0:T(2,128)(2,1)S(1)}, u32[]{:S(2)}, u32[]{:S(2)}) async-start(bf16[16,2,896]{2,1,0:T(2,128)(2,1)} %broadcast_in_dim.9), calls=%async_computation.1 | async-start | bytes 114688 | tf_op jit(solution)/shard_map/all_to_all | solution.py:340
  47.6 59.1 %copy-start.2 = (f32[64]{0:T(128)S(1)}, f32[64]{0:T(128)}, u32[]{:S(2)}) copy-start(f32[64]{0:T(128)} %param.11) | copy-start | bytes 772
  71.2 12.6 %all-to-all-start = ((bf16[8,7,2,16,128]{4,3,2,1,0:T(8,128)(2,1)}), bf16[8,7,2,16,128]{4,3,2,1,0:T(8,128)(2,1)S(1)}, u32[]{:S(2)}, u32[]{:S(2)}) async-start(bf16[8,7,2,16,128]{4,3,2,1,0:T(8,128)(2,1)} %shard_map.77), calls=%async_computation | async-start | bytes 917504 | tf_op jit(solution)/shard_map/all_to_all | solution.py:370
  84.6 22.1 %all-to-all-start.2 = ((bf16[8,32,896]{2,1,0:T(8,128)(2,1)}), bf16[8,32,896]{2,1,0:T(8,128)(2,1)S(1)}, u32[]{:S(2)}, u32[]{:S(2)}) async-start(bf16[8,32,896]{2,1,0:T(8,128)(2,1)} %broadcast_in_dim.10), calls=%async_computation.2 | async-start | bytes 917504 | tf_op jit(solution)/shard_map/all_to_all | solution.py:344
  88.4 8.3 %collective-permute-start = (bf16[4,4,16,128]{3,2,1,0:T(8,128)(2,1)S(1)}, bf16[4,4,16,128]{3,2,1,0:T(8,128)(2,1)S(1)}, u32[]{:S(2)}, u32[]{:S(2)}) collective-permute-start(bf16[4,4,16,128]{3,2,1,0:T(8,128)(2,1)S(1)} %get-tuple-element.18), channel_id=1, source_target_pairs={{0,16},{16,32},{32,48},{48,64},{64,80},{80,96},{96,112},{112,128},... | collective-permute-start | bytes 196616 | tf_op jit(solution)/shard_map/ppermute | solution.py:309
  92.3 7.1 %collective-permute-start.1 = (bf16[4,4,16,128]{3,2,1,0:T(8,128)(2,1)S(1)}, bf16[4,4,16,128]{3,2,1,0:T(8,128)(2,1)S(1)}, u32[]{:S(2)}, u32[]{:S(2)}) collective-permute-start(bf16[4,4,16,128]{3,2,1,0:T(8,128)(2,1)S(1)} %get-tuple-element.18), channel_id=1, source_target_pairs={{0,240},{16,0},{32,16},{48,32},{64,48},{80,64},{96,80},{112,96},{1... | collective-permute-start | bytes 196616 | tf_op jit(solution)/shard_map/ppermute | solution.py:310
  100.1 8.4 %collective-permute-start.3 = (bf16[16,4,8,128]{3,2,1,0:T(8,128)(2,1)}, bf16[16,4,8,128]{3,2,1,0:T(8,128)(2,1)S(1)}, u32[]{:S(2)}, u32[]{:S(2)}) collective-permute-start(bf16[16,4,8,128]{3,2,1,0:T(8,128)(2,1)} %pad_maximum_fusion.1), channel_id=1, source_target_pairs={{0,9},{2,0},{4,2},{6,4},{14,6},{12,14},{10,12},{8,10},{1,8},{3,1},... | collective-permute-start | bytes 393224 | tf_op jit(solution)/shard_map/ppermute | solution.py:329
  102.7 8.0 %collective-permute-start.2 = (bf16[16,4,8,128]{3,2,1,0:T(8,128)(2,1)}, bf16[16,4,8,128]{3,2,1,0:T(8,128)(2,1)}, u32[]{:S(2)}, u32[]{:S(2)}) collective-permute-start(bf16[16,4,8,128]{3,2,1,0:T(8,128)(2,1)} %pad_maximum_fusion), channel_id=1, source_target_pairs={{0,2},{2,4},{4,6},{6,14},{14,12},{12,10},{10,8},{8,1},{1,3},{3,5},... | collective-permute-start | bytes 393224 | tf_op jit(solution)/shard_map/ppermute | solution.py:328
  108.4 40.5 %copy-start = (bf16[4,768,256]{2,1,0:T(8,128)(2,1)}, bf16[4,768,256]{2,1,0:T(8,128)(2,1)S(1)}, u32[]{:S(2)}) copy-start(bf16[4,768,256]{2,1,0:T(8,128)(2,1)S(1)} %get-tuple-element.21.refs_5_.refs_6_.refs_7_) | copy-start | bytes 4718596
  114.8 9.5 %collective-permute-start.4 = (bf16[4,4,24,128]{3,2,1,0:T(8,128)(2,1)S(1)}, bf16[4,4,24,128]{3,2,1,0:T(8,128)(2,1)S(1)}, u32[]{:S(2)}, u32[]{:S(2)}) collective-permute-start(bf16[4,4,24,128]{3,2,1,0:T(8,128)(2,1)S(1)} %get-tuple-element.25.refs_5_), channel_id=1, source_target_pairs={{0,16},{16,32},{32,48},{48,64},{64,80},{80,96},{96,112},{112,128},... | collective-permute-start | bytes 294920 | tf_op jit(solution)/shard_map/ppermute | solution.py:309
  118.0 8.4 %collective-permute-start.5 = (bf16[4,4,24,128]{3,2,1,0:T(8,128)(2,1)S(1)}, bf16[4,4,24,128]{3,2,1,0:T(8,128)(2,1)S(1)}, u32[]{:S(2)}, u32[]{:S(2)}) collective-permute-start(bf16[4,4,24,128]{3,2,1,0:T(8,128)(2,1)S(1)} %get-tuple-element.25.refs_5_), channel_id=1, source_target_pairs={{0,240},{16,0},{32,16},{48,32},{64,48},{80,64},{96,80},{112,96},{1... | collective-permute-start | bytes 294920 | tf_op jit(solution)/shard_map/ppermute | solution.py:310
  128.9 8.4 %collective-permute-start.6 = (bf16[4,4,16,128]{3,2,1,0:T(8,128)(2,1)S(1)}, bf16[4,4,16,128]{3,2,1,0:T(8,128)(2,1)S(1)}, u32[]{:S(2)}, u32[]{:S(2)}) collective-permute-start(bf16[4,4,16,128]{3,2,1,0:T(8,128)(2,1)S(1)} %get-tuple-element.28), channel_id=1, source_target_pairs={{0,16},{16,32},{32,48},{48,64},{64,80},{80,96},{96,112},{112,128},... | collective-permute-start | bytes 196616 | tf_op jit(solution)/shard_map/ppermute | solution.py:309
  132.4 7.1 %collective-permute-start.7 = (bf16[4,4,16,128]{3,2,1,0:T(8,128)(2,1)S(1)}, bf16[4,4,16,128]{3,2,1,0:T(8,128)(2,1)S(1)}, u32[]{:S(2)}, u32[]{:S(2)}) collective-permute-start(bf16[4,4,16,128]{3,2,1,0:T(8,128)(2,1)S(1)} %get-tuple-element.28), channel_id=1, source_target_pairs={{0,240},{16,0},{32,16},{48,32},{64,48},{80,64},{96,80},{112,96},{1... | collective-permute-start | bytes 196616 | tf_op jit(solution)/shard_map/ppermute | solution.py:310
  139.6 6.9 %collective-permute-start.9 = (bf16[16,4,8,128]{3,2,1,0:T(8,128)(2,1)S(1)}, bf16[16,4,8,128]{3,2,1,0:T(8,128)(2,1)S(1)}, u32[]{:S(2)}, u32[]{:S(2)}) collective-permute-start(bf16[16,4,8,128]{3,2,1,0:T(8,128)(2,1)S(1)} %pad_maximum_fusion.3), channel_id=1, source_target_pairs={{0,9},{2,0},{4,2},{6,4},{14,6},{12,14},{10,12},{8,10},{1,8},{3,1},... | collective-permute-start | bytes 393224 | tf_op jit(solution)/shard_map/ppermute | solution.py:329
  141.6 7.4 %collective-permute-start.8 = (bf16[16,4,8,128]{3,2,1,0:T(8,128)(2,1)S(1)}, bf16[16,4,8,128]{3,2,1,0:T(8,128)(2,1)S(1)}, u32[]{:S(2)}, u32[]{:S(2)}) collective-permute-start(bf16[16,4,8,128]{3,2,1,0:T(8,128)(2,1)S(1)} %pad_maximum_fusion.2), channel_id=1, source_target_pairs={{0,2},{2,4},{4,6},{6,14},{14,12},{12,10},{10,8},{8,1},{1,3},{3,5},... | collective-permute-start | bytes 393224 | tf_op jit(solution)/shard_map/ppermute | solution.py:328
  152.2 9.3 %collective-permute-start.10 = (bf16[4,4,24,128]{3,2,1,0:T(8,128)(2,1)S(1)}, bf16[4,4,24,128]{3,2,1,0:T(8,128)(2,1)S(1)}, u32[]{:S(2)}, u32[]{:S(2)}) collective-permute-start(bf16[4,4,24,128]{3,2,1,0:T(8,128)(2,1)S(1)} %get-tuple-element.33.refs_5_), channel_id=1, source_target_pairs={{16,32},{32,16},{48,64},{64,48},{80,96},{96,80},{112,128},{128,112... | collective-permute-start | bytes 294920 | tf_op jit(solution)/shard_map/ppermute | solution.py:319
  158.4 8.4 %collective-permute-start.11 = (bf16[4,4,24,128]{3,2,1,0:T(8,128)(2,1)S(1)}, bf16[4,4,24,128]{3,2,1,0:T(8,128)(2,1)S(1)}, u32[]{:S(2)}, u32[]{:S(2)}) collective-permute-start(bf16[4,4,24,128]{3,2,1,0:T(8,128)(2,1)S(1)} %get-tuple-element.33.refs_5_), channel_id=1, source_target_pairs={{0,16},{16,0},{32,48},{48,32},{64,80},{80,64},{96,112},{112,96},{1... | collective-permute-start | bytes 294920 | tf_op jit(solution)/shard_map/ppermute | solution.py:318
  166.8 1.4 copy-start.1
